TPU v7x, 8 devices: a whole 2x2x1 slice. The times are simulated.
8 devices in a mesh: prompts: 1 (over z), model: 2 (over y), resp: 4 (over x, core).
Axes of the slice: x: 2, y: 2, z: 1, core: 2. Of those that a mesh axis runs over, the one named last changes fastest.
Arguments:
- x_prompt: bfloat16 [64, 1536], P(('prompts', 'resp'))
- x_resp: bfloat16 [4, 2048, 1536], P(('prompts', 'resp'))
- targets: int32 [4, 2048], P(('prompts', 'resp'))
- resp_lens: int32 [4], P(('prompts', 'resp'))
- attn_gain: float32 [2, 1536], replicated
- w_query: bfloat16 [2, 1536, 12, 128], P(None, None, 'model')
- w_key: bfloat16 [2, 1536, 2, 128], P(None, None, 'model')
- w_value: bfloat16 [2, 1536, 2, 128], P(None, None, 'model')
- w_out: bfloat16 [2, 12, 128, 1536], P(None, 'model')
- mlp_gain: float32 [2, 1536], replicated
- w_gate: bfloat16 [2, 1536, 8960], P(None, None, 'model')
- w_up: bfloat16 [2, 1536, 8960], P(None, None, 'model')
- w_down: bfloat16 [2, 8960, 1536], P(None, 'model')
- final_gain: float32 [1536], replicated
- w_vocab: bfloat16 [1536, 2048], P(None, 'model')
Outputs:
- output: float32 [4, 2048], P(('prompts', 'resp'))
All inputs are finite; a program needn't handle non-finite values.
Results may differ from a plain program's by a relative error of at most 0.00292731.
Values are sent between devices in bfloat16 or wider.
A program may use at most 1 GiB of HBM per device.

v0:
```python
import jax
import jax.numpy as jnp
from jax import lax
from jax.sharding import PartitionSpec as P

EPS = 1e-6
ROPE_BASE = 10000.0


def rms_norm(acts_in, gain_vec):
    acts_f = acts_in.astype(jnp.float32)
    inv_rms = lax.rsqrt(jnp.mean(acts_f * acts_f, axis=-1, keepdims=True) + EPS)
    return (acts_f * inv_rms * gain_vec).astype(jnp.bfloat16)


def rotary(projected, positions):
    half_dim = projected.shape[-1] // 2
    frequency = ROPE_BASE ** (-jnp.arange(half_dim, dtype=jnp.float32) / half_dim)
    angles = positions.astype(jnp.float32)[..., None] * frequency
    cos_part = jnp.cos(angles)[..., None, :]
    sin_part = jnp.sin(angles)[..., None, :]
    lower_half = projected[..., :half_dim]
    upper_half = projected[..., half_dim:]
    return jnp.concatenate([lower_half * cos_part - upper_half * sin_part, upper_half * cos_part + lower_half * sin_part], axis=-1)


def attend(queries, keys, values, query_pos, key_pos):
    heads, head_dim = queries.shape[-2], queries.shape[-1]
    kv_heads = keys.shape[-2]
    grouped = queries.reshape(queries.shape[:-2] + (kv_heads, heads // kv_heads, head_dim))
    scores = jnp.einsum('...tkrd,...skd->...krts', grouped, keys, preferred_element_type=jnp.float32) * (head_dim ** -0.5)
    visible = (key_pos[None, :] <= query_pos[..., :, None])[..., None, None, :, :]
    scores = jnp.where(visible, scores, -jnp.inf)
    row_max = jnp.max(scores, axis=-1, keepdims=True)
    exp_scores = jnp.exp(scores - row_max)
    row_sum = jnp.moveaxis(jnp.sum(exp_scores, axis=-1), -1, -3)
    mixed = jnp.einsum('...krts,...skd->...tkrd', exp_scores.astype(jnp.bfloat16), values, preferred_element_type=jnp.float32)
    return (mixed / row_sum[..., None]).reshape(queries.shape).astype(jnp.bfloat16)


def solution(mesh):
    groups = mesh.shape['resp']
    row_axes = ('prompts', 'resp')
    head_spec = P(None, None, 'model', None)
    in_specs = (P(row_axes, None), P(row_axes, None, None), P(row_axes, None), P(row_axes), P(None, None), head_spec, head_spec, head_spec, P(None, 'model', None, None), P(None, None), P(None, None, 'model'), P(None, None, 'model'), P(None, 'model', None), P(None), P(None, 'model'))

    def device_step(x_prompt, x_resp, targets, resp_lens, attn_gain, w_query, w_key, w_value, w_out, mlp_gain, w_gate, w_up, w_down, final_gain, w_vocab):
        prompt_rows = x_prompt.shape[0]
        resp_len = x_resp.shape[1]
        prompt_len = prompt_rows * groups
        num_layers = w_query.shape[0]
        resp_pos = prompt_len + jnp.arange(resp_len)
        tok_pos = jnp.concatenate([lax.axis_index('resp') * prompt_rows + jnp.arange(prompt_rows), resp_pos])
        key_pos = jnp.concatenate([jnp.arange(prompt_len), resp_pos])
        residual = jnp.concatenate([x_prompt, x_resp[0]], axis=0)
        for layer_idx in range(num_layers):
            hidden = rms_norm(residual, attn_gain[layer_idx])
            keys = rotary(jnp.einsum('td,dhe->the', hidden, w_key[layer_idx], preferred_element_type=jnp.float32), tok_pos).astype(jnp.bfloat16)
            values = jnp.einsum('td,dhe->the', hidden, w_value[layer_idx], preferred_element_type=jnp.float32).astype(jnp.bfloat16)
            prompt_keys = lax.all_gather(keys[:prompt_rows], 'resp', axis=0, tiled=True)
            prompt_values = lax.all_gather(values[:prompt_rows], 'resp', axis=0, tiled=True)
            all_keys = jnp.concatenate([prompt_keys, keys[prompt_rows:]], axis=0)
            all_values = jnp.concatenate([prompt_values, values[prompt_rows:]], axis=0)
            query_pos = tok_pos
            if layer_idx == num_layers - 1:
                residual = residual[prompt_rows:]
                hidden = hidden[prompt_rows:]
                query_pos = resp_pos
            queries = rotary(jnp.einsum('td,dhe->the', hidden, w_query[layer_idx], preferred_element_type=jnp.float32), query_pos).astype(jnp.bfloat16)
            mixed = attend(queries, all_keys, all_values, query_pos, key_pos)
            attn_part = jnp.einsum('the,hed->td', mixed, w_out[layer_idx], preferred_element_type=jnp.float32)
            residual = (residual.astype(jnp.float32) + lax.psum(attn_part, 'model')).astype(jnp.bfloat16)
            hidden = rms_norm(residual, mlp_gain[layer_idx])
            gate = jnp.dot(hidden, w_gate[layer_idx], preferred_element_type=jnp.float32)
            up_proj = jnp.dot(hidden, w_up[layer_idx], preferred_element_type=jnp.float32)
            inner = (jax.nn.silu(gate) * up_proj).astype(jnp.bfloat16)
            down_part = jnp.dot(inner, w_down[layer_idx], preferred_element_type=jnp.float32)
            residual = (residual.astype(jnp.float32) + lax.psum(down_part, 'model')).astype(jnp.bfloat16)
        logits = jnp.dot(rms_norm(residual, final_gain), w_vocab, preferred_element_type=jnp.float32)
        vocab_local = logits.shape[-1]
        vocab_ids = lax.axis_index('model') * vocab_local + jnp.arange(vocab_local)
        row_max = lax.pmax(jnp.max(logits, axis=-1), 'model')
        exp_total = lax.psum(jnp.sum(jnp.exp(logits - row_max[:, None]), axis=-1), 'model')
        picked = lax.psum(jnp.sum(jnp.where(vocab_ids[None, :] == targets[0][:, None], logits, 0.0), axis=-1), 'model')
        log_probs = picked - row_max - jnp.log(exp_total)
        log_probs = jnp.where(jnp.arange(resp_len) < resp_lens[0], log_probs, 0.0)
        return log_probs[None, :]

    return jax.shard_map(device_step, mesh=mesh, in_specs=in_specs, out_specs=P(row_axes, None), check_vma=False)
```

profile of v0, /device:TPU:0, one launch (start us, length us, event | category | flops | bytes accessed | tf_op | source)
XLA Modules:
  0.0 1798.5 jit_solution(8377391747456777032)
XLA Ops:
  23.5 6.3 fusion.110
  30.7 10.0 all_gather.13
  40.7 8.5 fusion.53
  49.4 7.1 all-gather
  64.9 45.5 %fusion.175 = (f32[6,2064]{1,0:T(8,128)S(1)}, f32[1,6,2064,2112]{3,2,1,0:T(8,128)}) fusion(bf16[2064,6,64]{2,0,1:T(8,128)(2,1)} %get-tuple-element.20, bf16[2064,6,64]{2,0,1:T(8,128)(2,1)} %get-tuple-element.19, bf16[2064,1,64]{2,0,1:T(8,128)(2,1)} %copy-done.7, bf16[2064,1,64]{2,0,1:T(8,128)(2,1)} %copy-done.6, bf16[64,1,128]{2,0,1:T(8,128)(2,1)S(1)} %all_gather.13, ...), kind=kOutput, calls=%fused_computation.199 | convolution fusion | flops 6782908416 | bytes 112743808 | tf_op jit(solution)/shard_map/...tkrd,...skd->...krts/dot_general | solution.py:31
  110.4 36.3 %fusion = f32[6,2064]{1,0:T(8,128)S(1)} fusion(f32[1,6,2064,2112]{3,2,1,0:T(8,128)} %get-tuple-element.34, f32[6,2064]{1,0:T(8,128)S(1)} %get-tuple-element.33), kind=kLoop, calls=%fused_computation.4 | loop fusion | flops 52297632 | bytes 104719104 | tf_op jit(solution)/shard_map/reduce_sum | solution.py:36
  146.8 37.0 %fusion.64.clone.5 = bf16[2064,6,128]{2,0,1:T(8,128)(2,1)} fusion(f32[1,6,2064,2112]{3,2,1,0:T(8,128)} %get-tuple-element.34, f32[6,2064]{1,0:T(8,128)S(1)} %get-tuple-element.33, f32[2064,6]{0,1:T(8,128)S(1)} %bitcast.245, bf16[2048,1,128]{2,0,1:T(8,128)(2,1)} %slice_bitcast_fusion.1, bf16[64,1,128]{2,0,1:T(8,128)(2,1)S(1)} %bitcast.247), kind=kOutput, calls=%fused_computation.86.clone.clone.clone.2 | convolution fusion | flops 6752243712 | bytes 108430080 | tf_op jit(solution)/shard_map/...krts,...skd->...tkrd/dot_general | solution.py:37
  183.7 9.8 convolution_bitcast_fusion
  194.8 284.7 %all-reduce.6.cloned.1.call-done = f32[2064,1536]{1,0:T(8,128)} async-done(((f32[2064,1536]{1,0:T(8,128)}), f32[2064,1536]{1,0:T(8,128)}) %all-reduce.6.cloned.1.call-update) | async-done | bytes 12681232 | tf_op jit(solution)/shard_map/psum | solution.py:72
  479.5 7.5 fusion.41
  489.7 36.3 %fusion.24 = f32[2064,4480]{1,0:T(8,128)} fusion(bf16[2,1536,4480]{2,1,0:T(8,128)(2,1)} %param.25, bf16[2064,1536]{1,0:T(8,128)(2,1)S(1)} %get-tuple-element.18, f32[1536]{0:T(1024)S(1)} %get-tuple-element.8, f32[2064]{0:T(1024)S(1)} %add_rsqrt_fusion.1), kind=kOutput, calls=%fused_computation.39 | convolution fusion | flops 28418605056 | bytes 57104448 | tf_op jit(solution)/shard_map/dot_general | solution.py:74
  525.9 41.1 %fusion.13.clone.5 = bf16[2064,4480]{1,0:T(8,128)(2,1)} fusion(f32[2064,4480]{1,0:T(8,128)} %fusion.24, bf16[2,1536,4480]{2,1,0:T(8,128)(2,1)} %param.26, bf16[2064,1536]{1,0:T(8,128)(2,1)} %copy-done.2, f32[1536]{0:T(1024)S(1)} %get-tuple-element.8, f32[2064]{0:T(1024)S(1)} %add_rsqrt_fusion.1), kind=kOutput, calls=%fused_computation.17.clone.clone.clone.2 | convolution fusion | flops 28474085376 | bytes 75597888 | tf_op jit(solution)/shard_map/dot_general | solution.py:75
  567.1 38.6 %fusion.20 = f32[2064,1536]{1,0:T(8,128)} fusion(bf16[2,4480,1536]{2,1,0:T(8,128)(2,1)} %param.27, bf16[2064,4480]{1,0:T(8,128)(2,1)} %fusion.13.clone.5), kind=kOutput, calls=%fused_computation.36 | convolution fusion | flops 28405923840 | bytes 44937216 | tf_op jit(solution)/shard_map/dot_general | solution.py:77
  621.0 269.7 %all-reduce.8.cloned.1.call-done = f32[2064,1536]{1,0:T(8,128)} async-done(((f32[2064,1536]{1,0:T(8,128)}), f32[2064,1536]{1,0:T(8,128)}) %all-reduce.8.cloned.1.call-update) | async-done | bytes 12681232 | tf_op jit(solution)/shard_map/psum | solution.py:78
  890.8 7.5 fusion.34
  910.5 8.1 all_gather.15
  918.6 5.1 fusion.57
  923.7 7.4 all-gather.1
  933.8 39.2 %fusion.4 = (f32[6,2048]{1,0:T(8,128)S(1)}, f32[2112,2048,6]{1,0,2:T(8,128)}) fusion(pred[2048,2112]{0,1:T(8,128)(4,1)} %broadcast_compare_fusion.1, bf16[2048,6,64]{0,2,1:T(8,128)(2,1)} %get-tuple-element.22, bf16[2048,6,64]{0,2,1:T(8,128)(2,1)} %get-tuple-element.21, bf16[2064,1,64]{2,0,1:T(8,128)(2,1)} %copy-done.9, bf16[2064,1,64]{2,0,1:T(8,128)(2,1)} %copy-done.8, ...), kind=kOutput, calls=%fused_computation.8 | convolution fusion | flops 6730346496 | bytes 111874048 | tf_op jit(solution)/shard_map/...tkrd,...skd->...krts/dot_general | solution.py:31
  973.0 33.5 %fusion.2 = f32[6,2048]{1,0:T(8,128)S(1)} fusion(f32[2112,2048,6]{1,0,2:T(8,128)} %get-tuple-element.36, f32[6,2048]{1,0:T(8,128)S(1)} %get-tuple-element.35, pred[2048,2112]{0,1:T(8,128)(4,1)} %broadcast_compare_fusion.1), kind=kLoop, calls=%fused_computation.6 | loop fusion | flops 103796736 | bytes 108232704 | tf_op jit(solution)/shard_map/reduce_sum | solution.py:36
  1006.6 41.1 %fusion.223 = bf16[2048,6,128]{0,2,1:T(8,128)(2,1)} fusion(f32[2112,2048,6]{1,0,2:T(8,128)} %get-tuple-element.36, f32[6,2048]{1,0:T(8,128)S(1)} %get-tuple-element.35, pred[2048,2112]{0,1:T(8,128)(4,1)} %broadcast_compare_fusion.1, f32[2048,6]{0,1:T(8,128)S(1)} %bitcast.246, bf16[2048,1,128]{2,0,1:T(8,128)(2,1)} %slice_bitcast_fusion, ...), kind=kOutput, calls=%fused_computation.99.clone.2 | convolution fusion | flops 6751813632 | bytes 111919104 | tf_op jit(solution)/shard_map/...krts,...skd->...tkrd/dot_general | solution.py:37
  1047.6 10.3 convolution_bitcast_fusion.1
  1058.0 283.0 %all-reduce.10.cloned.1.call-done = f32[2048,1536]{1,0:T(8,128)} async-done(((f32[2048,1536]{1,0:T(8,128)}), f32[2048,1536]{1,0:T(8,128)}) %all-reduce.10.cloned.1.call-update) | async-done | bytes 12582928 | tf_op jit(solution)/shard_map/psum | solution.py:72
  1341.0 7.4 fusion.48
  1351.0 35.8 %fusion.18 = f32[2048,4480]{1,0:T(8,128)} fusion(bf16[2,1536,4480]{2,1,0:T(8,128)(2,1)} %param.25, bf16[2048,1536]{1,0:T(8,128)(2,1)S(1)} %get-tuple-element.14, f32[1536]{0:T(1024)S(1)} %copy-done.24, f32[2048]{0:T(1024)S(1)} %add_rsqrt_fusion.4), kind=kOutput, calls=%fused_computation.34 | convolution fusion | flops 28198305792 | bytes 56768512 | tf_op jit(solution)/shard_map/dot_general | solution.py:74
  1386.8 46.4 %multiply_convert_fusion.clone.5 = bf16[2048,4480]{1,0:T(8,128)(2,1)} fusion(f32[2048,4480]{1,0:T(8,128)} %fusion.18, bf16[2,1536,4480]{2,1,0:T(8,128)(2,1)} %param.26, bf16[2048,1536]{1,0:T(8,128)(2,1)} %copy-done.4, f32[1536]{0:T(1024)S(1)} %copy-done.24, f32[2048]{0:T(1024)S(1)} %add_rsqrt_fusion.4), kind=kOutput, calls=%fused_computation.16.clone.clone.clone.2 | convolution fusion | flops 28253356032 | bytes 75118592 | tf_op jit(solution)/shard_map/dot_general | solution.py:75
  1433.2 37.9 %fusion.14 = f32[2048,1536]{1,0:T(8,128)} fusion(bf16[2,4480,1536]{2,1,0:T(8,128)(2,1)} %param.27, bf16[2048,4480]{1,0:T(8,128)(2,1)} %multiply_convert_fusion.clone.5), kind=kOutput, calls=%fused_computation.31 | convolution fusion | flops 28185722880 | bytes 44695552 | tf_op jit(solution)/shard_map/dot_general | solution.py:77
  1471.9 281.7 %all-reduce.12.cloned.1.call-done = f32[2048,1536]{1,0:T(8,128)} async-done(((f32[2048,1536]{1,0:T(8,128)}), f32[2048,1536]{1,0:T(8,128)}) %all-reduce.12.cloned.1.call-update) | async-done | bytes 12582928 | tf_op jit(solution)/shard_map/psum | solution.py:78
  1753.5 8.1 fusion.45
  1761.6 13.0 fusion.176
  1774.6 5.0 pmax.7
  1784.2 7.0 all-reduce
  (111 shorter events, 68.4 us)
Async XLA Ops:
  6.5 1755.1 %copy-start = (bf16[1536,1024]{1,0:T(8,128)(2,1)S(1)}, bf16[1536,1024]{1,0:T(8,128)(2,1)}, u32[]{:S(2)}) copy-start(bf16[1536,1024]{1,0:T(8,128)(2,1)} %param.29) | copy-start | bytes 9437188
  6.5 5.0 copy-start.13
  6.5 4.3 copy-start.22
  6.5 473.0 %all-reduce.6.cloned.1.call-start = ((), (), s32[]{:S(2)}) async-start(), calls=%async_computation | async-start | bytes 25362432 | tf_op jit(solution)/shard_map/psum | solution.py:72
  6.5 5.0 copy-start.3
  6.6 42.7 %copy-start.17 = (s32[2048]{0:T(1024)}, s32[2048]{0:T(1024)S(1)}, u32[]{:S(2)}) copy-start(s32[2048]{0:T(1024)S(1)} %iota_add_fusion) | copy-start | bytes 24580
  6.6 16.9 copy-start.26
  11.5 4.7 copy-start.28
  19.8 29.5 %copy-start.15 = (f32[2064]{0:T(1024)}, f32[2064]{0:T(1024)S(1)}, u32[]{:S(2)}) copy-start(f32[2064]{0:T(1024)S(1)} %get-tuple-element.31) | copy-start | bytes 24772
  40.7 8.6 slice-start
  49.4 15.5 copy-start.19
  193.5 286.0 %copy-start.14 = (bf16[16,1536]{1,0:T(8,128)(2,1)S(1)}, bf16[16,1536]{1,0:T(8,128)(2,1)}, u32[]{:S(2)}) copy-start(bf16[16,1536]{1,0:T(8,128)(2,1)} %param.15) | copy-start | bytes 147460
  193.5 697.3 %all-reduce.8.cloned.1.call-start = ((), (), s32[]{:S(2)}) async-start(), calls=%async_computation.1 | async-start | bytes 25362432 | tf_op jit(solution)/shard_map/psum | solution.py:78
  487.0 2.6 copy-start.2
  605.6 8.1 copy-start.27
  605.6 10.9 copy-start.18
  605.7 10.8 copy-start.20
  605.7 735.3 %all-reduce.10.cloned.1.call-start = ((), (), s32[]{:S(2)}) async-start(), calls=%async_computation.2 | async-start | bytes 25165824 | tf_op jit(solution)/shard_map/psum | solution.py:72
  621.0 277.3 %copy-start.21 = (f32[1536]{0:T(1024)S(1)}, f32[1536]{0:T(1024)}, u32[]{:S(2)}) copy-start(f32[1536]{0:T(1024)} %get-tuple-element.9) | copy-start | bytes 18436
  898.3 2.7 copy-start.1
  898.4 2.6 copy-start.29
  902.9 2.7 copy-start.16
  902.9 15.7 copy-start.5
  910.4 8.2 copy-start.8
  910.4 8.2 copy-start.9
  918.6 12.5 copy-start.10
  918.6 12.5 copy-start.11
  1057.9 293.1 %copy-start.24 = (f32[1536]{0:T(1024)S(1)}, f32[1536]{0:T(1024)}, u32[]{:S(2)}) copy-start(f32[1536]{0:T(1024)} %get-tuple-element.7) | copy-start | bytes 18436
  1057.9 695.6 %all-reduce.12.cloned.1.call-start = ((), (), s32[]{:S(2)}) async-start(), calls=%async_computation.3 | async-start | bytes 25165824 | tf_op jit(solution)/shard_map/psum | solution.py:78
  1348.4 2.6 copy-start.4
  1471.9 289.8 %copy-start.31 = (f32[1536]{0:T(1024)S(1)}, f32[1536]{0:T(1024)}, u32[]{:S(2)}) copy-start(f32[1536]{0:T(1024)} %param.28) | copy-start | bytes 18436
  1761.6 18.0 copy-start.25
  (5 other events, 5.3 us)
Sparse Core Ops, SparseCore 0:
  193.6 285.8 all-reduce.5
  605.8 284.9 all-reduce.7
  1058.0 282.8 all-reduce.9
  1471.3 282.1 all-reduce.11
where the time goes:
time: 1810 us; the launch traced here: 1800 us
  waiting for transfers between devices  1120 us (62%)
  matrix products  456 us (25%)
  other arithmetic  145 us (8%)
  blocking collectives  44.4 us (2%)
  local copies, waits for them, and re-layouts  19 us (1%)
    psum x2, waiting for transfers between devices, device_step(): lax.psum(attn_part, 'model')  568 us
    psum x2, waiting for transfers between devices, device_step(): lax.psum(down_part, 'model')  551 us
    dot_general x2, matrix products, device_step(): jnp.dot(hidden, w_up[layer_idx], preferred_element_type=jnp.float32)  87.5 us
    dot_general x2, matrix products, attend(): jnp.einsum('...tkrd,...skd->...krts', grouped, keys, preferred_element_ty...  84.8 us
    dot_general x2, matrix products, attend(): jnp.einsum('...krts,...skd->...tkrd', exp_scores.astype(jnp.bfloat16), va...  78 us
    dot_general x2, matrix products, device_step(): jnp.dot(inner, w_down[layer_idx], preferred_element_type=jnp.float32)  76.5 us
    dot_general x2, matrix products, device_step(): jnp.dot(hidden, w_gate[layer_idx], preferred_element_type=jnp.float32)  72.1 us
    reduce_sum x2, other arithmetic, attend(): row_sum = jnp.moveaxis(jnp.sum(exp_scores, axis=-1), -1, -3)  69.8 us
  transfers between devices with their start and end apart: 4, of which 4 were waited for; matrix products, arithmetic and copies ran while one was open for 1% of the time, Pallas kernels for 0%

commit v1 on v0

v1 whole, which is shorter than its diff:
```python
import functools

import jax
import jax.numpy as jnp
from jax import lax
from jax.experimental import pallas as pl
from jax.experimental.pallas import tpu as pltpu
from jax.sharding import PartitionSpec as P

EPS = 1e-6
ROPE_BASE = 10000.0
HEAD = 128
BLOCK = 352
OWNED = ((0, 3, 5), (1, 2, 4))


def rms_norm(acts_in, gain_vec):
    acts_f = acts_in.astype(jnp.float32)
    inv_rms = lax.rsqrt(jnp.mean(acts_f * acts_f, axis=-1, keepdims=True) + EPS)
    return (acts_f * inv_rms * gain_vec).astype(jnp.bfloat16)


def dot(a, b):
    return jnp.dot(a, b, preferred_element_type=jnp.float32)


def attention_kernel(num_blocks, heads, ids_ref, q_ref, k_ref, v_ref, o_ref):
    block_id = ids_ref[pl.program_id(1)]
    rows = q_ref.shape[0]

    def body(i):
        first = i * rows
        low = first // 128 * 128
        high = min(-(-(first + rows) // 128) * 128, k_ref.shape[0])
        row = first + lax.broadcasted_iota(jnp.int32, (rows, high - low), 0)
        col = low + lax.broadcasted_iota(jnp.int32, (rows, high - low), 1)
        seen = col <= row
        for h in range(heads):
            q = q_ref[:, h * HEAD:(h + 1) * HEAD]
            nt = (((1,), (1,)), ((), ()))
            s_hi = lax.dot_general(q, k_ref[low:high, :], nt, preferred_element_type=jnp.float32)
            s_hi = jnp.where(seen, s_hi, -jnp.inf)
            m = jnp.max(s_hi, axis=-1, keepdims=True)
            if low:
                s_lo = lax.dot_general(q, k_ref[:low, :], nt, preferred_element_type=jnp.float32)
                m = jnp.maximum(m, jnp.max(s_lo, axis=-1, keepdims=True))
            scale = HEAD ** -0.5
            p_hi = jnp.exp((s_hi - m) * scale)
            total = jnp.sum(p_hi, axis=-1, keepdims=True)
            out = dot(p_hi.astype(jnp.bfloat16), v_ref[low:high, :])
            if low:
                p_lo = jnp.exp((s_lo - m) * scale)
                total = total + jnp.sum(p_lo, axis=-1, keepdims=True)
                out = out + dot(p_lo.astype(jnp.bfloat16), v_ref[:low, :])
            o_ref[:, h * HEAD:(h + 1) * HEAD] = (out / total).astype(jnp.bfloat16)

    for i in range(num_blocks):
        pl.when(block_id == i)(functools.partial(body, i))


def attention(ids, q, k, v, num_blocks):
    rows, width = q.shape
    per_step = 2
    n = rows // BLOCK
    keys = k.shape[0]
    spec = pltpu.PrefetchScalarGridSpec(
        num_scalar_prefetch=1,
        grid=(width // (per_step * HEAD), n),
        in_specs=[
            pl.BlockSpec((BLOCK, per_step * HEAD), lambda h, b, ids: (b, h)),
            pl.BlockSpec((keys, HEAD), lambda h, b, ids: (0, 0)),
            pl.BlockSpec((keys, HEAD), lambda h, b, ids: (0, 0)),
        ],
        out_specs=pl.BlockSpec((BLOCK, per_step * HEAD), lambda h, b, ids: (b, h)),
    )
    return pl.pallas_call(
        functools.partial(attention_kernel, num_blocks, per_step),
        grid_spec=spec,
        out_shape=jax.ShapeDtypeStruct((rows, width), jnp.bfloat16),
        compiler_params=pltpu.CompilerParams(
            dimension_semantics=("arbitrary", "arbitrary"), vmem_limit_bytes=48 * 2**20),
        cost_estimate=pl.CostEstimate(
            flops=int(rows * keys * width * 4), bytes_accessed=rows * width * 4 + keys * HEAD * 4,
            transcendentals=rows * keys * width // HEAD // 2),
    )(ids, q, k, v)


def solution(mesh):
    groups = mesh.shape['resp']
    row_axes = ('prompts', 'resp')
    head_spec = P(None, None, 'model', None)
    in_specs = (P(row_axes, None), P(row_axes, None, None), P(row_axes, None), P(row_axes), P(None, None), head_spec, head_spec, head_spec, P(None, 'model', None, None), P(None, None), P(None, None, 'model'), P(None, None, 'model'), P(None, 'model', None), P(None), P(None, 'model'))
    across = [(0, 1), (1, 0)]
    core = [(i, i ^ 1) for i in range(groups)]
    chip = [(i, i ^ 2) for i in range(groups)]

    def swap(a):
        return lax.ppermute(a, 'model', across)

    def spread(a):
        far = lax.ppermute(a, 'resp', chip)
        return [a, lax.ppermute(a, 'resp', core), far, lax.ppermute(far, 'resp', core)]

    def device_step(x_prompt, x_resp, targets, resp_lens, attn_gain, w_query, w_key, w_value, w_out, mlp_gain, w_gate, w_up, w_down, final_gain, w_vocab):
        me = lax.axis_index('resp')
        side = lax.axis_index('model')
        resp_len = x_resp.shape[1]
        dim = x_resp.shape[2]
        prompt_len = x_prompt.shape[0] * groups
        tokens = prompt_len + resp_len
        blocks = tokens // BLOCK
        keys_pad = -(-tokens // 128) * 128
        q_width = w_query.shape[2] * HEAD
        ffn = w_gate.shape[2]
        vocab = w_vocab.shape[1]

        def in_order(pieces):
            stack = jnp.stack(pieces)
            return jnp.concatenate([lax.dynamic_index_in_dim(stack, me ^ j, 0, keepdims=False) for j in range(groups)], axis=0)

        def quarter(w, axis):
            size = w.shape[axis] // groups
            return lax.dynamic_slice_in_dim(w, me * size, size, axis)

        def own_qkv(l):
            return jnp.concatenate([w_query[l].reshape(dim, q_width), w_key[l].reshape(dim, HEAD), w_value[l].reshape(dim, HEAD)], axis=1)

        def own_out(l):
            return w_out[l].reshape(q_width, dim)

        def fetch_rows(w):
            return in_order(spread(swap(quarter(w, 0))))

        qkv_own = [own_qkv(0), own_qkv(1)]
        out_own = [own_out(0), own_out(1)]
        qkv_far0 = fetch_rows(qkv_own[0])
        out_far0 = fetch_rows(out_own[0])

        prompt = in_order(spread(x_prompt))
        x = jnp.concatenate([prompt, x_resp[0]], axis=0)

        half = HEAD // 2
        frequency = ROPE_BASE ** (-jnp.arange(half, dtype=jnp.float32) / half)
        angles = jnp.arange(tokens).astype(jnp.float32)[:, None] * frequency
        cos_all, sin_all = jnp.cos(angles), jnp.sin(angles)

        def rotary(a, cos_part, sin_part):
            a = a.reshape(a.shape[0], -1, HEAD)
            low, high = a[..., :half], a[..., half:]
            c, s = cos_part[:, None, :], sin_part[:, None, :]
            out = jnp.concatenate([low * c - high * s, high * c + low * s], axis=-1).astype(jnp.bfloat16)
            return out.reshape(a.shape[0], -1)

        def project(h, w, cos_part, sin_part):
            f = dot(h, w)
            qk = rotary(f[:, :q_width + HEAD], cos_part, sin_part)
            return qk[:, :q_width], qk[:, q_width:], f[:, q_width + HEAD:].astype(jnp.bfloat16)

        def pad(a):
            return jnp.pad(a, ((0, keys_pad - tokens), (0, 0)))

        h = rms_norm(x, attn_gain[0])
        ids_all = jnp.arange(blocks, dtype=jnp.int32)
        q, k, v = project(h, qkv_own[0], cos_all, sin_all)
        mixed_own = attention(ids_all, q, pad(k), pad(v), blocks)
        q, k, v = project(h, qkv_far0, cos_all, sin_all)
        mixed_far = attention(ids_all, q, pad(k), pad(v), blocks)
        x = (x.astype(jnp.float32) + (dot(mixed_own, out_own[0]) + dot(mixed_far, out_far0))).astype(jnp.bfloat16)

        owned = jnp.array(OWNED, jnp.int32)
        mine = owned[side]
        theirs = owned[1 - side]

        def take(a, ids):
            return jnp.concatenate([lax.dynamic_slice_in_dim(a, ids[i] * BLOCK, BLOCK, 0) for i in range(ids.shape[0])], axis=0)

        u = rms_norm(x, mlp_gain[0])

        def mlp(rows, gate_w, up_w, down_w):
            inner = (jax.nn.silu(dot(rows, gate_w)) * dot(rows, up_w)).astype(jnp.bfloat16)
            return dot(inner, down_w)

        u_theirs = take(u, theirs)
        got = []
        for i in range(theirs.shape[0]):
            part = mlp(u_theirs[i * BLOCK:(i + 1) * BLOCK], w_gate[0], w_up[0], w_down[0])
            got.append(swap(part))
        part_mine = mlp(take(u, mine), w_gate[0], w_up[0], w_down[0])
        x = (take(x, mine).astype(jnp.float32) + (part_mine + jnp.concatenate(got, axis=0))).astype(jnp.bfloat16)

        qkv_far1 = fetch_rows(qkv_own[1])
        out_far1 = fetch_rows(out_own[1])
        cos_own, sin_own = take(cos_all, mine), take(sin_all, mine)
        h = rms_norm(x, attn_gain[1])
        q_own, k_own, v_own = project(h, qkv_own[1], cos_own, sin_own)
        q_far, k_far, v_far = project(h, qkv_far1, cos_own, sin_own)
        kv_mine = jnp.concatenate([k_own, v_own, k_far, v_far], axis=1)
        kv_sent = jnp.concatenate([k_far, v_far, k_own, v_own], axis=1)
        kv_got = swap(kv_sent)

        def merge(own_part, far_part):
            def split(a):
                return [a[i * BLOCK:(i + 1) * BLOCK] for i in range(a.shape[0] // BLOCK)]
            a, b = split(own_part), split(far_part)
            order = [[None] * blocks, [None] * blocks]
            for s in range(2):
                for i, blk in enumerate(OWNED[s]):
                    order[s][blk] = a[i]
                for i, blk in enumerate(OWNED[1 - s]):
                    order[s][blk] = b[i]
            return jnp.concatenate([jnp.where(side == 0, p0, p1) for p0, p1 in zip(*order)], axis=0)

        kv = pad(merge(kv_mine, kv_got))
        mixed_own = attention(mine, q_own, kv[:, :HEAD], kv[:, HEAD:2 * HEAD], blocks)
        mixed_far = attention(mine, q_far, kv[:, 2 * HEAD:3 * HEAD], kv[:, 3 * HEAD:], blocks)
        x = (x.astype(jnp.float32) + (dot(mixed_own, out_own[1]) + dot(mixed_far, out_far1))).astype(jnp.bfloat16)

        u = rms_norm(x, mlp_gain[1])
        total = mlp(u, w_gate[1], w_up[1], w_down[1])
        base = me * (ffn // groups)
        done = 0
        for size in (256, 256, 256, 256, 96):
            at = base + done
            gate_up = jnp.concatenate([lax.dynamic_slice_in_dim(w_gate[1], at, size, 1), lax.dynamic_slice_in_dim(w_up[1], at, size, 1)], axis=1)
            down = lax.dynamic_slice_in_dim(w_down[1], at, size, 0)
            gate_up = spread(swap(gate_up))
            down = spread(swap(down))
            total = total + mlp(u, jnp.concatenate([g[:, :size] for g in gate_up], axis=1), jnp.concatenate([g[:, size:] for g in gate_up], axis=1), jnp.concatenate(down, axis=0))
            done += size
        x = (x.astype(jnp.float32) + total).astype(jnp.bfloat16)

        vocab_far = spread(swap(quarter(w_vocab, 1)))
        logits = dot(rms_norm(x, final_gain), jnp.concatenate([w_vocab] + vocab_far, axis=1))
        piece = vocab // groups
        ids = [side * vocab + jnp.arange(vocab)] + [(1 - side) * vocab + (me ^ j) * piece + jnp.arange(piece) for j in range(groups)]
        vocab_ids = jnp.concatenate(ids)
        padded_targets = jnp.concatenate([jnp.zeros((prompt_len,), targets.dtype), targets[0]])[:, None]
        target_own = take(padded_targets, mine)
        row_max = jnp.max(logits, axis=-1)
        exp_total = jnp.sum(jnp.exp(logits - row_max[:, None]), axis=-1)
        picked = jnp.sum(jnp.where(vocab_ids[None, :] == target_own, logits, 0.0), axis=-1)
        log_probs = picked - row_max - jnp.log(exp_total)
        log_probs = merge(log_probs, swap(log_probs))[prompt_len:]
        log_probs = jnp.where(jnp.arange(resp_len) < resp_lens[0], log_probs, 0.0)
        return log_probs[None, :]

    return jax.shard_map(device_step, mesh=mesh, in_specs=in_specs, out_specs=P(row_axes, None), check_vma=False)
```

time: 1810 us -> 1150 us (0.64)
  waiting for transfers between devices: 1120 us -> 312 us
  local copies, waits for them, and re-layouts: 19 us -> 232 us
  Pallas kernels: 0 us -> 110 us
  other arithmetic: 145 us -> 45.2 us
  matrix products: 456 us -> 398 us
  blocking collectives: 44.4 us -> 0 us
  starting transfers between devices: 0.13 us -> 41.7 us
    psum x4 -> x0, waiting for transfers between devices: 1120 us -> none  [the longest x2 568 us: device_step(): lax.psum(attn_part, 'model')]
    ppermute x0 -> x68, waiting for transfers between devices: none -> 312 us  [the longest x20 200 us: swap(): return lax.ppermute(a, 'model', across)]
    slice x8 -> x51, local copies, waits for them, and re-layouts: 6.29 us -> 130 us  [the longest x8 41.4 us: project(): qk = rotary(f[:, :q_width + HEAD], cos_part, sin_part)]
    pallas_call x0 -> x4, Pallas kernels: none -> 110 us  [attention(): pl.pallas_call(functools.partial(attention_kernel, num_blocks, per_step),...]
    reduce_sum x3 -> x1, other arithmetic: 74.4 us -> 3.32 us  [device_step(): jnp.sum(jnp.where(vocab_ids[None, :] == target_own, logits, 0.0), axis=-1)]
    dot_general x18 -> x31, matrix products: 451 us -> 398 us  [dot(): return jnp.dot(a, b, preferred_element_type=jnp.float32)]
    unnamed x65 -> x226, local copies, waits for them, and re-layouts: 12.7 us -> 59 us
    ppermute x0 -> x68, starting transfers between devices: none -> 41.7 us  [the longest x20 21 us: swap(): return lax.ppermute(a, 'model', across)]
  transfers between devices with their start and end apart: 4 -> 68, of which waited for: 4 -> 14; matrix products, arithmetic and copies ran while one was open for 1% -> 53% of each run, Pallas kernels for 0% -> 10%
where the time goes in v1:
time: 1150 us; the launch traced here: 1140 us
  matrix products  398 us (35%)
  waiting for transfers between devices  312 us (27%)
  local copies, waits for them, and re-layouts  232 us (20%)
  Pallas kernels  110 us (10%)
  other arithmetic  45.2 us (4%)
  starting transfers between devices  41.7 us (4%)
    dot_general x31, matrix products, dot(): return jnp.dot(a, b, preferred_element_type=jnp.float32)  398 us
    ppermute x20, waiting for transfers between devices, swap(): return lax.ppermute(a, 'model', across)  200 us
    ppermute x16, waiting for transfers between devices, spread(): far = lax.ppermute(a, 'resp', chip)  112 us
    pallas_call x4, Pallas kernels, attention(): pl.pallas_call(functools.partial(attention_kernel, num_blocks, per_step),...  110 us
    unnamed x226, local copies, waits for them, and re-layouts  59 us
    slice x8, local copies, waits for them, and re-layouts, project(): qk = rotary(f[:, :q_width + HEAD], cos_part, sin_part)  41.4 us
    slice x20, local copies, waits for them, and re-layouts, device_step(): g[:, size:]  37.6 us
    slice x3, local copies, waits for them, and re-layouts, device_step(): total = mlp(u, w_gate[1], w_up[1], w_down[1])  26.7 us
  transfers between devices with their start and end apart: 68, of which 14 were waited for; matrix products, arithmetic and copies ran while one was open for 53% of the time, Pallas kernels for 10%

profile of v1, /device:TPU:0, one launch (start us, length us, event | category | flops | bytes accessed | tf_op | source)
XLA Modules:
  0.0 1143.8 jit_solution(1852130486991884188)
XLA Ops:
  10.0 13.5 %slice.416 = bf16[1,1536,4480]{2,1,0:T(8,128)(2,1)} slice(bf16[2,1536,4480]{2,1,0:T(8,128)(2,1)} %param.26), slice={[1:2], [0:1536], [0:4480]} | slice | bytes 27525120 | tf_op jit(solution)/shard_map/slice | solution.py:219
  169.3 41.4 %collective-permute-done.19 = bf16[192,1536]{1,0:T(8,128)(2,1)S(1)} collective-permute-done((bf16[192,1536]{1,0:T(8,128)(2,1)S(1)}, bf16[192,1536]{1,0:T(8,128)(2,1)S(1)}, u32[]{:S(2)}, u32[]{:S(2)}) %collective-permute-start.19) | collective-permute-done | bytes 589856 | tf_op jit(solution)/shard_map/ppermute | solution.py:98
  216.7 42.7 %collective-permute-done.3 = bf16[384,1024]{0,1:T(8,128)(2,1)S(1)} collective-permute-done((bf16[384,1024]{0,1:T(8,128)(2,1)S(1)}, bf16[384,1024]{0,1:T(8,128)(2,1)S(1)}, u32[]{:S(2)}, u32[]{:S(2)}) %collective-permute-start.3) | collective-permute-done | bytes 786464 | tf_op jit(solution)/shard_map/ppermute | solution.py:98
  281.2 11.7 %collective-permute-done.5 = bf16[384,1024]{0,1:T(8,128)(2,1)S(1)} collective-permute-done((bf16[384,1024]{0,1:T(8,128)(2,1)S(1)}, bf16[384,1024]{0,1:T(8,128)(2,1)S(1)}, u32[]{:S(2)}, u32[]{:S(2)}) %collective-permute-start.5) | collective-permute-done | bytes 786464 | tf_op jit(solution)/shard_map/ppermute | solution.py:101
  296.7 13.1 %collective-permute-done.16 = bf16[384,1024]{0,1:T(8,128)(2,1)} collective-permute-done((bf16[384,1024]{0,1:T(8,128)(2,1)}, bf16[384,1024]{0,1:T(8,128)(2,1)}, u32[]{:S(2)}, u32[]{:S(2)}) %collective-permute-start.16) | collective-permute-done | bytes 786464 | tf_op jit(solution)/shard_map/ppermute | solution.py:101
  363.5 36.0 %shard_map.154 = bf16[2112,768]{1,0:T(8,128)(2,1)S(1)} custom-call(s32[6]{0:T(128)S(1)} %iota.91.ids_ref, bf16[2112,768]{1,0:T(8,128)(2,1)} %copy.58.q_ref, bf16[2176,128]{1,0:T(8,128)(2,1)S(1)} %pad.18.k_ref, bf16[2176,128]{1,0:T(8,128)(2,1)S(1)} %pad.19.v_ref), custom_call_target="tpu_custom_call" | custom-call | flops 14118027264 | bytes 7602176 | tf_op jit(solution)/shard_map/pallas_call | solution.py:76
  407.6 36.0 %shard_map.155 = bf16[2112,768]{1,0:T(8,128)(2,1)S(1)} custom-call(s32[6]{0:T(128)S(1)} %iota.94.ids_ref, bf16[2112,768]{1,0:T(8,128)(2,1)} %copy.60.q_ref, bf16[2176,128]{1,0:T(8,128)(2,1)S(1)} %pad.20.k_ref, bf16[2176,128]{1,0:T(8,128)(2,1)S(1)} %pad.21.v_ref), custom_call_target="tpu_custom_call" | custom-call | flops 14118027264 | bytes 7602176 | tf_op jit(solution)/shard_map/pallas_call | solution.py:76
  443.6 10.8 fusion.34
  461.3 20.7 %fusion.32 = f32[1056,4480]{1,0:T(8,128)} fusion(bf16[2,1536,4480]{2,1,0:T(8,128)(2,1)} %param.26, bf16[352,1536]{1,0:T(8,128)(2,1)S(1)} %get-tuple-element.28, bf16[352,1536]{1,0:T(8,128)(2,1)S(1)} %get-tuple-element.29, bf16[352,1536]{1,0:T(8,128)(2,1)S(1)} %get-tuple-element.27), kind=kOutput, calls=%fused_computation.35 | convolution fusion | flops 14542995456 | bytes 35930112 | tf_op jit(solution)/shard_map/dot_general | solution.py:24
  482.0 23.6 %fusion.clone.3.clone.5 = bf16[1056,4480]{1,0:T(8,128)(2,1)} fusion(f32[1056,4480]{1,0:T(8,128)} %fusion.32, bf16[2,1536,4480]{2,1,0:T(8,128)(2,1)} %param.27, bf16[352,1536]{1,0:T(8,128)(2,1)} %copy-done.31, bf16[352,1536]{1,0:T(8,128)(2,1)} %copy-done.32, bf16[352,1536]{1,0:T(8,128)(2,1)S(1)} %get-tuple-element.27), kind=kOutput, calls=%fused_computation.5.clone.clone.clone.clone.clone.clone.clone.2 | convolution fusion | flops 14571380736 | bytes 45391872 | tf_op jit(solution)/shard_map/dot_general | solution.py:24
  505.6 13.1 %fusion.30 = f32[352,4480]{1,0:T(8,128)} fusion(bf16[2,1536,4480]{2,1,0:T(8,128)(2,1)} %param.26, bf16[2112,1536]{1,0:T(8,128)(2,1)} %copy-done.2, s32[]{:T(128)S(6)} %select_n.179), kind=kOutput, calls=%fused_computation.33 | convolution fusion | flops 4844421120 | bytes 21151748 | tf_op jit(solution)/shard_map/dot_general | solution.py:24
  518.7 17.3 %fusion.13 = f32[352,1536]{1,0:T(8,128)} fusion(bf16[2,4480,1536]{2,1,0:T(8,128)(2,1)} %param.28, bf16[2,1536,4480]{2,1,0:T(8,128)(2,1)} %param.27, f32[352,4480]{1,0:T(8,128)} %fusion.30, bf16[2112,1536]{1,0:T(8,128)(2,1)} %copy-done.2, s32[]{:T(128)S(6)} %select_n.179), kind=kOutput, calls=%fused_computation.18 | convolution fusion | flops 9698304000 | bytes 37076996 | tf_op jit(solution)/shard_map/dot_general | solution.py:24
  536.0 13.1 %fusion.28 = f32[352,4480]{1,0:T(8,128)} fusion(bf16[2,1536,4480]{2,1,0:T(8,128)(2,1)} %param.26, bf16[2112,1536]{1,0:T(8,128)(2,1)} %copy-done.2, s32[]{:T(128)S(6)} %select_n.180), kind=kOutput, calls=%fused_computation.31 | convolution fusion | flops 4844421120 | bytes 21151748 | tf_op jit(solution)/shard_map/dot_general | solution.py:24
  549.1 17.4 %fusion.11 = f32[352,1536]{1,0:T(8,128)} fusion(bf16[2,4480,1536]{2,1,0:T(8,128)(2,1)} %param.28, bf16[2,1536,4480]{2,1,0:T(8,128)(2,1)} %param.27, f32[352,4480]{1,0:T(8,128)} %fusion.28, bf16[2112,1536]{1,0:T(8,128)(2,1)} %copy-done.2, s32[]{:T(128)S(6)} %select_n.180), kind=kOutput, calls=%fused_computation.16 | convolution fusion | flops 9698304000 | bytes 37076996 | tf_op jit(solution)/shard_map/dot_general | solution.py:24
  566.5 13.1 %fusion.26 = f32[352,4480]{1,0:T(8,128)} fusion(bf16[2,1536,4480]{2,1,0:T(8,128)(2,1)} %param.26, bf16[2112,1536]{1,0:T(8,128)(2,1)} %copy-done.2, s32[]{:T(128)S(6)} %select_n.181), kind=kOutput, calls=%fused_computation.29 | convolution fusion | flops 4844421120 | bytes 21151748 | tf_op jit(solution)/shard_map/dot_general | solution.py:24
  579.6 17.3 %fusion.9 = f32[352,1536]{1,0:T(8,128)} fusion(bf16[2,4480,1536]{2,1,0:T(8,128)(2,1)} %param.28, bf16[2,1536,4480]{2,1,0:T(8,128)(2,1)} %param.27, f32[352,4480]{1,0:T(8,128)} %fusion.26, bf16[2112,1536]{1,0:T(8,128)(2,1)} %copy-done.2, s32[]{:T(128)S(6)} %select_n.181), kind=kOutput, calls=%fused_computation.14 | convolution fusion | flops 9698304000 | bytes 37076996 | tf_op jit(solution)/shard_map/dot_general | solution.py:24
  613.4 20.7 %collective-permute-done.25 = bf16[1536,512]{1,0:T(8,128)(2,1)} collective-permute-done((bf16[1536,512]{1,0:T(8,128)(2,1)}, bf16[1536,512]{1,0:T(8,128)(2,1)}, u32[]{:S(2)}, u32[]{:S(2)}) %collective-permute-start.25) | collective-permute-done | bytes 1572896 | tf_op jit(solution)/shard_map/ppermute | solution.py:101
  638.8 29.0 %collective-permute-done.41 = bf16[1536,512]{1,0:T(8,128)(2,1)} collective-permute-done((bf16[1536,512]{1,0:T(8,128)(2,1)S(1)}, bf16[1536,512]{1,0:T(8,128)(2,1)}, u32[]{:S(2)}, u32[]{:S(2)}) %collective-permute-start.41) | collective-permute-done | bytes 1572896 | tf_op jit(solution)/shard_map/ppermute | solution.py:101
  674.6 26.0 %collective-permute-done.49 = bf16[1536,512]{1,0:T(8,128)(2,1)S(1)} collective-permute-done((bf16[1536,512]{1,0:T(8,128)(2,1)S(1)}, bf16[1536,512]{1,0:T(8,128)(2,1)S(1)}, u32[]{:S(2)}, u32[]{:S(2)}) %collective-permute-start.49) | collective-permute-done | bytes 1572896 | tf_op jit(solution)/shard_map/ppermute | solution.py:101
  705.2 25.2 %collective-permute-done.12 = f32[352,1536]{1,0:T(8,128)S(1)} collective-permute-done((f32[352,1536]{1,0:T(8,128)S(1)}, f32[352,1536]{1,0:T(8,128)S(1)}, u32[]{:S(2)}, u32[]{:S(2)}) %collective-permute-start.12) | collective-permute-done | bytes 2162720 | tf_op jit(solution)/shard_map/ppermute | solution.py:98
  730.4 46.3 %collective-permute-done.13 = f32[352,1536]{1,0:T(8,128)S(1)} collective-permute-done((f32[352,1536]{1,0:T(8,128)S(1)}, f32[352,1536]{1,0:T(8,128)S(1)}, u32[]{:S(2)}, u32[]{:S(2)}) %collective-permute-start.13) | collective-permute-done | bytes 2162720 | tf_op jit(solution)/shard_map/ppermute | solution.py:98
  778.2 22.9 %fusion.82 = (f32[1056]{0:T(1024)S(1)}, bf16[1056,1536]{1,0:T(8,128)(2,1)S(1)}) fusion(f32[352,1536]{1,0:T(8,128)} %copy-done.95, f32[352,1536]{1,0:T(8,128)} %copy-done.94, f32[352,1536]{1,0:T(8,128)} %copy-done.93, bf16[2,4480,1536]{2,1,0:T(8,128)(2,1)} %param.28, bf16[352,1536]{1,0:T(8,128)(2,1)S(1)} %get-tuple-element.31, ...), kind=kOutput, calls=%fused_computation.86 | convolution fusion | flops 14555970560 | bytes 36204672 | tf_op jit(solution)/shard_map/dot_general | solution.py:24
  860.4 32.9 %collective-permute-done.51 = bf16[256,1536]{1,0:T(8,128)(2,1)} collective-permute-done((bf16[256,1536]{1,0:T(8,128)(2,1)S(1)}, bf16[256,1536]{1,0:T(8,128)(2,1)}, u32[]{:S(2)}, u32[]{:S(2)}) %collective-permute-start.51) | collective-permute-done | bytes 786464 | tf_op jit(solution)/shard_map/ppermute | solution.py:98
  895.1 18.8 %shard_map.156 = bf16[1056,768]{1,0:T(8,128)(2,1)S(1)} custom-call(s32[3]{0:T(128)S(1)} %get-tuple-element.129.ids_ref, bf16[1056,768]{1,0:T(8,128)(2,1)S(1)} %copy.65.q_ref, bf16[2176,128]{1,0:T(8,128)(2,1)S(1)} %get-tuple-element.60.k_ref, bf16[2176,128]{1,0:T(8,128)(2,1)S(1)} %get-tuple-element.58.v_ref), custom_call_target="tpu_custom_call" | custom-call | flops 7059013632 | bytes 4358144 | tf_op jit(solution)/shard_map/pallas_call | solution.py:76
  916.7 18.8 %shard_map.157 = bf16[1056,768]{1,0:T(8,128)(2,1)S(1)} custom-call(s32[3]{0:T(128)S(1)} %get-tuple-element.129.ids_ref, bf16[1056,768]{1,0:T(8,128)(2,1)S(1)} %copy.68.q_ref, bf16[2176,128]{1,0:T(8,128)(2,1)S(1)} %get-tuple-element.59.k_ref, bf16[2176,128]{1,0:T(8,128)(2,1)S(1)} %get-tuple-element.57.v_ref), custom_call_target="tpu_custom_call" | custom-call | flops 7059013632 | bytes 4358144 | tf_op jit(solution)/shard_map/pallas_call | solution.py:76
  940.7 22.1 %fusion.7 = f32[1056,4480]{1,0:T(8,128)} fusion(bf16[2,1536,4480]{2,1,0:T(8,128)(2,1)} %param.26, bf16[1056,1536]{1,0:T(8,128)(2,1)S(1)} %get-tuple-element.142, f32[1536]{0:T(1024)S(1)} %copy-done.83, f32[1056]{0:T(1024)S(1)} %add_rsqrt_fusion.3), kind=kOutput, calls=%fused_computation.12 | convolution fusion | flops 14539751424 | bytes 35940480 | tf_op jit(solution)/shard_map/dot_general | solution.py:24
  962.7 23.8 %fusion.1.clone.5 = bf16[1056,4480]{1,0:T(8,128)(2,1)} fusion(f32[1056,4480]{1,0:T(8,128)} %fusion.7, bf16[2,1536,4480]{2,1,0:T(8,128)(2,1)} %param.27, bf16[1056,1536]{1,0:T(8,128)(2,1)S(1)} %get-tuple-element.142, f32[1536]{0:T(1024)S(1)} %copy-done.83, f32[1056]{0:T(1024)S(1)} %add_rsqrt_fusion.3), kind=kOutput, calls=%fused_computation.6.clone.clone.clone.2 | convolution fusion | flops 14568136704 | bytes 45402240 | tf_op jit(solution)/shard_map/dot_general | solution.py:24
  986.5 22.5 %fusion.2 = f32[1056,1536]{1,0:T(8,128)} fusion(bf16[2,4480,1536]{2,1,0:T(8,128)(2,1)} %param.28, bf16[1056,4480]{1,0:T(8,128)(2,1)} %fusion.1.clone.5), kind=kOutput, calls=%fused_computation.9 | convolution fusion | flops 14533263360 | bytes 29712384 | tf_op jit(solution)/shard_map/dot_general | solution.py:24
  1022.8 14.1 %fusion.186 = f32[1056,1536]{1,0:T(8,128)} fusion(f32[1056,1024]{1,0:T(8,128)} %fusion.168, bf16[1536,256]{1,0:T(8,128)(2,1)} %get-tuple-element.83, bf16[1536,256]{1,0:T(8,128)(2,1)S(1)} %copy-done.51, bf16[1536,256]{1,0:T(8,128)(2,1)S(1)} %copy-done.52, bf16[1536,256]{1,0:T(8,128)(2,1)S(1)} %copy-done.39, bf16[256,1536]{1,0:T(8,128)(2,1)} %collective-permute-done.46, ...), kind=kOutput, calls=%fused_computation.192 | convolution fusion | flops 6681919488 | bytes 20359296 | tf_op jit(solution)/shard_map/dot_general | solution.py:24
  1048.2 14.1 %fusion.214 = f32[1056,1536]{1,0:T(8,128)} fusion(f32[1056,1024]{1,0:T(8,128)} %fusion.196, bf16[1536,256]{1,0:T(8,128)(2,1)} %get-tuple-element.91, bf16[1536,256]{1,0:T(8,128)(2,1)S(1)} %copy-done.47, bf16[1536,256]{1,0:T(8,128)(2,1)S(1)} %copy-done.48, bf16[1536,256]{1,0:T(8,128)(2,1)S(1)} %copy-done.38, bf16[256,1536]{1,0:T(8,128)(2,1)} %collective-permute-done.54, ...), kind=kOutput, calls=%fused_computation.216 | convolution fusion | flops 6681919488 | bytes 20359296 | tf_op jit(solution)/shard_map/dot_general | solution.py:24
  1071.3 16.2 %convolution_add_fusion.3 = f32[1056,1536]{1,0:T(8,128)} fusion(f32[1056,1536]{1,0:T(8,128)} %fusion.2, f32[1056,1024]{1,0:T(8,128)} %fusion.116, bf16[1536,256]{1,0:T(8,128)(2,1)} %get-tuple-element.75, bf16[1536,256]{1,0:T(8,128)(2,1)S(1)} %copy-done.45, bf16[1536,256]{1,0:T(8,128)(2,1)S(1)} %copy-done.46, bf16[1536,256]{1,0:T(8,128)(2,1)S(1)} %copy-done.36, ...), kind=kOutput, calls=%fused_computation.56 | convolution fusion | flops 6683541504 | bytes 26847360 | tf_op jit(solution)/shard_map/dot_general | solution.py:24
  1102.2 23.1 %fusion.79 = (f32[1056]{0:T(1024)S(1)}, bf16[1056,1536]{1,0:T(8,128)(2,1)}) fusion(f32[1056,1536]{1,0:T(8,128)} %fusion.261, f32[1056,1536]{1,0:T(8,128)} %fusion.214, f32[1056,1536]{1,0:T(8,128)} %fusion.186, f32[1056,1536]{1,0:T(8,128)} %convolution_add_fusion.3, bf16[256,1536]{1,0:T(8,128)(2,1)} %collective-permute-done.38, ...), kind=kOutput, calls=%fused_computation.83 | convolution fusion | flops 6698138624 | bytes 43071744 | tf_op jit(solution)/shard_map/dot_general | solution.py:24
  (497 shorter events, 420.2 us)
Async XLA Ops:
  0.0 110.9 %collective-permute-start.1 = (bf16[16,1536]{1,0:T(8,128)(2,1)}, bf16[16,1536]{1,0:T(8,128)(2,1)}, u32[]{:S(2)}, u32[]{:S(2)}) collective-permute-start(bf16[16,1536]{1,0:T(8,128)(2,1)} %param.16), channel_id=1, source_target_pairs={{0,2},{1,3},{2,0},{3,1},{4,6},{5,7},{6,4},{7,5}} | collective-permute-start | bytes 147464 | tf_op jit(solution)/shard_map/ppermute | solution.py:101
  3.3 111.9 %collective-permute-start = (bf16[16,1536]{1,0:T(8,128)(2,1)}, bf16[16,1536]{1,0:T(8,128)(2,1)}, u32[]{:S(2)}, u32[]{:S(2)}) collective-permute-start(bf16[16,1536]{1,0:T(8,128)(2,1)} %param.16), channel_id=1, source_target_pairs={{0,1},{1,0},{2,3},{3,2},{4,5},{5,4},{6,7},{7,6}} | collective-permute-start | bytes 147464 | tf_op jit(solution)/shard_map/ppermute | solution.py:102
  8.5 159.2 %collective-permute-start.7 = (bf16[192,1536]{1,0:T(8,128)(2,1)}, bf16[192,1536]{1,0:T(8,128)(2,1)}, u32[]{:S(2)}, u32[]{:S(2)}) collective-permute-start(bf16[192,1536]{1,0:T(8,128)(2,1)} %constant_dynamic-slice_fusion.18), channel_id=1, source_target_pairs={{0,4},{4,0},{1,5},{5,1},{2,6},{6,2},{3,7},{7,3}} | collective-permute-start | bytes 1769480 | tf_op jit(solution)/shard_map/ppermute | solution.py:98
  44.3 120.3 %collective-permute-start.31 = (bf16[1536,512]{1,0:T(8,128)(2,1)}, bf16[1536,512]{1,0:T(8,128)(2,1)}, u32[]{:S(2)}, u32[]{:S(2)}) collective-permute-start(bf16[1536,512]{1,0:T(8,128)(2,1)} %pad_maximum_fusion.12), channel_id=1, source_target_pairs={{0,4},{4,0},{1,5},{5,1},{2,6},{6,2},{3,7},{7,3}} | collective-permute-start | bytes 4718600 | tf_op jit(solution)/shard_map/ppermute | solution.py:98
  46.0 165.2 %collective-permute-start.23 = (bf16[1536,512]{1,0:T(8,128)(2,1)}, bf16[1536,512]{1,0:T(8,128)(2,1)}, u32[]{:S(2)}, u32[]{:S(2)}) collective-permute-start(bf16[1536,512]{1,0:T(8,128)(2,1)} %pad_maximum_fusion.11), channel_id=1, source_target_pairs={{0,4},{4,0},{1,5},{5,1},{2,6},{6,2},{3,7},{7,3}} | collective-permute-start | bytes 4718600 | tf_op jit(solution)/shard_map/ppermute | solution.py:98
  160.8 53.1 %collective-permute-start.39 = (bf16[1536,512]{1,0:T(8,128)(2,1)}, bf16[1536,512]{1,0:T(8,128)(2,1)S(1)}, u32[]{:S(2)}, u32[]{:S(2)}) collective-permute-start(bf16[1536,512]{1,0:T(8,128)(2,1)} %pad_maximum_fusion.13), channel_id=1, source_target_pairs={{0,4},{4,0},{1,5},{5,1},{2,6},{6,2},{3,7},{7,3}} | collective-permute-start | bytes 4718600 | tf_op jit(solution)/shard_map/ppermute | solution.py:98
  162.2 48.6 %collective-permute-start.19 = (bf16[192,1536]{1,0:T(8,128)(2,1)S(1)}, bf16[192,1536]{1,0:T(8,128)(2,1)S(1)}, u32[]{:S(2)}, u32[]{:S(2)}) collective-permute-start(bf16[192,1536]{1,0:T(8,128)(2,1)S(1)} %copy-done.61), channel_id=1, source_target_pairs={{0,4},{4,0},{1,5},{5,1},{2,6},{6,2},{3,7},{7,3}} | collective-permute-start | bytes 1769480 | tf_op jit(solution)/shard_map/ppermute | solution.py:98
  164.6 95.3 %collective-permute-start.47 = (bf16[1536,512]{1,0:T(8,128)(2,1)S(1)}, bf16[1536,512]{1,0:T(8,128)(2,1)S(1)}, u32[]{:S(2)}, u32[]{:S(2)}) collective-permute-start(bf16[1536,512]{1,0:T(8,128)(2,1)S(1)} %pad_maximum_fusion.14), channel_id=1, source_target_pairs={{0,4},{4,0},{1,5},{5,1},{2,6},{6,2},{3,7},{7,3}} | collective-permute-start | bytes 4718600 | tf_op jit(solution)/shard_map/ppermute | solution.py:98
  167.8 91.6 %collective-permute-start.3 = (bf16[384,1024]{0,1:T(8,128)(2,1)S(1)}, bf16[384,1024]{0,1:T(8,128)(2,1)S(1)}, u32[]{:S(2)}, u32[]{:S(2)}) collective-permute-start(bf16[384,1024]{0,1:T(8,128)(2,1)S(1)} %copy-done.34), channel_id=1, source_target_pairs={{0,4},{4,0},{1,5},{5,1},{2,6},{6,2},{3,7},{7,3}} | collective-permute-start | bytes 2359304 | tf_op jit(solution)/shard_map/ppermute | solution.py:98
  210.7 49.2 %collective-permute-start.9 = (bf16[192,1536]{1,0:T(8,128)(2,1)}, bf16[192,1536]{1,0:T(8,128)(2,1)S(1)}, u32[]{:S(2)}, u32[]{:S(2)}) collective-permute-start(bf16[192,1536]{1,0:T(8,128)(2,1)} %collective-permute-done.7), channel_id=1, source_target_pairs={{0,2},{1,3},{2,0},{3,1},{4,6},{5,7},{6,4},{7,5}} | collective-permute-start | bytes 1769480 | tf_op jit(solution)/shard_map/ppermute | solution.py:101
  211.2 49.3 %collective-permute-start.64 = (bf16[1536,256]{1,0:T(8,128)(2,1)}, bf16[1536,256]{1,0:T(8,128)(2,1)S(1)}, u32[]{:S(2)}, u32[]{:S(2)}) collective-permute-start(bf16[1536,256]{1,0:T(8,128)(2,1)} %collective-permute-done.63), channel_id=1, source_target_pairs={{0,1},{1,0},{2,3},{3,2},{4,5},{5,4},{6,7},{7,6}} | collective-permute-start | bytes 2359304 | tf_op jit(solution)/shard_map/ppermute | solution.py:102
  213.9 49.1 %collective-permute-start.65 = (bf16[1536,256]{1,0:T(8,128)(2,1)}, bf16[1536,256]{1,0:T(8,128)(2,1)}, u32[]{:S(2)}, u32[]{:S(2)}) collective-permute-start(bf16[1536,256]{1,0:T(8,128)(2,1)} %collective-permute-done.63), channel_id=1, source_target_pairs={{0,2},{1,3},{2,0},{3,1},{4,6},{5,7},{6,4},{7,5}} | collective-permute-start | bytes 2359304 | tf_op jit(solution)/shard_map/ppermute | solution.py:101
  280.7 318.9 %collective-permute-start.15 = (bf16[384,1024]{0,1:T(8,128)(2,1)}, bf16[384,1024]{0,1:T(8,128)(2,1)}, u32[]{:S(2)}, u32[]{:S(2)}) collective-permute-start(bf16[384,1024]{0,1:T(8,128)(2,1)} %collective-permute-done.14), channel_id=1, source_target_pairs={{0,1},{1,0},{2,3},{3,2},{4,5},{5,4},{6,7},{7,6}} | collective-permute-start | bytes 2359304 | tf_op jit(solution)/shard_map/ppermute | solution.py:102
  295.2 311.6 %collective-permute-start.33 = (bf16[1536,512]{1,0:T(8,128)(2,1)}, bf16[1536,512]{1,0:T(8,128)(2,1)}, u32[]{:S(2)}, u32[]{:S(2)}) collective-permute-start(bf16[1536,512]{1,0:T(8,128)(2,1)} %collective-permute-done.31), channel_id=1, source_target_pairs={{0,2},{1,3},{2,0},{3,1},{4,6},{5,7},{6,4},{7,5}} | collective-permute-start | bytes 4718600 | tf_op jit(solution)/shard_map/ppermute | solution.py:101
  296.7 313.2 %collective-permute-start.32 = (bf16[1536,512]{1,0:T(8,128)(2,1)}, bf16[1536,512]{1,0:T(8,128)(2,1)}, u32[]{:S(2)}, u32[]{:S(2)}) collective-permute-start(bf16[1536,512]{1,0:T(8,128)(2,1)} %collective-permute-done.31), channel_id=1, source_target_pairs={{0,1},{1,0},{2,3},{3,2},{4,5},{5,4},{6,7},{7,6}} | collective-permute-start | bytes 4718600 | tf_op jit(solution)/shard_map/ppermute | solution.py:102
  309.8 287.1 %collective-permute-start.66 = (bf16[1536,256]{1,0:T(8,128)(2,1)}, bf16[1536,256]{1,0:T(8,128)(2,1)}, u32[]{:S(2)}, u32[]{:S(2)}) collective-permute-start(bf16[1536,256]{1,0:T(8,128)(2,1)} %collective-permute-done.65), channel_id=1, source_target_pairs={{0,1},{1,0},{2,3},{3,2},{4,5},{5,4},{6,7},{7,6}} | collective-permute-start | bytes 2359304 | tf_op jit(solution)/shard_map/ppermute | solution.py:102
  309.8 289.8 %collective-permute-start.17 = (bf16[384,1024]{0,1:T(8,128)(2,1)}, bf16[384,1024]{0,1:T(8,128)(2,1)}, u32[]{:S(2)}, u32[]{:S(2)}) collective-permute-start(bf16[384,1024]{0,1:T(8,128)(2,1)} %collective-permute-done.16), channel_id=1, source_target_pairs={{0,1},{1,0},{2,3},{3,2},{4,5},{5,4},{6,7},{7,6}} | collective-permute-start | bytes 2359304 | tf_op jit(solution)/shard_map/ppermute | solution.py:102
  599.6 68.2 %collective-permute-start.41 = (bf16[1536,512]{1,0:T(8,128)(2,1)S(1)}, bf16[1536,512]{1,0:T(8,128)(2,1)}, u32[]{:S(2)}, u32[]{:S(2)}) collective-permute-start(bf16[1536,512]{1,0:T(8,128)(2,1)S(1)} %copy-done.20), channel_id=1, source_target_pairs={{0,2},{1,3},{2,0},{3,1},{4,6},{5,7},{6,4},{7,5}} | collective-permute-start | bytes 4718600 | tf_op jit(solution)/shard_map/ppermute | solution.py:101
  606.9 63.8 %collective-permute-start.40 = (bf16[1536,512]{1,0:T(8,128)(2,1)S(1)}, bf16[1536,512]{1,0:T(8,128)(2,1)S(1)}, u32[]{:S(2)}, u32[]{:S(2)}) collective-permute-start(bf16[1536,512]{1,0:T(8,128)(2,1)S(1)} %copy-done.20), channel_id=1, source_target_pairs={{0,1},{1,0},{2,3},{3,2},{4,5},{5,4},{6,7},{7,6}} | collective-permute-start | bytes 4718600 | tf_op jit(solution)/shard_map/ppermute | solution.py:102
  609.8 90.8 %collective-permute-start.49 = (bf16[1536,512]{1,0:T(8,128)(2,1)S(1)}, bf16[1536,512]{1,0:T(8,128)(2,1)S(1)}, u32[]{:S(2)}, u32[]{:S(2)}) collective-permute-start(bf16[1536,512]{1,0:T(8,128)(2,1)S(1)} %copy-done.18), channel_id=1, source_target_pairs={{0,2},{1,3},{2,0},{3,1},{4,6},{5,7},{6,4},{7,5}} | collective-permute-start | bytes 4718600 | tf_op jit(solution)/shard_map/ppermute | solution.py:101
  634.2 71.0 %collective-permute-start.11 = (f32[352,1536]{1,0:T(8,128)S(1)}, f32[352,1536]{1,0:T(8,128)S(1)}, u32[]{:S(2)}, u32[]{:S(2)}) collective-permute-start(f32[352,1536]{1,0:T(8,128)S(1)} %copy-done.92), channel_id=1, source_target_pairs={{0,4},{4,0},{1,5},{5,1},{2,6},{6,2},{3,7},{7,3}} | collective-permute-start | bytes 6488072 | tf_op jit(solution)/shard_map/ppermute | solution.py:98
  638.4 92.0 %collective-permute-start.12 = (f32[352,1536]{1,0:T(8,128)S(1)}, f32[352,1536]{1,0:T(8,128)S(1)}, u32[]{:S(2)}, u32[]{:S(2)}) collective-permute-start(f32[352,1536]{1,0:T(8,128)S(1)} %copy-done.91), channel_id=1, source_target_pairs={{0,4},{4,0},{1,5},{5,1},{2,6},{6,2},{3,7},{7,3}} | collective-permute-start | bytes 6488072 | tf_op jit(solution)/shard_map/ppermute | solution.py:98
  667.9 108.9 %collective-permute-start.13 = (f32[352,1536]{1,0:T(8,128)S(1)}, f32[352,1536]{1,0:T(8,128)S(1)}, u32[]{:S(2)}, u32[]{:S(2)}) collective-permute-start(f32[352,1536]{1,0:T(8,128)S(1)} %copy-done.90), channel_id=1, source_target_pairs={{0,4},{4,0},{1,5},{5,1},{2,6},{6,2},{3,7},{7,3}} | collective-permute-start | bytes 6488072 | tf_op jit(solution)/shard_map/ppermute | solution.py:98
  700.6 319.9 %collective-permute-start.27 = (bf16[256,1536]{1,0:T(8,128)(2,1)}, bf16[256,1536]{1,0:T(8,128)(2,1)}, u32[]{:S(2)}, u32[]{:S(2)}) collective-permute-start(bf16[256,1536]{1,0:T(8,128)(2,1)} %get-tuple-element.22), channel_id=1, source_target_pairs={{0,4},{4,0},{1,5},{5,1},{2,6},{6,2},{3,7},{7,3}} | collective-permute-start | bytes 2359304 | tf_op jit(solution)/shard_map/ppermute | solution.py:98
  703.4 150.5 %collective-permute-start.43 = (bf16[256,1536]{1,0:T(8,128)(2,1)}, bf16[256,1536]{1,0:T(8,128)(2,1)}, u32[]{:S(2)}, u32[]{:S(2)}) collective-permute-start(bf16[256,1536]{1,0:T(8,128)(2,1)} %get-tuple-element.21), channel_id=1, source_target_pairs={{0,4},{4,0},{1,5},{5,1},{2,6},{6,2},{3,7},{7,3}} | collective-permute-start | bytes 2359304 | tf_op jit(solution)/shard_map/ppermute | solution.py:98
  705.2 141.8 %collective-permute-start.34 = (bf16[1536,512]{1,0:T(8,128)(2,1)}, bf16[1536,512]{1,0:T(8,128)(2,1)}, u32[]{:S(2)}, u32[]{:S(2)}) collective-permute-start(bf16[1536,512]{1,0:T(8,128)(2,1)} %collective-permute-done.33), channel_id=1, source_target_pairs={{0,1},{1,0},{2,3},{3,2},{4,5},{5,4},{6,7},{7,6}} | collective-permute-start | bytes 4718600 | tf_op jit(solution)/shard_map/ppermute | solution.py:102
  730.4 119.3 %collective-permute-start.26 = (bf16[1536,512]{1,0:T(8,128)(2,1)}, bf16[1536,512]{1,0:T(8,128)(2,1)}, u32[]{:S(2)}, u32[]{:S(2)}) collective-permute-start(bf16[1536,512]{1,0:T(8,128)(2,1)} %collective-permute-done.25), channel_id=1, source_target_pairs={{0,1},{1,0},{2,3},{3,2},{4,5},{5,4},{6,7},{7,6}} | collective-permute-start | bytes 4718600 | tf_op jit(solution)/shard_map/ppermute | solution.py:102
  776.8 77.7 %collective-permute-start.42 = (bf16[1536,512]{1,0:T(8,128)(2,1)}, bf16[1536,512]{1,0:T(8,128)(2,1)}, u32[]{:S(2)}, u32[]{:S(2)}) collective-permute-start(bf16[1536,512]{1,0:T(8,128)(2,1)} %collective-permute-done.41), channel_id=1, source_target_pairs={{0,1},{1,0},{2,3},{3,2},{4,5},{5,4},{6,7},{7,6}} | collective-permute-start | bytes 4718600 | tf_op jit(solution)/shard_map/ppermute | solution.py:102
  857.7 162.8 %collective-permute-start.59 = (bf16[96,1536]{1,0:T(8,128)(2,1)}, bf16[96,1536]{1,0:T(8,128)(2,1)}, u32[]{:S(2)}, u32[]{:S(2)}) collective-permute-start(bf16[96,1536]{1,0:T(8,128)(2,1)} %dynamic-slice_bitcast_fusion.28), channel_id=1, source_target_pairs={{0,4},{4,0},{1,5},{5,1},{2,6},{6,2},{3,7},{7,3}} | collective-permute-start | bytes 884744 | tf_op jit(solution)/shard_map/ppermute | solution.py:98
  893.3 128.7 %collective-permute-start.44 = (bf16[256,1536]{1,0:T(8,128)(2,1)}, bf16[256,1536]{1,0:T(8,128)(2,1)}, u32[]{:S(2)}, u32[]{:S(2)}) collective-permute-start(bf16[256,1536]{1,0:T(8,128)(2,1)} %collective-permute-done.43), channel_id=1, source_target_pairs={{0,1},{1,0},{2,3},{3,2},{4,5},{5,4},{6,7},{7,6}} | collective-permute-start | bytes 2359304 | tf_op jit(solution)/shard_map/ppermute | solution.py:102
  893.3 128.7 %collective-permute-start.53 = (bf16[256,1536]{1,0:T(8,128)(2,1)}, bf16[256,1536]{1,0:T(8,128)(2,1)}, u32[]{:S(2)}, u32[]{:S(2)}) collective-permute-start(bf16[256,1536]{1,0:T(8,128)(2,1)} %collective-permute-done.51), channel_id=1, source_target_pairs={{0,2},{1,3},{2,0},{3,1},{4,6},{5,7},{6,4},{7,5}} | collective-permute-start | bytes 2359304 | tf_op jit(solution)/shard_map/ppermute | solution.py:101
  893.9 128.7 %collective-permute-start.46 = (bf16[256,1536]{1,0:T(8,128)(2,1)}, bf16[256,1536]{1,0:T(8,128)(2,1)}, u32[]{:S(2)}, u32[]{:S(2)}) collective-permute-start(bf16[256,1536]{1,0:T(8,128)(2,1)} %collective-permute-done.45), channel_id=1, source_target_pairs={{0,1},{1,0},{2,3},{3,2},{4,5},{5,4},{6,7},{7,6}} | collective-permute-start | bytes 2359304 | tf_op jit(solution)/shard_map/ppermute | solution.py:102
  (138 other events, 2356.5 us)

commit v2 on v1

v2 whole, which is shorter than its diff:
```python
import functools

import jax
import jax.numpy as jnp
from jax import lax
from jax.experimental import pallas as pl
from jax.experimental.pallas import tpu as pltpu
from jax.sharding import PartitionSpec as P


EPS = 1e-6
ROPE_BASE = 10000.0
HEAD = 128
BLOCK = 352
TILE = 896
OWNED = ((0, 3, 5), (1, 2, 4))
CHUNKS = (384, 256, 256, 128)
TAIL = 128
MIB = 2**20


def dot(a, b):
    return jnp.dot(a, b, preferred_element_type=jnp.float32)


def normalize(x, gain):
    f = x.astype(jnp.float32)
    inv_rms = lax.rsqrt(jnp.mean(f * f, axis=-1, keepdims=True) + EPS)
    return (f * inv_rms * gain).astype(jnp.bfloat16)


def params(vmem_mib):
    return pltpu.CompilerParams(dimension_semantics=("arbitrary",), vmem_limit_bytes=vmem_mib * MIB)


def cost(flops, data):
    return pl.CostEstimate(flops=int(flops), bytes_accessed=int(data), transcendentals=0)


def project_kernel(q_width, ids_ref, x_ref, gain_ref, w_ref, cos_ref, sin_ref, q_ref, k_ref, v_ref):
    h = normalize(x_ref[...], gain_ref[...])
    f = dot(h, w_ref[...])
    cos_part, sin_part = cos_ref[...], sin_ref[...]
    for i in range(q_width // HEAD + 1):
        a = f[:, i * HEAD:(i + 1) * HEAD]
        r = (a * cos_part + pltpu.roll(a, HEAD // 2, 1) * sin_part).astype(jnp.bfloat16)
        if i < q_width // HEAD:
            q_ref[:, i * HEAD:(i + 1) * HEAD] = r
        else:
            k_ref[...] = r
    v_ref[...] = f[:, q_width + HEAD:].astype(jnp.bfloat16)


def project(ids, x, gain, w, cos_all, sin_all, key_rows):
    rows, dim = x.shape
    width = w.shape[1]
    q_width = width - 2 * HEAD
    row = lambda b, ids: (b, 0)
    whole = lambda b, ids: (0, 0)
    table = lambda b, ids: (ids[b], 0)
    return pl.pallas_call(
        functools.partial(project_kernel, q_width),
        grid_spec=pltpu.PrefetchScalarGridSpec(
            num_scalar_prefetch=1,
            grid=(rows // BLOCK,),
            in_specs=[
                pl.BlockSpec((BLOCK, dim), row),
                pl.BlockSpec((1, dim), whole),
                pl.BlockSpec((dim, width), whole),
                pl.BlockSpec((BLOCK, HEAD), table),
                pl.BlockSpec((BLOCK, HEAD), table),
            ],
            out_specs=[pl.BlockSpec((BLOCK, q_width), row), pl.BlockSpec((BLOCK, HEAD), row), pl.BlockSpec((BLOCK, HEAD), row)],
        ),
        out_shape=[
            jax.ShapeDtypeStruct((rows, q_width), jnp.bfloat16),
            jax.ShapeDtypeStruct((key_rows, HEAD), jnp.bfloat16),
            jax.ShapeDtypeStruct((key_rows, HEAD), jnp.bfloat16),
        ],
        compiler_params=params(40),
        cost_estimate=cost(2 * rows * dim * width, 2 * (rows * dim + dim * width + rows * width)),
    )(ids, x, gain[None, :], w, cos_all, sin_all)


def attention_kernel(num_blocks, heads, ids_ref, q_ref, k_ref, v_ref, o_ref):
    block_id = ids_ref[pl.program_id(1)]
    rows = q_ref.shape[0]
    nt = (((1,), (1,)), ((), ()))
    scale = HEAD ** -0.5

    def body(i):
        first = i * rows
        low = first // 128 * 128
        high = -(-(first + rows) // 128) * 128
        row = first + lax.broadcasted_iota(jnp.int32, (rows, high - low), 0)
        col = low + lax.broadcasted_iota(jnp.int32, (rows, high - low), 1)
        seen = col <= row
        v_hi = v_ref[low:high, :]
        if high > num_blocks * rows:
            at = low + lax.broadcasted_iota(jnp.int32, v_hi.shape, 0)
            v_hi = jnp.where(at < num_blocks * rows, v_hi, jnp.zeros_like(v_hi))
        for h in range(heads):
            q = q_ref[:, h * HEAD:(h + 1) * HEAD]
            s_hi = lax.dot_general(q, k_ref[low:high, :], nt, preferred_element_type=jnp.float32)
            s_hi = jnp.where(seen, s_hi, -jnp.inf)
            m = jnp.max(s_hi, axis=-1, keepdims=True)
            if low:
                s_lo = lax.dot_general(q, k_ref[:low, :], nt, preferred_element_type=jnp.float32)
                m = jnp.maximum(m, jnp.max(s_lo, axis=-1, keepdims=True))
            p_hi = jnp.exp((s_hi - m) * scale)
            total = jnp.sum(p_hi, axis=-1, keepdims=True)
            out = dot(p_hi.astype(jnp.bfloat16), v_hi)
            if low:
                p_lo = jnp.exp((s_lo - m) * scale)
                total = total + jnp.sum(p_lo, axis=-1, keepdims=True)
                out = out + dot(p_lo.astype(jnp.bfloat16), v_ref[:low, :])
            o_ref[:, h * HEAD:(h + 1) * HEAD] = (out / total).astype(jnp.bfloat16)

    for i in range(num_blocks):
        pl.when(block_id == i)(functools.partial(body, i))


def attention(ids, q, k, v, num_blocks):
    rows, width = q.shape
    per_step = 2
    keys = k.shape[0]
    return pl.pallas_call(
        functools.partial(attention_kernel, num_blocks, per_step),
        grid_spec=pltpu.PrefetchScalarGridSpec(
            num_scalar_prefetch=1,
            grid=(width // (per_step * HEAD), rows // BLOCK),
            in_specs=[
                pl.BlockSpec((BLOCK, per_step * HEAD), lambda h, b, ids: (b, h)),
                pl.BlockSpec((keys, HEAD), lambda h, b, ids: (0, 0)),
                pl.BlockSpec((keys, HEAD), lambda h, b, ids: (0, 0)),
            ],
            out_specs=pl.BlockSpec((BLOCK, per_step * HEAD), lambda h, b, ids: (b, h)),
        ),
        out_shape=jax.ShapeDtypeStruct((rows, width), jnp.bfloat16),
        compiler_params=pltpu.CompilerParams(
            dimension_semantics=("arbitrary", "arbitrary"), vmem_limit_bytes=40 * MIB),
        cost_estimate=cost(8 * rows * keys * width, rows * width * 4 + keys * HEAD * 4),
    )(ids, q, k, v)


def output_kernel(x_ref, a_ref, b_ref, wa_ref, wb_ref, gain_ref, x_out, u_out):
    total = dot(a_ref[...], wa_ref[0]) + dot(b_ref[...], wb_ref[...])
    x = (x_ref[...].astype(jnp.float32) + total).astype(jnp.bfloat16)
    x_out[...] = x
    u_out[...] = normalize(x, gain_ref[...])


def project_out(layer, x, a, b, w_own, w_far, gain):
    rows, dim = x.shape
    width = a.shape[1]
    row = lambda i: (i, 0)
    return pl.pallas_call(
        output_kernel,
        grid=(rows // BLOCK,),
        in_specs=[
            pl.BlockSpec((BLOCK, dim), row),
            pl.BlockSpec((BLOCK, width), row),
            pl.BlockSpec((BLOCK, width), row),
            pl.BlockSpec((1, width, dim), lambda i: (layer, 0, 0)),
            pl.BlockSpec((width, dim), lambda i: (0, 0)),
            pl.BlockSpec((1, dim), lambda i: (0, 0)),
        ],
        out_specs=[pl.BlockSpec((BLOCK, dim), row), pl.BlockSpec((BLOCK, dim), row)],
        out_shape=[jax.ShapeDtypeStruct((rows, dim), jnp.bfloat16)] * 2,
        compiler_params=params(40),
        cost_estimate=cost(4 * rows * dim * width, 6 * rows * dim + 8 * width * dim),
    )(x, a, b, w_own, w_far, gain[None, :])


def mlp_rows(u_ref, out_ref, gate, up, down, fresh):
    def rows(i, _):
        at = pl.ds(pl.multiple_of(i * BLOCK, BLOCK), BLOCK)
        u = u_ref[at, :]
        g = dot(u, gate())
        inner = (jax.nn.silu(g) * dot(u, up())).astype(jnp.bfloat16)
        part = dot(inner, down())
        if fresh is None:
            out_ref[at, :] += part
        else:
            out_ref[at, :] = jnp.where(fresh, part, out_ref[at, :] + part)
        return 0

    n = u_ref.shape[0] // BLOCK
    if n == 1:
        rows(0, 0)
    else:
        lax.fori_loop(0, n, rows, 0)


def mlp_kernel(ids_ref, u_ref, gate_ref, up_ref, down_ref, out_ref):
    first = pl.program_id(0) == 0

    @pl.when(first)
    def _():
        out_ref[...] = jnp.zeros_like(out_ref)

    mlp_rows(u_ref, out_ref, lambda: gate_ref[0], lambda: up_ref[0], lambda: down_ref[0], None)


def mlp_own(layer, ids, u, rows, w_gate, w_up, w_down):
    dim = u.shape[1]
    ffn = w_gate.shape[2]
    return pl.pallas_call(
        mlp_kernel,
        grid_spec=pltpu.PrefetchScalarGridSpec(
            num_scalar_prefetch=1,
            grid=(ffn // TILE,),
            in_specs=[
                pl.BlockSpec((rows, dim), lambda j, ids: (ids[0], 0)),
                pl.BlockSpec((1, dim, TILE), lambda j, ids: (layer, 0, j)),
                pl.BlockSpec((1, dim, TILE), lambda j, ids: (layer, 0, j)),
                pl.BlockSpec((1, TILE, dim), lambda j, ids: (layer, j, 0)),
            ],
            out_specs=pl.BlockSpec((rows, dim), lambda j, ids: (0, 0)),
        ),
        out_shape=jax.ShapeDtypeStruct((rows, dim), jnp.float32),
        compiler_params=params(56),
        cost_estimate=cost(6 * rows * dim * ffn, 6 * dim * ffn + 6 * rows * dim),
    )(ids, u, w_gate, w_up, w_down)


def mlp_pieces_kernel(n, u_ref, acc_ref, *refs):
    wide, tall = refs[:n], refs[n:2 * n]
    out_ref, wide_v, tall_v, sems = refs[2 * n:]
    size = wide_v.shape[2] // 2
    copies = []
    for j in range(n):
        pair = (pltpu.make_async_copy(wide[j], wide_v.at[j], sems.at[2 * j]), pltpu.make_async_copy(tall[j], tall_v.at[j], sems.at[2 * j + 1]))
        for c in pair:
            c.start()
        copies.append(pair)
    out_ref[...] = acc_ref[...]
    for j in range(n):
        for c in copies[j]:
            c.wait()
        mlp_rows(u_ref, out_ref, lambda: wide_v[j, :, :size], lambda: wide_v[j, :, size:], lambda: tall_v[j], None)


def mlp_pieces(u, acc, wide, tall):
    rows, dim = u.shape
    size = tall[0].shape[0]
    n = len(wide)
    vmem = pl.BlockSpec(memory_space=pltpu.VMEM)
    hbm = pl.BlockSpec(memory_space=pl.ANY)
    return pl.pallas_call(
        functools.partial(mlp_pieces_kernel, n),
        in_specs=[vmem, vmem] + [hbm] * (2 * n),
        out_specs=vmem,
        out_shape=jax.ShapeDtypeStruct((rows, dim), jnp.float32),
        scratch_shapes=[
            pltpu.VMEM((n, dim, 2 * size), jnp.bfloat16),
            pltpu.VMEM((n, size, dim), jnp.bfloat16),
            pltpu.SemaphoreType.DMA((2 * n,)),
        ],
        compiler_params=pltpu.CompilerParams(vmem_limit_bytes=56 * MIB),
        cost_estimate=cost(6 * rows * dim * size * n, 6 * dim * size * n + 10 * rows * dim),
    )(u, acc, *wide, *tall)


def solution(mesh):
    groups = mesh.shape['resp']
    row_axes = ('prompts', 'resp')
    head_spec = P(None, None, 'model', None)
    in_specs = (P(row_axes, None), P(row_axes, None, None), P(row_axes, None), P(row_axes), P(None, None), head_spec, head_spec, head_spec, P(None, 'model', None, None), P(None, None), P(None, None, 'model'), P(None, None, 'model'), P(None, 'model', None), P(None), P(None, 'model'))
    across = [(0, 1), (1, 0)]
    core = [(i, i ^ 1) for i in range(groups)]
    chip = [(i, i ^ 2) for i in range(groups)]
    both = [(i, i ^ 3) for i in range(groups)]

    def swap(a):
        return lax.ppermute(a, 'model', across)

    def spread(a):
        return [a, lax.ppermute(a, 'resp', core), lax.ppermute(a, 'resp', chip), lax.ppermute(a, 'resp', both)]

    def device_body(x_prompt, x_resp, targets, resp_lens, attn_gain, w_query, w_key, w_value, w_out, mlp_gain, w_gate, w_up, w_down, final_gain, w_vocab):
        me = lax.axis_index('resp')
        side = lax.axis_index('model')
        resp_len = x_resp.shape[1]
        dim = x_resp.shape[2]
        prompt_len = x_prompt.shape[0] * groups
        tokens = prompt_len + resp_len
        blocks = tokens // BLOCK
        key_rows = -(-tokens // 128) * 128
        q_width = w_query.shape[2] * HEAD
        ffn = w_gate.shape[2]
        vocab = w_vocab.shape[1]
        w_out = w_out.reshape(w_out.shape[0], q_width, dim)

        def in_order(pieces):
            stack = jnp.stack(pieces)
            return jnp.concatenate([lax.dynamic_index_in_dim(stack, me ^ j, 0, keepdims=False) for j in range(groups)], axis=0)

        def rows_of(w):
            size = w.shape[0] // groups
            return lax.dynamic_slice_in_dim(w, me * size, size, 0)

        def qkv(l, part):
            return jnp.concatenate([part(w_query[l]).reshape(-1, q_width), part(w_key[l]).reshape(-1, HEAD), part(w_value[l]).reshape(-1, HEAD)], axis=1)

        def fetch_rows(piece):
            return spread(swap(piece))

        qkv_far0 = in_order(fetch_rows(qkv(0, rows_of)))
        out_far0 = fetch_rows(rows_of(w_out[0]))
        qkv_far1 = fetch_rows(qkv(1, rows_of))
        out_far1 = fetch_rows(rows_of(w_out[1]))

        base = me * (sum(CHUNKS))
        wide, tall = [], []
        done = 0
        for c, size in enumerate(CHUNKS + (TAIL,)):
            if c < len(CHUNKS):
                at = base + done
            else:
                at = groups * done + jnp.minimum(me, (ffn - groups * done) // TAIL - 1) * TAIL
            w = jnp.concatenate([lax.dynamic_slice(w_gate, (1, 0, at), (1, dim, size))[0], lax.dynamic_slice(w_up, (1, 0, at), (1, dim, size))[0]], axis=1)
            t = lax.dynamic_slice(w_down, (1, at, 0), (1, size, dim))[0]
            if c == len(CHUNKS):
                t = jnp.where(me < (ffn - groups * done) // TAIL, t, jnp.zeros_like(t))
            w, t = swap(w), swap(t)
            wf, tf = lax.ppermute(w, 'resp', chip), lax.ppermute(t, 'resp', chip)
            wide.append([w, lax.ppermute(w, 'resp', core), wf, lax.ppermute(wf, 'resp', core)])
            tall.append([t, lax.ppermute(t, 'resp', core), tf, lax.ppermute(tf, 'resp', core)])
            done += size
        piece = vocab // groups
        vocab_far = spread(swap(lax.dynamic_slice_in_dim(w_vocab, me * piece, piece, 1)))

        prompt = in_order(spread(x_prompt))
        x = jnp.concatenate([prompt, x_resp[0]], axis=0)

        half = HEAD // 2
        frequency = ROPE_BASE ** (-jnp.arange(half, dtype=jnp.float32) / half)
        angles = jnp.arange(tokens).astype(jnp.float32)[:, None] * frequency
        cos_half, sin_half = jnp.cos(angles), jnp.sin(angles)
        cos_all = jnp.concatenate([cos_half, cos_half], axis=1)
        sin_all = jnp.concatenate([-sin_half, sin_half], axis=1)

        every = jnp.arange(blocks, dtype=jnp.int32)
        whole = lambda w: w
        q, k, v = project(every, x, attn_gain[0], qkv(0, whole), cos_all, sin_all, key_rows)
        mixed_own = attention(every, q, k, v, blocks)
        q, k, v = project(every, x, attn_gain[0], qkv_far0, cos_all, sin_all, key_rows)
        mixed_far = attention(every, q, k, v, blocks)
        q, out_far0 = lax.optimization_barrier((q, out_far0))
        out_far0 = in_order(out_far0)
        x, u = project_out(0, x, mixed_own, mixed_far, w_out, out_far0, mlp_gain[0])

        owned = jnp.array(OWNED, jnp.int32)
        mine = owned[side]
        theirs = owned[1 - side]
        per_side = len(OWNED[0])

        def take(a, ids):
            return jnp.concatenate([lax.dynamic_slice_in_dim(a, ids[i] * BLOCK, BLOCK, 0) for i in range(per_side)], axis=0)

        got = []
        for i in range(per_side):
            part = mlp_own(0, theirs[i:i + 1], u, BLOCK, w_gate, w_up, w_down)
            got.append(swap(part))
        zero = jnp.zeros((1,), jnp.int32)
        part_mine = mlp_own(0, zero, take(u, mine), per_side * BLOCK, w_gate, w_up, w_down)
        x = (take(x, mine).astype(jnp.float32) + (part_mine + jnp.concatenate(got, axis=0))).astype(jnp.bfloat16)

        x, qkv_far1 = lax.optimization_barrier((x, qkv_far1))
        qkv_far1 = in_order(qkv_far1)
        q_own, k_own, v_own = project(mine, x, attn_gain[1], qkv(1, whole), cos_all, sin_all, per_side * BLOCK)
        q_far, k_far, v_far = project(mine, x, attn_gain[1], qkv_far1, cos_all, sin_all, per_side * BLOCK)
        kv_mine = jnp.concatenate([k_own, v_own, k_far, v_far], axis=1)
        kv_sent = jnp.concatenate([k_far, v_far, k_own, v_own], axis=1)
        kv_got = swap(kv_sent)
        kv_mine, out_far1 = lax.optimization_barrier((kv_mine, out_far1))
        out_far1 = in_order(out_far1)

        def merge(own_part, far_part):
            def split(a):
                return [a[i * BLOCK:(i + 1) * BLOCK] for i in range(a.shape[0] // BLOCK)]

            a, b = split(own_part), split(far_part)
            order = [[None] * blocks, [None] * blocks]
            for s in range(2):
                for i, blk in enumerate(OWNED[s]):
                    order[s][blk] = a[i]
                for i, blk in enumerate(OWNED[1 - s]):
                    order[s][blk] = b[i]
            return jnp.concatenate([jnp.where(side == 0, p0, p1) for p0, p1 in zip(*order)], axis=0)

        kv = jnp.pad(merge(kv_mine, kv_got), ((0, key_rows - tokens), (0, 0)))
        mixed_own = attention(mine, q_own, kv[:, :HEAD], kv[:, HEAD:2 * HEAD], blocks)
        mixed_far = attention(mine, q_far, kv[:, 2 * HEAD:3 * HEAD], kv[:, 3 * HEAD:], blocks)
        x, u = project_out(1, x, mixed_own, mixed_far, w_out, out_far1, mlp_gain[1])
        total = mlp_own(1, zero, u, per_side * BLOCK, w_gate, w_up, w_down)
        for c in range(len(wide)):
            total = mlp_pieces(u, total, wide[c], tall[c])
        x = (x.astype(jnp.float32) + total).astype(jnp.bfloat16)

        logits = dot(normalize(x, final_gain), jnp.concatenate([w_vocab] + vocab_far, axis=1))
        ids = [side * vocab + jnp.arange(vocab)] + [(1 - side) * vocab + (me ^ j) * piece + jnp.arange(piece) for j in range(groups)]
        vocab_ids = jnp.concatenate(ids)
        padded_targets = jnp.concatenate([jnp.zeros((prompt_len,), targets.dtype), targets[0]])[:, None]
        target_own = take(padded_targets, mine)
        row_max = jnp.max(logits, axis=-1)
        exp_total = jnp.sum(jnp.exp(logits - row_max[:, None]), axis=-1)
        picked = jnp.sum(jnp.where(vocab_ids[None, :] == target_own, logits, 0.0), axis=-1)
        log_probs = picked - row_max - jnp.log(exp_total)
        log_probs = merge(log_probs, swap(log_probs))[prompt_len:]
        log_probs = jnp.where(jnp.arange(resp_len) < resp_lens[0], log_probs, 0.0)
        return log_probs[None, :]

    return jax.shard_map(device_body, mesh=mesh, in_specs=in_specs, out_specs=P(row_axes, None), check_vma=False)
```

time: 1150 us -> 1110 us (0.965)
  matrix products: 398 us -> 9.8 us
  Pallas kernels: 110 us -> 482 us
  local copies, waits for them, and re-layouts: 232 us -> 96.5 us
  waiting for transfers between devices: 312 us -> 406 us
  starting transfers between devices: 41.7 us -> 53.3 us
    dot_general x31 -> x1, matrix products: 398 us -> 9.8 us  [dot(): return jnp.dot(a, b, preferred_element_type=jnp.float32)]
    pallas_call x0 -> x16, Pallas kernels: none -> 374 us  [the longest x5 198 us: mlp_own(): pl.pallas_call(mlp_kernel, grid_spec=pltpu.PrefetchScalarGridSpec(num_sca...]
    slice x51 -> x6, local copies, waits for them, and re-layouts: 130 us -> 10.9 us  [the longest x1 5.01 us: device_body(): out_far1 = fetch_rows(rows_of(w_out[1]))]
    ppermute x32 -> x42, waiting for transfers between devices: 112 us -> 160 us  [the longest x10 111 us: device_body(): wf, tf = (lax.ppermute(w, 'resp', chip), lax.ppermute(t, 'resp', chip))]
    ppermute x20, waiting for transfers between devices: 200 us -> 246 us  [swap(): return lax.ppermute(a, 'model', across)]
    unnamed x226 -> x170, local copies, waits for them, and re-layouts: 59 us -> 27.4 us
    squeeze x0 -> x6, local copies, waits for them, and re-layouts: none -> 14.5 us  [the longest x3 9.46 us: device_body(): lax.dynamic_slice(w_up, (1, 0, at), (1, dim, size))[0]]
    ppermute x32 -> x42, starting transfers between devices: 18.8 us -> 28.8 us  [the longest x10 12.2 us: device_body(): wf, tf = (lax.ppermute(w, 'resp', chip), lax.ppermute(t, 'resp', chip))]
  transfers between devices with their start and end apart: 68 -> 68, of which waited for: 14 -> 17; matrix products, arithmetic and copies ran while one was open for 53% -> 11% of each run, Pallas kernels for 10% -> 42%
where the time goes in v2:
time: 1110 us; the launch traced here: 1100 us
  Pallas kernels  482 us (43%)
  waiting for transfers between devices  406 us (37%)
  local copies, waits for them, and re-layouts  96.5 us (9%)
  starting transfers between devices  53.3 us (5%)
  other arithmetic  45.1 us (4%)
    ppermute x20, waiting for transfers between devices, swap(): return lax.ppermute(a, 'model', across)  246 us
    pallas_call x5, Pallas kernels, mlp_own(): pl.pallas_call(mlp_kernel, grid_spec=pltpu.PrefetchScalarGridSpec(num_sca...  198 us
    pallas_call x5, Pallas kernels, mlp_pieces(): pl.pallas_call(functools.partial(mlp_pieces_kernel, n), in_specs=[vmem, v...  116 us
    ppermute x10, waiting for transfers between devices, device_body(): wf, tf = (lax.ppermute(w, 'resp', chip), lax.ppermute(t, 'resp', chip))  111 us
    pallas_call x4, Pallas kernels, attention(): pl.pallas_call(functools.partial(attention_kernel, num_blocks, per_step),...  108 us
    pallas_call x4, Pallas kernels, project(): pl.pallas_call(functools.partial(project_kernel, q_width), grid_spec=pltp...  35.8 us
    ppermute x6, waiting for transfers between devices, spread(): lax.ppermute(a, 'resp', both)  29.5 us
    unnamed x170, local copies, waits for them, and re-layouts  27.4 us
  transfers between devices with their start and end apart: 68, of which 17 were waited for; matrix products, arithmetic and copies ran while one was open for 11% of the time, Pallas kernels for 42%

profile of v2, /device:TPU:0, one launch (start us, length us, event | category | flops | bytes accessed | tf_op | source)
XLA Modules:
  0.0 1097.2 jit_solution(11384693408883655231)
XLA Ops:
  91.2 12.4 %shard_map.154 = (bf16[2112,768]{1,0:T(8,128)(2,1)S(1)}, bf16[2176,128]{1,0:T(8,128)(2,1)S(1)}, bf16[2176,128]{1,0:T(8,128)(2,1)S(1)}) custom-call(s32[6]{0:T(128)S(1)} %iota.56.ids_ref, bf16[2112,1536]{1,0:T(8,128)(2,1)} %copy-done.66, f32[1,1536]{1,0:T(1,128)S(1)} %get-tuple-element.131.gain_ref, bf16[1536,1024]{1,0:T(8,128)(2,1)S(1)} %get-tuple-element.149.w_ref, ...), custom_call_target="tpu_custom_call" | custom-call | flops 6643777536 | bytes 13959168 | tf_op jit(solution)/shard_map/pallas_call | solution.py:61
  105.6 35.4 %shard_map.155.a_ref = bf16[2112,768]{1,0:T(8,128)(2,1)S(1)} custom-call(s32[6]{0:T(128)S(1)} %iota.55.ids_ref, bf16[2112,768]{1,0:T(8,128)(2,1)S(1)} %get-tuple-element.35.q_ref, bf16[2176,128]{1,0:T(8,128)(2,1)S(1)} %get-tuple-element.36.k_ref, bf16[2176,128]{1,0:T(8,128)(2,1)S(1)} %get-tuple-element.37.v_ref), custom_call_target="tpu_custom_call" | custom-call | flops 28236054528 | bytes 7602176 | tf_op jit(solution)/shard_map/pallas_call | solution.py:127
  153.5 12.3 %shard_map.156 = (bf16[2112,768]{1,0:T(8,128)(2,1)S(1)}, bf16[2176,128]{1,0:T(8,128)(2,1)S(1)}, bf16[2176,128]{1,0:T(8,128)(2,1)S(1)}) custom-call(s32[6]{0:T(128)S(1)} %iota.60.ids_ref, bf16[2112,1536]{1,0:T(8,128)(2,1)} %copy-done.66, f32[1,1536]{1,0:T(1,128)S(1)} %get-tuple-element.131.gain_ref, bf16[1536,1024]{1,0:T(8,128)(2,1)S(1)} %pad_maximum_fusion.3.w_ref, ...), custom_call_target="tpu_custom_call" | custom-call | flops 6643777536 | bytes 13959168 | tf_op jit(solution)/shard_map/pallas_call | solution.py:61
  172.2 35.0 %shard_map.157.b_ref = bf16[2112,768]{1,0:T(8,128)(2,1)S(1)} custom-call(s32[6]{0:T(128)S(1)} %iota.59.ids_ref, bf16[2112,768]{1,0:T(8,128)(2,1)S(1)} %get-tuple-element.38.q_ref, bf16[2176,128]{1,0:T(8,128)(2,1)S(1)} %get-tuple-element.39.k_ref, bf16[2176,128]{1,0:T(8,128)(2,1)S(1)} %get-tuple-element.40.v_ref), custom_call_target="tpu_custom_call" | custom-call | flops 28236054528 | bytes 7602176 | tf_op jit(solution)/shard_map/pallas_call | solution.py:127
  209.1 15.6 %shard_map.158 = (bf16[2112,1536]{1,0:T(8,128)(2,1)}, bf16[2112,1536]{1,0:T(8,128)(2,1)}) custom-call(bf16[2112,1536]{1,0:T(8,128)(2,1)} %copy-done.66, bf16[2112,768]{1,0:T(8,128)(2,1)S(1)} %copy-done.10, bf16[2112,768]{1,0:T(8,128)(2,1)S(1)} %shard_map.157.b_ref, bf16[2,768,1536]{2,1,0:T(8,128)(2,1)S(1)} %bitcast.123, ...), custom_call_target="tpu_custom_call" | custom-call | flops 9965666304 | bytes 28901376 | tf_op jit(solution)/shard_map/pallas_call | solution.py:157
  226.8 24.7 %shard_map.160 = f32[352,1536]{1,0:T(8,128)} custom-call(s32[1]{0:T(128)} %bitcast.38.ids_ref, bf16[2112,1536]{1,0:T(8,128)(2,1)} %get-tuple-element.46.u_ref, bf16[2,1536,4480]{2,1,0:T(8,128)(2,1)} %gate_ref.9, bf16[2,1536,4480]{2,1,0:T(8,128)(2,1)} %up_ref.9, bf16[2,4480,1536]{2,1,0:T(8,128)(2,1)} %down_ref.9), custom_call_target="tpu_custom_call" | custom-call | flops 14533263360 | bytes 44531712 | tf_op jit(solution)/shard_map/pallas_call | solution.py:208
  251.8 24.4 %shard_map.161 = f32[352,1536]{1,0:T(8,128)} custom-call(s32[1]{0:T(128)} %bitcast.39.ids_ref, bf16[2112,1536]{1,0:T(8,128)(2,1)} %get-tuple-element.46.u_ref, bf16[2,1536,4480]{2,1,0:T(8,128)(2,1)} %gate_ref.9, bf16[2,1536,4480]{2,1,0:T(8,128)(2,1)} %up_ref.9, bf16[2,4480,1536]{2,1,0:T(8,128)(2,1)} %down_ref.9), custom_call_target="tpu_custom_call" | custom-call | flops 14533263360 | bytes 44531712 | tf_op jit(solution)/shard_map/pallas_call | solution.py:208
  278.0 24.4 %shard_map.162 = f32[352,1536]{1,0:T(8,128)} custom-call(s32[1]{0:T(128)} %bitcast.40.ids_ref, bf16[2112,1536]{1,0:T(8,128)(2,1)} %get-tuple-element.46.u_ref, bf16[2,1536,4480]{2,1,0:T(8,128)(2,1)} %gate_ref.9, bf16[2,1536,4480]{2,1,0:T(8,128)(2,1)} %up_ref.9, bf16[2,4480,1536]{2,1,0:T(8,128)(2,1)} %down_ref.9), custom_call_target="tpu_custom_call" | custom-call | flops 14533263360 | bytes 44531712 | tf_op jit(solution)/shard_map/pallas_call | solution.py:208
  304.5 62.1 %shard_map.159 = f32[1056,1536]{1,0:T(8,128)} custom-call(s32[1]{0:T(128)} %constant.115.clone.1.ids_ref, bf16[1056,1536]{1,0:T(8,128)(2,1)} %pad_maximum_fusion.u_ref, bf16[2,1536,4480]{2,1,0:T(8,128)(2,1)} %gate_ref.9, bf16[2,1536,4480]{2,1,0:T(8,128)(2,1)} %up_ref.9, bf16[2,4480,1536]{2,1,0:T(8,128)(2,1)} %down_ref.9), custom_call_target="tpu_custom_call" | custom-call | flops 43599790080 | bytes 51019776 | tf_op jit(solution)/shard_map/pallas_call | solution.py:208
  375.2 46.9 %collective-permute-done.18 = bf16[192,1536]{1,0:T(8,128)(2,1)} collective-permute-done((bf16[192,1536]{1,0:T(8,128)(2,1)S(1)}, bf16[192,1536]{1,0:T(8,128)(2,1)}, u32[]{:S(2)}, u32[]{:S(2)}) %collective-permute-start.18) | collective-permute-done | bytes 589856 | tf_op jit(solution)/shard_map/ppermute | solution.py:276
  429.6 13.8 %collective-permute-done.16 = bf16[384,1024]{0,1:T(8,128)(2,1)S(1)} collective-permute-done((bf16[384,1024]{0,1:T(8,128)(2,1)S(1)}, bf16[384,1024]{0,1:T(8,128)(2,1)S(1)}, u32[]{:S(2)}, u32[]{:S(2)}) %collective-permute-start.16) | collective-permute-done | bytes 786464 | tf_op jit(solution)/shard_map/ppermute | solution.py:279
  443.4 16.0 %collective-permute-done.17 = bf16[384,1024]{0,1:T(8,128)(2,1)S(1)} collective-permute-done((bf16[384,1024]{0,1:T(8,128)(2,1)S(1)}, bf16[384,1024]{0,1:T(8,128)(2,1)S(1)}, u32[]{:S(2)}, u32[]{:S(2)}) %collective-permute-start.17) | collective-permute-done | bytes 786464 | tf_op jit(solution)/shard_map/ppermute | solution.py:279
  487.1 13.6 %collective-permute-done.66 = bf16[1536,256]{1,0:T(8,128)(2,1)} collective-permute-done((bf16[1536,256]{1,0:T(8,128)(2,1)}, bf16[1536,256]{1,0:T(8,128)(2,1)}, u32[]{:S(2)}, u32[]{:S(2)}) %collective-permute-start.66) | collective-permute-done | bytes 786464 | tf_op jit(solution)/shard_map/ppermute | solution.py:279
  510.6 92.5 %collective-permute-done.59.refs_4_ = bf16[128,1536]{1,0:T(8,128)(2,1)S(1)} collective-permute-done((bf16[128,1536]{1,0:T(8,128)(2,1)S(1)}, bf16[128,1536]{1,0:T(8,128)(2,1)S(1)}, u32[]{:S(2)}, u32[]{:S(2)}) %collective-permute-start.59) | collective-permute-done | bytes 393248 | tf_op jit(solution)/shard_map/ppermute | solution.py:276
  607.1 13.0 %collective-permute-done.43.refs_4_ = bf16[256,1536]{1,0:T(8,128)(2,1)S(1)} collective-permute-done((bf16[256,1536]{1,0:T(8,128)(2,1)S(1)}, bf16[256,1536]{1,0:T(8,128)(2,1)S(1)}, u32[]{:S(2)}, u32[]{:S(2)}) %collective-permute-start.43) | collective-permute-done | bytes 786464 | tf_op jit(solution)/shard_map/ppermute | solution.py:276
  621.8 15.1 %collective-permute-done.47.refs_0_ = bf16[1536,256]{1,0:T(8,128)(2,1)S(1)} collective-permute-done((bf16[1536,256]{1,0:T(8,128)(2,1)S(1)}, bf16[1536,256]{1,0:T(8,128)(2,1)S(1)}, u32[]{:S(2)}, u32[]{:S(2)}) %collective-permute-start.47) | collective-permute-done | bytes 786464 | tf_op jit(solution)/shard_map/ppermute | solution.py:276
  642.1 11.6 %collective-permute-done.55.refs_0_ = bf16[1536,256]{1,0:T(8,128)(2,1)S(1)} collective-permute-done((bf16[1536,256]{1,0:T(8,128)(2,1)S(1)}, bf16[1536,256]{1,0:T(8,128)(2,1)S(1)}, u32[]{:S(2)}, u32[]{:S(2)}) %collective-permute-start.55) | collective-permute-done | bytes 786464 | tf_op jit(solution)/shard_map/ppermute | solution.py:276
  657.5 55.2 %collective-permute-done.27.refs_4_ = bf16[384,1536]{1,0:T(8,128)(2,1)S(1)} collective-permute-done((bf16[384,1536]{1,0:T(8,128)(2,1)S(1)}, bf16[384,1536]{1,0:T(8,128)(2,1)S(1)}, u32[]{:S(2)}, u32[]{:S(2)}) %collective-permute-start.27) | collective-permute-done | bytes 1179680 | tf_op jit(solution)/shard_map/ppermute | solution.py:276
  715.0 18.8 %shard_map.166.b_ref = bf16[1056,768]{1,0:T(8,128)(2,1)S(1)} custom-call(s32[3]{0:T(128)S(1)} %get-tuple-element.135.ids_ref, bf16[1056,768]{1,0:T(8,128)(2,1)S(1)} %get-tuple-element.58.q_ref, bf16[2176,128]{1,0:T(8,128)(2,1)S(1)} %get-tuple-element.107.k_ref, bf16[2176,128]{1,0:T(8,128)(2,1)S(1)} %get-tuple-element.105.v_ref), custom_call_target="tpu_custom_call" | custom-call | flops 14118027264 | bytes 4358144 | tf_op jit(solution)/shard_map/pallas_call | solution.py:127
  735.5 10.7 collective-permute-done.39.refs_0_
  748.3 18.9 %shard_map.165.a_ref = bf16[1056,768]{1,0:T(8,128)(2,1)S(1)} custom-call(s32[3]{0:T(128)S(1)} %get-tuple-element.135.ids_ref, bf16[1056,768]{1,0:T(8,128)(2,1)S(1)} %get-tuple-element.48.q_ref, bf16[2176,128]{1,0:T(8,128)(2,1)S(1)} %get-tuple-element.108.k_ref, bf16[2176,128]{1,0:T(8,128)(2,1)S(1)} %get-tuple-element.106.v_ref), custom_call_target="tpu_custom_call" | custom-call | flops 14118027264 | bytes 4358144 | tf_op jit(solution)/shard_map/pallas_call | solution.py:127
  777.5 31.6 %collective-permute-done.29.refs_6_ = bf16[384,1536]{1,0:T(8,128)(2,1)} collective-permute-done((bf16[384,1536]{1,0:T(8,128)(2,1)S(1)}, bf16[384,1536]{1,0:T(8,128)(2,1)}, u32[]{:S(2)}, u32[]{:S(2)}) %collective-permute-start.29) | collective-permute-done | bytes 1179680 | tf_op jit(solution)/shard_map/ppermute | solution.py:327
  809.7 33.2 %collective-permute-done.33.refs_2_ = bf16[1536,512]{1,0:T(8,128)(2,1)} collective-permute-done((bf16[1536,512]{1,0:T(8,128)(2,1)}, bf16[1536,512]{1,0:T(8,128)(2,1)}, u32[]{:S(2)}, u32[]{:S(2)}) %collective-permute-start.33) | collective-permute-done | bytes 1572896 | tf_op jit(solution)/shard_map/ppermute | solution.py:327
  842.8 33.1 %collective-permute-done.41.refs_2_ = bf16[1536,512]{1,0:T(8,128)(2,1)S(1)} collective-permute-done((bf16[1536,512]{1,0:T(8,128)(2,1)S(1)}, bf16[1536,512]{1,0:T(8,128)(2,1)S(1)}, u32[]{:S(2)}, u32[]{:S(2)}) %collective-permute-start.41) | collective-permute-done | bytes 1572896 | tf_op jit(solution)/shard_map/ppermute | solution.py:327
  877.1 62.4 %shard_map.168.acc_ref = f32[1056,1536]{1,0:T(8,128)} custom-call(s32[1]{0:T(128)} %constant.115.clone.1.ids_ref, bf16[1056,1536]{1,0:T(8,128)(2,1)} %copy-done, bf16[2,1536,4480]{2,1,0:T(8,128)(2,1)} %gate_ref.9, bf16[2,1536,4480]{2,1,0:T(8,128)(2,1)} %up_ref.9, bf16[2,4480,1536]{2,1,0:T(8,128)(2,1)} %down_ref.9), custom_call_target="tpu_custom_call" | custom-call | flops 43599790080 | bytes 51019776 | tf_op jit(solution)/shard_map/pallas_call | solution.py:208
  940.6 31.7 %shard_map.169.acc_ref = f32[1056,1536]{1,0:T(8,128)} custom-call(bf16[1056,1536]{1,0:T(8,128)(2,1)} %copy-done, f32[1056,1536]{1,0:T(8,128)} %shard_map.168.acc_ref, bf16[1536,768]{1,0:T(8,128)(2,1)} %copy-done.67, bf16[1536,768]{1,0:T(8,128)(2,1)} %collective-permute-done.24.refs_1_, bf16[1536,768]{1,0:T(8,128)(2,1)} %collective-permute-done.25.refs_2_, ...), custom_call_target="tpu_custom_call" | custom-call | flops 14948499456 | bytes 30375936 | tf_op jit(solution)/shard_map/pallas_call | solution.py:250
  974.3 21.2 %shard_map.170.acc_ref = f32[1056,1536]{1,0:T(8,128)} custom-call(bf16[1056,1536]{1,0:T(8,128)(2,1)} %copy-done, f32[1056,1536]{1,0:T(8,128)} %shard_map.169.acc_ref, bf16[1536,512]{1,0:T(8,128)(2,1)} %collective-permute-done.31.refs_0_, bf16[1536,512]{1,0:T(8,128)(2,1)} %collective-permute-done.32.refs_1_, ...), custom_call_target="tpu_custom_call" | custom-call | flops 9965666304 | bytes 25657344 | tf_op jit(solution)/shard_map/pallas_call | solution.py:250
  996.1 12.5 %collective-permute-done.57.refs_2_ = bf16[1536,256]{1,0:T(8,128)(2,1)S(1)} collective-permute-done((bf16[1536,256]{1,0:T(8,128)(2,1)S(1)}, bf16[1536,256]{1,0:T(8,128)(2,1)S(1)}, u32[]{:S(2)}, u32[]{:S(2)}) %collective-permute-start.57) | collective-permute-done | bytes 786464 | tf_op jit(solution)/shard_map/ppermute | solution.py:327
  1009.7 21.3 %shard_map.171.acc_ref = f32[1056,1536]{1,0:T(8,128)} custom-call(bf16[1056,1536]{1,0:T(8,128)(2,1)} %copy-done, f32[1056,1536]{1,0:T(8,128)} %shard_map.170.acc_ref, bf16[1536,512]{1,0:T(8,128)(2,1)} %copy-done.68, bf16[1536,512]{1,0:T(8,128)(2,1)} %collective-permute-done.40.refs_1_, bf16[1536,512]{1,0:T(8,128)(2,1)} %copy-done.69, ...), custom_call_target="tpu_custom_call" | custom-call | flops 9965666304 | bytes 25657344 | tf_op jit(solution)/shard_map/pallas_call | solution.py:250
  1032.0 20.8 %shard_map.172.acc_ref = f32[1056,1536]{1,0:T(8,128)} custom-call(bf16[1056,1536]{1,0:T(8,128)(2,1)} %copy-done, f32[1056,1536]{1,0:T(8,128)} %shard_map.171.acc_ref, bf16[1536,256]{1,0:T(8,128)(2,1)} %copy-done.39, bf16[1536,256]{1,0:T(8,128)(2,1)} %copy-done.43, bf16[1536,256]{1,0:T(8,128)(2,1)} %copy-done.41, ...), custom_call_target="tpu_custom_call" | custom-call | flops 4982833152 | bytes 20938752 | tf_op jit(solution)/shard_map/pallas_call | solution.py:250
  1053.8 20.8 %shard_map.173 = f32[1056,1536]{1,0:T(8,128)} custom-call(bf16[1056,1536]{1,0:T(8,128)(2,1)} %copy-done, f32[1056,1536]{1,0:T(8,128)} %shard_map.172.acc_ref, bf16[1536,256]{1,0:T(8,128)(2,1)} %copy-done.38, bf16[1536,256]{1,0:T(8,128)(2,1)} %copy-done.42, bf16[1536,256]{1,0:T(8,128)(2,1)} %copy-done.40, bf16[1536,256]{1,0:T(8,128)(2,1)} %collective-permute-done.58.refs_3_, ...), custom_call_target="tpu_custom_call" | custom-call | flops 4982833152 | bytes 20938752 | tf_op jit(solution)/shard_map/pallas_call | solution.py:250
  1079.3 9.8 fusion.17
  (391 shorter events, 222.3 us)
Async XLA Ops:
  0.0 82.4 %collective-permute-start = (bf16[16,1536]{1,0:T(8,128)(2,1)}, bf16[16,1536]{1,0:T(8,128)(2,1)S(1)}, u32[]{:S(2)}, u32[]{:S(2)}) collective-permute-start(bf16[16,1536]{1,0:T(8,128)(2,1)} %param.16), channel_id=1, source_target_pairs={{0,1},{1,0},{2,3},{3,2},{4,5},{5,4},{6,7},{7,6}} | collective-permute-start | bytes 147464 | tf_op jit(solution)/shard_map/ppermute | solution.py:279
  0.8 83.3 %collective-permute-start.1 = (bf16[16,1536]{1,0:T(8,128)(2,1)}, bf16[16,1536]{1,0:T(8,128)(2,1)}, u32[]{:S(2)}, u32[]{:S(2)}) collective-permute-start(bf16[16,1536]{1,0:T(8,128)(2,1)} %param.16), channel_id=1, source_target_pairs={{0,2},{1,3},{2,0},{3,1},{4,6},{5,7},{6,4},{7,5}} | collective-permute-start | bytes 147464 | tf_op jit(solution)/shard_map/ppermute | solution.py:279
  3.3 80.8 %collective-permute-start.2 = (bf16[16,1536]{1,0:T(8,128)(2,1)}, bf16[16,1536]{1,0:T(8,128)(2,1)}, u32[]{:S(2)}, u32[]{:S(2)}) collective-permute-start(bf16[16,1536]{1,0:T(8,128)(2,1)} %param.16), channel_id=1, source_target_pairs={{0,3},{1,2},{2,1},{3,0},{4,7},{5,6},{6,5},{7,4}} | collective-permute-start | bytes 147464 | tf_op jit(solution)/shard_map/ppermute | solution.py:279
  22.1 81.6 %collective-permute-start.3 = (bf16[384,1024]{0,1:T(8,128)(2,1)}, bf16[384,1024]{0,1:T(8,128)(2,1)}, u32[]{:S(2)}, u32[]{:S(2)}) collective-permute-start(bf16[384,1024]{0,1:T(8,128)(2,1)} %pad_maximum_fusion.18), channel_id=1, source_target_pairs={{0,4},{4,0},{1,5},{5,1},{2,6},{6,2},{3,7},{7,3}} | collective-permute-start | bytes 2359304 | tf_op jit(solution)/shard_map/ppermute | solution.py:276
  30.8 110.2 %collective-permute-start.7 = (bf16[192,1536]{1,0:T(8,128)(2,1)}, bf16[192,1536]{1,0:T(8,128)(2,1)}, u32[]{:S(2)}, u32[]{:S(2)}) collective-permute-start(bf16[192,1536]{1,0:T(8,128)(2,1)} %constant_dynamic-slice_fusion.14), channel_id=1, source_target_pairs={{0,4},{4,0},{1,5},{5,1},{2,6},{6,2},{3,7},{7,3}} | collective-permute-start | bytes 1769480 | tf_op jit(solution)/shard_map/ppermute | solution.py:276
  145.7 220.9 %collective-permute-start.64 = (bf16[1536,256]{1,0:T(8,128)(2,1)}, bf16[1536,256]{1,0:T(8,128)(2,1)}, u32[]{:S(2)}, u32[]{:S(2)}) collective-permute-start(bf16[1536,256]{1,0:T(8,128)(2,1)} %collective-permute-done.63), channel_id=1, source_target_pairs={{0,1},{1,0},{2,3},{3,2},{4,5},{5,4},{6,7},{7,6}} | collective-permute-start | bytes 2359304 | tf_op jit(solution)/shard_map/ppermute | solution.py:279
  145.7 222.7 %collective-permute-start.65 = (bf16[1536,256]{1,0:T(8,128)(2,1)}, bf16[1536,256]{1,0:T(8,128)(2,1)}, u32[]{:S(2)}, u32[]{:S(2)}) collective-permute-start(bf16[1536,256]{1,0:T(8,128)(2,1)} %collective-permute-done.63), channel_id=1, source_target_pairs={{0,2},{1,3},{2,0},{3,1},{4,6},{5,7},{6,4},{7,5}} | collective-permute-start | bytes 2359304 | tf_op jit(solution)/shard_map/ppermute | solution.py:279
  251.6 170.9 %collective-permute-start.11 = (f32[352,1536]{1,0:T(8,128)}, f32[352,1536]{1,0:T(8,128)S(1)}, u32[]{:S(2)}, u32[]{:S(2)}) collective-permute-start(f32[352,1536]{1,0:T(8,128)} %shard_map.160), channel_id=1, source_target_pairs={{0,4},{4,0},{1,5},{5,1},{2,6},{6,2},{3,7},{7,3}} | collective-permute-start | bytes 6488072 | tf_op jit(solution)/shard_map/ppermute | solution.py:276
  276.2 146.8 %collective-permute-start.12 = (f32[352,1536]{1,0:T(8,128)}, f32[352,1536]{1,0:T(8,128)}, u32[]{:S(2)}, u32[]{:S(2)}) collective-permute-start(f32[352,1536]{1,0:T(8,128)} %shard_map.161), channel_id=1, source_target_pairs={{0,4},{4,0},{1,5},{5,1},{2,6},{6,2},{3,7},{7,3}} | collective-permute-start | bytes 6488072 | tf_op jit(solution)/shard_map/ppermute | solution.py:276
  302.4 122.2 %collective-permute-start.13 = (f32[352,1536]{1,0:T(8,128)}, f32[352,1536]{1,0:T(8,128)}, u32[]{:S(2)}, u32[]{:S(2)}) collective-permute-start(f32[352,1536]{1,0:T(8,128)} %shard_map.162), channel_id=1, source_target_pairs={{0,4},{4,0},{1,5},{5,1},{2,6},{6,2},{3,7},{7,3}} | collective-permute-start | bytes 6488072 | tf_op jit(solution)/shard_map/ppermute | solution.py:276
  422.1 86.6 %collective-permute-start.51 = (bf16[128,1536]{1,0:T(8,128)(2,1)}, bf16[128,1536]{1,0:T(8,128)(2,1)}, u32[]{:S(2)}, u32[]{:S(2)}) collective-permute-start(bf16[128,1536]{1,0:T(8,128)(2,1)} %get-tuple-element.68), channel_id=1, source_target_pairs={{0,4},{4,0},{1,5},{5,1},{2,6},{6,2},{3,7},{7,3}} | collective-permute-start | bytes 1179656 | tf_op jit(solution)/shard_map/ppermute | solution.py:276
  422.4 82.0 %collective-permute-start.19 = (bf16[192,1536]{1,0:T(8,128)(2,1)}, bf16[192,1536]{1,0:T(8,128)(2,1)}, u32[]{:S(2)}, u32[]{:S(2)}) collective-permute-start(bf16[192,1536]{1,0:T(8,128)(2,1)} %collective-permute-done.18), channel_id=1, source_target_pairs={{0,1},{1,0},{2,3},{3,2},{4,5},{5,4},{6,7},{7,6}} | collective-permute-start | bytes 1769480 | tf_op jit(solution)/shard_map/ppermute | solution.py:279
  428.2 76.6 %collective-permute-start.20 = (bf16[192,1536]{1,0:T(8,128)(2,1)}, bf16[192,1536]{1,0:T(8,128)(2,1)}, u32[]{:S(2)}, u32[]{:S(2)}) collective-permute-start(bf16[192,1536]{1,0:T(8,128)(2,1)} %collective-permute-done.18), channel_id=1, source_target_pairs={{0,2},{1,3},{2,0},{3,1},{4,6},{5,7},{6,4},{7,5}} | collective-permute-start | bytes 1769480 | tf_op jit(solution)/shard_map/ppermute | solution.py:279
  443.3 63.1 %collective-permute-start.21 = (bf16[192,1536]{1,0:T(8,128)(2,1)}, bf16[192,1536]{1,0:T(8,128)(2,1)}, u32[]{:S(2)}, u32[]{:S(2)}) collective-permute-start(bf16[192,1536]{1,0:T(8,128)(2,1)} %collective-permute-done.18), channel_id=1, source_target_pairs={{0,3},{1,2},{2,1},{3,0},{4,7},{5,6},{6,5},{7,4}} | collective-permute-start | bytes 1769480 | tf_op jit(solution)/shard_map/ppermute | solution.py:279
  500.6 104.8 %collective-permute-start.22 = (bf16[1056,512]{1,0:T(8,128)(2,1)S(1)}, bf16[1056,512]{1,0:T(8,128)(2,1)S(1)}, u32[]{:S(2)}, u32[]{:S(2)}) collective-permute-start(bf16[1056,512]{1,0:T(8,128)(2,1)S(1)} %get-tuple-element.110), channel_id=1, source_target_pairs={{0,4},{4,0},{1,5},{5,1},{2,6},{6,2},{3,7},{7,3}} | collective-permute-start | bytes 3244040 | tf_op jit(solution)/shard_map/ppermute | solution.py:276
  504.5 210.1 %collective-permute-start.23 = (bf16[1536,768]{1,0:T(8,128)(2,1)S(1)}, bf16[1536,768]{1,0:T(8,128)(2,1)S(1)}, u32[]{:S(2)}, u32[]{:S(2)}) collective-permute-start(bf16[1536,768]{1,0:T(8,128)(2,1)S(1)} %copy-done.25), channel_id=1, source_target_pairs={{0,4},{4,0},{1,5},{5,1},{2,6},{6,2},{3,7},{7,3}} | collective-permute-start | bytes 7077896 | tf_op jit(solution)/shard_map/ppermute | solution.py:276
  504.8 100.3 %collective-permute-start.35 = (bf16[256,1536]{1,0:T(8,128)(2,1)S(1)}, bf16[256,1536]{1,0:T(8,128)(2,1)S(1)}, u32[]{:S(2)}, u32[]{:S(2)}) collective-permute-start(bf16[256,1536]{1,0:T(8,128)(2,1)S(1)} %copy-done.49), channel_id=1, source_target_pairs={{0,4},{4,0},{1,5},{5,1},{2,6},{6,2},{3,7},{7,3}} | collective-permute-start | bytes 2359304 | tf_op jit(solution)/shard_map/ppermute | solution.py:276
  506.5 96.7 %collective-permute-start.59 = (bf16[128,1536]{1,0:T(8,128)(2,1)S(1)}, bf16[128,1536]{1,0:T(8,128)(2,1)S(1)}, u32[]{:S(2)}, u32[]{:S(2)}) collective-permute-start(bf16[128,1536]{1,0:T(8,128)(2,1)S(1)} %copy-done.53), channel_id=1, source_target_pairs={{0,4},{4,0},{1,5},{5,1},{2,6},{6,2},{3,7},{7,3}} | collective-permute-start | bytes 1179656 | tf_op jit(solution)/shard_map/ppermute | solution.py:276
  508.7 111.3 %collective-permute-start.43 = (bf16[256,1536]{1,0:T(8,128)(2,1)S(1)}, bf16[256,1536]{1,0:T(8,128)(2,1)S(1)}, u32[]{:S(2)}, u32[]{:S(2)}) collective-permute-start(bf16[256,1536]{1,0:T(8,128)(2,1)S(1)} %copy-done.48), channel_id=1, source_target_pairs={{0,4},{4,0},{1,5},{5,1},{2,6},{6,2},{3,7},{7,3}} | collective-permute-start | bytes 2359304 | tf_op jit(solution)/shard_map/ppermute | solution.py:276
  620.1 92.7 %collective-permute-start.31 = (bf16[1536,512]{1,0:T(8,128)(2,1)S(1)}, bf16[1536,512]{1,0:T(8,128)(2,1)}, u32[]{:S(2)}, u32[]{:S(2)}) collective-permute-start(bf16[1536,512]{1,0:T(8,128)(2,1)S(1)} %copy-done.32), channel_id=1, source_target_pairs={{0,4},{4,0},{1,5},{5,1},{2,6},{6,2},{3,7},{7,3}} | collective-permute-start | bytes 4718600 | tf_op jit(solution)/shard_map/ppermute | solution.py:276
  636.9 75.8 %collective-permute-start.27 = (bf16[384,1536]{1,0:T(8,128)(2,1)S(1)}, bf16[384,1536]{1,0:T(8,128)(2,1)S(1)}, u32[]{:S(2)}, u32[]{:S(2)}) collective-permute-start(bf16[384,1536]{1,0:T(8,128)(2,1)S(1)} %copy-done.37), channel_id=1, source_target_pairs={{0,4},{4,0},{1,5},{5,1},{2,6},{6,2},{3,7},{7,3}} | collective-permute-start | bytes 3538952 | tf_op jit(solution)/shard_map/ppermute | solution.py:276
  655.5 90.7 %collective-permute-start.39 = (bf16[1536,512]{1,0:T(8,128)(2,1)S(1)}, bf16[1536,512]{1,0:T(8,128)(2,1)S(1)}, u32[]{:S(2)}, u32[]{:S(2)}) collective-permute-start(bf16[1536,512]{1,0:T(8,128)(2,1)S(1)} %copy-done.31), channel_id=1, source_target_pairs={{0,4},{4,0},{1,5},{5,1},{2,6},{6,2},{3,7},{7,3}} | collective-permute-start | bytes 4718600 | tf_op jit(solution)/shard_map/ppermute | solution.py:276
  714.6 161.4 %collective-permute-start.25 = (bf16[1536,768]{1,0:T(8,128)(2,1)S(1)}, bf16[1536,768]{1,0:T(8,128)(2,1)}, u32[]{:S(2)}, u32[]{:S(2)}) collective-permute-start(bf16[1536,768]{1,0:T(8,128)(2,1)S(1)} %collective-permute-done.23.refs_0_), channel_id=1, source_target_pairs={{0,2},{1,3},{2,0},{3,1},{4,6},{5,7},{6,4},{7,5}} | collective-permute-start | bytes 7077896 | tf_op jit(solution)/shard_map/ppermute | solution.py:327
  733.9 75.2 %collective-permute-start.29 = (bf16[384,1536]{1,0:T(8,128)(2,1)S(1)}, bf16[384,1536]{1,0:T(8,128)(2,1)}, u32[]{:S(2)}, u32[]{:S(2)}) collective-permute-start(bf16[384,1536]{1,0:T(8,128)(2,1)S(1)} %collective-permute-done.27.refs_4_), channel_id=1, source_target_pairs={{0,2},{1,3},{2,0},{3,1},{4,6},{5,7},{6,4},{7,5}} | collective-permute-start | bytes 3538952 | tf_op jit(solution)/shard_map/ppermute | solution.py:327
  746.2 96.6 %collective-permute-start.33 = (bf16[1536,512]{1,0:T(8,128)(2,1)}, bf16[1536,512]{1,0:T(8,128)(2,1)}, u32[]{:S(2)}, u32[]{:S(2)}) collective-permute-start(bf16[1536,512]{1,0:T(8,128)(2,1)} %collective-permute-done.31.refs_0_), channel_id=1, source_target_pairs={{0,2},{1,3},{2,0},{3,1},{4,6},{5,7},{6,4},{7,5}} | collective-permute-start | bytes 4718600 | tf_op jit(solution)/shard_map/ppermute | solution.py:327
  747.8 128.1 %collective-permute-start.41 = (bf16[1536,512]{1,0:T(8,128)(2,1)S(1)}, bf16[1536,512]{1,0:T(8,128)(2,1)S(1)}, u32[]{:S(2)}, u32[]{:S(2)}) collective-permute-start(bf16[1536,512]{1,0:T(8,128)(2,1)S(1)} %collective-permute-done.39.refs_0_), channel_id=1, source_target_pairs={{0,2},{1,3},{2,0},{3,1},{4,6},{5,7},{6,4},{7,5}} | collective-permute-start | bytes 4718600 | tf_op jit(solution)/shard_map/ppermute | solution.py:327
  809.1 164.7 %collective-permute-start.32 = (bf16[1536,512]{1,0:T(8,128)(2,1)}, bf16[1536,512]{1,0:T(8,128)(2,1)}, u32[]{:S(2)}, u32[]{:S(2)}) collective-permute-start(bf16[1536,512]{1,0:T(8,128)(2,1)} %collective-permute-done.31.refs_0_), channel_id=1, source_target_pairs={{0,1},{1,0},{2,3},{3,2},{4,5},{5,4},{6,7},{7,6}} | collective-permute-start | bytes 4718600 | tf_op jit(solution)/shard_map/ppermute | solution.py:328
  809.1 130.9 %collective-permute-start.24 = (bf16[1536,768]{1,0:T(8,128)(2,1)S(1)}, bf16[1536,768]{1,0:T(8,128)(2,1)}, u32[]{:S(2)}, u32[]{:S(2)}) collective-permute-start(bf16[1536,768]{1,0:T(8,128)(2,1)S(1)} %collective-permute-done.23.refs_0_), channel_id=1, source_target_pairs={{0,1},{1,0},{2,3},{3,2},{4,5},{5,4},{6,7},{7,6}} | collective-permute-start | bytes 7077896 | tf_op jit(solution)/shard_map/ppermute | solution.py:328
  842.8 96.7 %collective-permute-start.30 = (bf16[384,1536]{1,0:T(8,128)(2,1)}, bf16[384,1536]{1,0:T(8,128)(2,1)}, u32[]{:S(2)}, u32[]{:S(2)}) collective-permute-start(bf16[384,1536]{1,0:T(8,128)(2,1)} %collective-permute-done.29.refs_6_), channel_id=1, source_target_pairs={{0,1},{1,0},{2,3},{3,2},{4,5},{5,4},{6,7},{7,6}} | collective-permute-start | bytes 3538952 | tf_op jit(solution)/shard_map/ppermute | solution.py:329
  876.0 98.4 %collective-permute-start.34 = (bf16[1536,512]{1,0:T(8,128)(2,1)}, bf16[1536,512]{1,0:T(8,128)(2,1)}, u32[]{:S(2)}, u32[]{:S(2)}) collective-permute-start(bf16[1536,512]{1,0:T(8,128)(2,1)} %collective-permute-done.33.refs_2_), channel_id=1, source_target_pairs={{0,1},{1,0},{2,3},{3,2},{4,5},{5,4},{6,7},{7,6}} | collective-permute-start | bytes 4718600 | tf_op jit(solution)/shard_map/ppermute | solution.py:328
  939.6 69.6 %collective-permute-start.40 = (bf16[1536,512]{1,0:T(8,128)(2,1)}, bf16[1536,512]{1,0:T(8,128)(2,1)}, u32[]{:S(2)}, u32[]{:S(2)}) collective-permute-start(bf16[1536,512]{1,0:T(8,128)(2,1)} %copy-done.68), channel_id=1, source_target_pairs={{0,1},{1,0},{2,3},{3,2},{4,5},{5,4},{6,7},{7,6}} | collective-permute-start | bytes 4718600 | tf_op jit(solution)/shard_map/ppermute | solution.py:328
  940.1 69.1 %collective-permute-start.42 = (bf16[1536,512]{1,0:T(8,128)(2,1)}, bf16[1536,512]{1,0:T(8,128)(2,1)}, u32[]{:S(2)}, u32[]{:S(2)}) collective-permute-start(bf16[1536,512]{1,0:T(8,128)(2,1)} %copy-done.69), channel_id=1, source_target_pairs={{0,1},{1,0},{2,3},{3,2},{4,5},{5,4},{6,7},{7,6}} | collective-permute-start | bytes 4718600 | tf_op jit(solution)/shard_map/ppermute | solution.py:328
  (116 other events, 3521.0 us)

commit v3 on v0

v3 whole, which is shorter than its diff:
```python
import functools
import math

import jax
import jax.numpy as jnp
import numpy as np
from jax import lax
from jax.experimental import pallas as pl
from jax.experimental.pallas import tpu as pltpu
from jax.sharding import PartitionSpec as P


EPS = 1e-6
ROPE_BASE = 10000.0
HEAD = 128
BLOCK = 352
TILE = 1024
SUB = 256
OWNED = ((0, 3, 5), (1, 2, 4))
CHUNKS = (256,) + (128,) * 6
CALLS = ((0,), (1, 2), (3, 4), (5, 6), (7,))
SPLIT = 2048
TAIL = 128
MIB = 2**20


def dot(a, b):
    return jnp.dot(a, b, preferred_element_type=jnp.float32)


def normalize(x, gain):
    f = x.astype(jnp.float32)
    inv_rms = lax.rsqrt(jnp.mean(f * f, axis=-1, keepdims=True) + EPS)
    return (f * inv_rms * gain).astype(jnp.bfloat16)


def params(vmem_mib):
    return pltpu.CompilerParams(dimension_semantics=("arbitrary",), vmem_limit_bytes=vmem_mib * MIB)


def cost(flops, data):
    return pl.CostEstimate(flops=int(flops), bytes_accessed=int(data), transcendentals=0)


def pack(jobs, shapes, *arrays):
    n = len(arrays)

    def kernel(*refs):
        srcs, dsts = refs[:n], refs[n:n + len(shapes)]
        stages, sems = refs[n + len(shapes):-1], refs[-1]
        me = lax.axis_index('resp')
        ins = []
        for t, (a, at, b, to) in enumerate(jobs):
            c = pltpu.make_async_copy(srcs[a].at[at(me)], stages[t], sems.at[2 * t])
            c.start()
            ins.append(c)
        outs = []
        for t, (a, at, b, to) in enumerate(jobs):
            ins[t].wait()
            c = pltpu.make_async_copy(stages[t], dsts[b].at[to], sems.at[2 * t + 1])
            c.start()
            outs.append(c)
        for c in outs:
            c.wait()

    out_shape = [jax.ShapeDtypeStruct(shape, jnp.bfloat16) for shape in shapes]
    sizes = [jax.eval_shape(lambda r, to=to: r[to], out_shape[b]).shape for _, _, b, to in jobs]
    hbm = pl.BlockSpec(memory_space=pltpu.HBM)
    return pl.pallas_call(
        kernel,
        in_specs=[hbm] * n,
        out_specs=[hbm] * len(shapes),
        out_shape=out_shape,
        scratch_shapes=[pltpu.VMEM(z, jnp.bfloat16) for z in sizes] + [pltpu.SemaphoreType.DMA((2 * len(jobs),))],
        compiler_params=pltpu.CompilerParams(vmem_limit_bytes=62 * MIB),
        cost_estimate=cost(10**9, 2 * sum(2 * o.size for o in out_shape)),
    )(*arrays)


def project_kernel(layer, far, q_heads, ids_ref, x_ref, gain_ref, far_turn_ref, near_turn_ref, *refs):
    w_refs, (q_ref, kv_ref, w_s) = refs[:-3], refs[-3:]

    @pl.when(pl.program_id(0) == 0)
    def _():
        if far:
            me = lax.axis_index('resp')
            for j, piece in enumerate(w_refs):
                size = piece.shape[1]
                at = pl.ds(pl.multiple_of((me ^ j) * size, size), size)
                for i in range(piece.shape[0]):
                    w_s[at, i * HEAD:(i + 1) * HEAD] = piece[i]
        else:
            for i in range(q_heads):
                w_s[:, i * HEAD:(i + 1) * HEAD] = w_refs[0][0, i]
            w_s[:, q_heads * HEAD:(q_heads + 1) * HEAD] = w_refs[1][0, 0]
            w_s[:, (q_heads + 1) * HEAD:] = w_refs[2][0, 0]

    h = normalize(x_ref[...], gain_ref[layer:layer + 1, :])
    f = dot(h, w_s[...])
    cos_a, sin_a = far_turn_ref[0, 0:1], far_turn_ref[0, 1:2]
    cos_b, sin_b = near_turn_ref[0], near_turn_ref[1]
    cos_part = cos_a * cos_b - sin_a * sin_b
    sin_part = sin_a * cos_b + cos_a * sin_b
    lane = lax.broadcasted_iota(jnp.int32, sin_part.shape, 1)
    sin_part = jnp.where(lane < HEAD // 2, -sin_part, sin_part)
    for i in range(q_heads + 1):
        a = f[:, i * HEAD:(i + 1) * HEAD]
        r = (a * cos_part + pltpu.roll(a, HEAD // 2, 1) * sin_part).astype(jnp.bfloat16)
        if i < q_heads:
            q_ref[:, i * HEAD:(i + 1) * HEAD] = r
        else:
            kv_ref[:, :HEAD] = r
    kv_ref[:, HEAD:] = f[:, (q_heads + 1) * HEAD:].astype(jnp.bfloat16)


def project(layer, ids, x, gain, ws, far, turns, key_rows):
    rows, dim = x.shape
    q_heads = ws[0].shape[0] - 2 if far else ws[0].shape[1]
    q_width = q_heads * HEAD
    width = q_width + 2 * HEAD
    row = lambda b, ids: (b, 0)
    if far:
        w_specs = [pl.BlockSpec(w.shape, lambda b, ids: (0, 0, 0)) for w in ws]
    else:
        w_specs = [pl.BlockSpec((1,) + w.shape[1:], lambda b, ids: (layer, 0, 0, 0)) for w in ws]
    return pl.pallas_call(
        functools.partial(project_kernel, layer, far, q_heads),
        grid_spec=pltpu.PrefetchScalarGridSpec(
            num_scalar_prefetch=1,
            grid=(rows // BLOCK,),
            in_specs=[
                pl.BlockSpec((BLOCK, dim), row),
                pl.BlockSpec(gain.shape, lambda b, ids: (0, 0)),
                pl.BlockSpec((1, 2, HEAD), lambda b, ids: (ids[b], 0, 0)),
                pl.BlockSpec((2, BLOCK, HEAD), lambda b, ids: (0, 0, 0)),
            ] + w_specs,
            out_specs=[pl.BlockSpec((BLOCK, q_width), row), pl.BlockSpec((BLOCK, 2 * HEAD), row)],
            scratch_shapes=[pltpu.VMEM((dim, width), jnp.bfloat16)],
        ),
        out_shape=[
            jax.ShapeDtypeStruct((rows, q_width), jnp.bfloat16),
            jax.ShapeDtypeStruct((key_rows, 2 * HEAD), jnp.bfloat16),
        ],
        compiler_params=params(40),
        cost_estimate=cost(2 * rows * dim * width, 2 * (rows * dim + dim * width + rows * width)),
    )(ids, x, gain, *turns, *ws)


def attention_kernel(num_blocks, heads, parts, ids_ref, q_ref, *refs):
    kvs = refs[:parts]
    o_ref, s0, s1, m0, m1 = refs[parts:parts + 5]
    step = pl.program_id(0)
    block_id = ids_ref[step]
    rows = q_ref.shape[0]
    nt = (((1,), (1,)), ((), ()))
    scale = HEAD ** -0.5 * math.log2(math.e)
    group = 512
    if parts == 1:
        kv_ref = kvs[0]
    else:
        kv_ref = refs[parts + 5]
        per = kvs[0].shape[0] // rows

        @pl.when(step == 0)
        def _():
            for p in range(parts):
                for i in range(per):
                    at = pl.ds(pl.multiple_of(ids_ref[p * per + i] * rows, rows), rows)
                    kv_ref[at, :] = kvs[p][i * rows:(i + 1) * rows, :]

    def body(i):
        first = i * rows
        low = first // 128 * 128
        high = -(-(first + rows) // 128) * 128
        cuts = [(low, high - low)] + [(c, min(group, low - c)) for c in range(0, low, group)]

        def columns(h):
            return pl.ds(pl.multiple_of(h * HEAD, HEAD), HEAD)

        def interleave(h_s, s_out, m_out, h_v, s_in, m_in):
            if h_s is not None:
                q = q_ref[:, columns(h_s)]
                top = None
            if h_v is not None:
                m = m_in[...]
                total, out = None, None
            for c, w in cuts:
                if h_s is not None:
                    s = lax.dot_general(q, kv_ref[c:c + w, :HEAD], nt, preferred_element_type=jnp.float32)
                    if c == low:
                        row = first + lax.broadcasted_iota(jnp.int32, s.shape, 0)
                        col = low + lax.broadcasted_iota(jnp.int32, s.shape, 1)
                        s = jnp.where(col <= row, s, -jnp.inf)
                    s_out[:, c:c + w] = s
                    for g in range(0, w, 128):
                        top = s[:, g:g + 128] if top is None else jnp.maximum(top, s[:, g:g + 128])
                if h_v is not None:
                    ps = []
                    for g in range(c, c + w, 128):
                        p = jnp.exp2((s_in[:, g:g + 128] - m) * scale)
                        total = p if total is None else total + p
                        ps.append(p.astype(jnp.bfloat16))
                    v = kv_ref[c:c + w, HEAD:]
                    if c + w > num_blocks * rows:
                        at = c + lax.broadcasted_iota(jnp.int32, v.shape, 0)
                        v = jnp.where(at < num_blocks * rows, v, jnp.zeros_like(v))
                    pv = dot(jnp.concatenate(ps, axis=1), v)
                    out = pv if out is None else out + pv
            if h_s is not None:
                m_out[...] = jnp.broadcast_to(jnp.max(top, axis=-1, keepdims=True), top.shape)
            if h_v is not None:
                o_ref[:, columns(h_v)] = (out / jnp.sum(total, axis=-1, keepdims=True)).astype(jnp.bfloat16)

        interleave(0, s0, m0, None, None, None)

        def pair(t, _):
            interleave(2 * t + 1, s1, m1, 2 * t, s0, m0)
            interleave(2 * t + 2, s0, m0, 2 * t + 1, s1, m1)
            return 0

        lax.fori_loop(0, heads // 2 - 1, pair, 0)
        interleave(heads - 1, s1, m1, heads - 2, s0, m0)
        interleave(None, None, None, heads - 1, s1, m1)

    for i in range(num_blocks):
        pl.when(block_id == i)(functools.partial(body, i))


def attention(ids, q, kvs, num_blocks, count, pick):
    rows, width = count * BLOCK, q.shape[1]
    keys = -(-num_blocks * BLOCK // 128) * 128
    scratch = [pltpu.VMEM((BLOCK, keys), jnp.float32)] * 2 + [pltpu.VMEM((BLOCK, HEAD), jnp.float32)] * 2
    if len(kvs) > 1:
        scratch.append(pltpu.VMEM((keys, 2 * HEAD), jnp.bfloat16))
    return pl.pallas_call(
        functools.partial(attention_kernel, num_blocks, width // HEAD, len(kvs)),
        grid_spec=pltpu.PrefetchScalarGridSpec(
            num_scalar_prefetch=1,
            grid=(rows // BLOCK,),
            in_specs=[pl.BlockSpec((BLOCK, width), lambda b, ids: (ids[b] if pick else b, 0))]
            + [pl.BlockSpec(kv.shape, lambda b, ids: (0, 0)) for kv in kvs],
            out_specs=pl.BlockSpec((BLOCK, width), lambda b, ids: (b, 0)),
            scratch_shapes=scratch,
        ),
        out_shape=jax.ShapeDtypeStruct((rows, width), jnp.bfloat16),
        compiler_params=params(40),
        cost_estimate=cost(8 * rows * keys * width, rows * width * 4 + keys * HEAD * 4),
    )(ids, q, *kvs)


def output_kernel(layer, ids_ref, x_ref, a_ref, b_ref, wa_ref, gain_ref, *refs):
    pieces, (x_out, u_out, w_s) = refs[:-3], refs[-3:]

    @pl.when(pl.program_id(0) == 0)
    def _():
        me = lax.axis_index('resp')
        for j, piece in enumerate(pieces):
            size = piece.shape[0]
            w_s[pl.ds(pl.multiple_of((me ^ j) * size, size), size), :] = piece[...]

    total = dot(a_ref[...], wa_ref[0]) + dot(b_ref[...], w_s[...])
    x = (x_ref[...].astype(jnp.float32) + total).astype(jnp.bfloat16)
    x_out[...] = x
    u_out[...] = normalize(x, gain_ref[layer:layer + 1, :])


def project_out(layer, ids, x, a, b, w_own, pieces, gain, pick):
    dim = x.shape[1]
    rows, width = a.shape
    row = lambda i, ids: (i, 0)
    return pl.pallas_call(
        functools.partial(output_kernel, layer),
        grid_spec=pltpu.PrefetchScalarGridSpec(
            num_scalar_prefetch=1,
            grid=(rows // BLOCK,),
            in_specs=[
                pl.BlockSpec((BLOCK, dim), lambda i, ids: (ids[i] if pick else i, 0)),
                pl.BlockSpec((BLOCK, width), row),
                pl.BlockSpec((BLOCK, width), row),
                pl.BlockSpec((1, width, dim), lambda i, ids: (layer, 0, 0)),
                pl.BlockSpec(gain.shape, lambda i, ids: (0, 0)),
            ] + [pl.BlockSpec(p.shape, lambda i, ids: (0, 0)) for p in pieces],
            out_specs=[pl.BlockSpec((BLOCK, dim), row), pl.BlockSpec((BLOCK, dim), row)],
            scratch_shapes=[pltpu.VMEM((width, dim), jnp.bfloat16)],
        ),
        out_shape=[jax.ShapeDtypeStruct((rows, dim), jnp.bfloat16)] * 2,
        compiler_params=params(40),
        cost_estimate=cost(4 * rows * dim * width, 6 * rows * dim + 8 * width * dim),
    )(ids, x, a, b, w_own, gain, *pieces)


def mlp_rows(u_ref, out_ref, row_tile, hidden, downs):
    def rows(i, _):
        at = pl.ds(pl.multiple_of(i * row_tile, row_tile), row_tile)
        u = u_ref[at, :]
        part = None
        for inner, down in zip(hidden(u), downs()):
            p = dot(inner, down)
            part = p if part is None else part + p
        out_ref[at, :] += part
        return 0

    n = u_ref.shape[0] // row_tile
    if n == 1:
        rows(0, 0)
    else:
        lax.fori_loop(0, n, rows, 0)


def gated(g, up):
    return (jax.nn.silu(g) * up).astype(jnp.bfloat16)


def mlp_kernel(columns, tile, ids_ref, u_ref, gate_ref, up_ref, down_ref, *refs):
    acc_ref, out_ref = refs if len(refs) == 2 else (None, refs[0])
    step = pl.program_id(0)
    steps = -(-columns // tile)

    @pl.when(step == 0)
    def _():
        out_ref[...] = jnp.zeros_like(out_ref) if acc_ref is None else acc_ref[...]

    def run(width):
        cuts = [(c, min(SUB, width - c)) for c in range(0, width, SUB)]

        def hidden(u):
            return [gated(dot(u, gate_ref[0, :, c:c + w]), dot(u, up_ref[0, :, c:c + w])) for c, w in cuts]

        mlp_rows(u_ref, out_ref, BLOCK, hidden, lambda: [down_ref[0, c:c + w, :] for c, w in cuts])

    pl.when(step < steps - 1)(lambda: run(tile))
    pl.when(step == steps - 1)(lambda: run(columns - (steps - 1) * tile))


def mlp_own(layer, ids, u, rows, tile, w_gate, w_up, w_down, acc=None, first=0, columns=None):
    dim = u.shape[1]
    columns = columns or w_gate.shape[2]
    skip = first // tile
    return pl.pallas_call(
        functools.partial(mlp_kernel, columns, tile),
        grid_spec=pltpu.PrefetchScalarGridSpec(
            num_scalar_prefetch=1,
            grid=(-(-columns // tile),),
            in_specs=[
                pl.BlockSpec((rows, dim), lambda j, ids: (ids[0], 0)),
                pl.BlockSpec((1, dim, tile), lambda j, ids: (layer, 0, skip + j)),
                pl.BlockSpec((1, dim, tile), lambda j, ids: (layer, 0, skip + j)),
                pl.BlockSpec((1, tile, dim), lambda j, ids: (layer, skip + j, 0)),
            ] + [pl.BlockSpec((rows, dim), lambda j, ids: (0, 0), pipeline_mode=pl.Buffered(1))] * (acc is not None),
            out_specs=pl.BlockSpec((rows, dim), lambda j, ids: (0, 0)),
        ),
        out_shape=jax.ShapeDtypeStruct((rows, dim), jnp.float32),
        compiler_params=params(60),
        cost_estimate=cost(6 * rows * dim * columns, 6 * dim * columns + 6 * rows * dim),
    )(ids, u, w_gate, w_up, w_down, *([] if acc is None else [acc]))


def log_prob_rows(x_ref, gain_ref, target_ref, vocab_refs, total):
    me, side = lax.axis_index('resp'), lax.axis_index('model')
    x = (x_ref[...].astype(jnp.float32) + total).astype(jnp.bfloat16)
    h = normalize(x, gain_ref[...])
    target = target_ref[...]
    parts = [dot(h, w[...]) for w in vocab_refs]
    top = None
    picked = 0.0
    for j, logits in enumerate(parts):
        width = logits.shape[1]
        own = vocab_refs[0].shape[1]
        first = side * own if j == 0 else (1 - side) * own + (me ^ (j - 1)) * width
        ids = first + lax.broadcasted_iota(jnp.int32, logits.shape, 1)
        picked = picked + jnp.sum(jnp.where(ids == target, logits, 0.0), axis=-1, keepdims=True)
        m = jnp.max(logits, axis=-1, keepdims=True)
        top = m if top is None else jnp.maximum(top, m)
    exp_total = sum(jnp.sum(jnp.exp(logits - top), axis=-1, keepdims=True) for logits in parts)
    return picked - top - jnp.log(exp_total)


def mlp_pieces_kernel(counts, sizes, tail_blocks, has_acc, head, u_ref, *refs):
    n = sum(counts)
    acc_ref, refs = (refs[0], refs[1:]) if has_acc else (None, refs)
    head_refs, refs = refs[:head], refs[head:]
    wide, tall = refs[:n], refs[n:2 * n]
    out_ref, wide_s, tall_s, sems = refs[2 * n], refs[2 * n + 1:3 * n + 1], refs[-2], refs[-1]
    kinds = [k for k, count in enumerate(counts) for _ in range(count)]
    me = lax.axis_index('resp')

    @pl.when(pl.program_id(0) == 0)
    def _():
        copies = []
        at = 0
        for j, k in enumerate(kinds):
            for i, (src, dst) in enumerate(((wide[j], wide_s[j]), (tall[j], tall_s.at[at:at + sizes[k]]))):
                c = pltpu.make_async_copy(src, dst, sems.at[2 * j + i])
                c.start()
                copies.append(c)
            at += sizes[k]
        for c in copies:
            c.wait()

    u = u_ref[...]
    parts = []
    for j, k in enumerate(kinds):
        f = dot(u, wide_s[j][...])
        inner = gated(f[:, :sizes[k]], f[:, sizes[k]:])
        if tail_blocks and k == len(counts) - 1:
            inner = jnp.where((me ^ (j - sum(counts[:k]))) < tail_blocks, inner, jnp.zeros_like(inner))
        parts.append(inner)
    total = dot(jnp.concatenate(parts, axis=1), tall_s[...])
    if acc_ref is not None:
        total = acc_ref[...] + total
    out_ref[...] = log_prob_rows(*head_refs[:3], head_refs[3:], total) if head else total


def mlp_pieces(u, acc, wides, talls, tail_blocks, head):
    rows, dim = u.shape
    counts = [len(w) for w in wides]
    sizes = [t[0].shape[0] for t in talls]
    wide = [p for w in wides for p in w]
    tall = [p for t in talls for p in t]
    n = len(wide)
    row = lambda i: (i, 0)
    hbm = pl.BlockSpec(memory_space=pltpu.HBM)
    hidden = sum(p.shape[0] for p in tall)
    return pl.pallas_call(
        functools.partial(mlp_pieces_kernel, counts, sizes, tail_blocks, acc is not None, len(head)),
        grid=(rows // BLOCK,),
        in_specs=[pl.BlockSpec((BLOCK, dim), row)] * (1 if acc is None else 2)
        + [pl.BlockSpec((BLOCK if a.shape[0] == rows else a.shape[0], a.shape[1]), row if a.shape[0] == rows else lambda i: (0, 0)) for a in head]
        + [hbm] * (2 * n),
        out_specs=pl.BlockSpec((BLOCK, 1 if head else dim), row),
        out_shape=jax.ShapeDtypeStruct((rows, 1 if head else dim), jnp.float32),
        scratch_shapes=[pltpu.VMEM(p.shape, jnp.bfloat16) for p in wide]
        + [pltpu.VMEM((hidden, dim), jnp.bfloat16), pltpu.SemaphoreType.DMA((2 * n,))],
        compiler_params=params(48),
        cost_estimate=cost(6 * rows * dim * hidden, 6 * dim * hidden + 10 * rows * dim),
    )(u, *([] if acc is None else [acc]), *head, *wide, *tall)


def solution(mesh):
    groups = mesh.shape['resp']
    row_axes = ('prompts', 'resp')
    head_spec = P(None, None, 'model', None)
    in_specs = (P(row_axes, None), P(row_axes, None, None), P(row_axes, None), P(row_axes), P(None, None), head_spec, head_spec, head_spec, P(None, 'model', None, None), P(None, None), P(None, None, 'model'), P(None, None, 'model'), P(None, 'model', None), P(None), P(None, 'model'))
    across = [(0, 1), (1, 0)]
    core = [(i, i ^ 1) for i in range(groups)]
    chip = [(i, i ^ 2) for i in range(groups)]
    both = [(i, i ^ 3) for i in range(groups)]

    def swap(a):
        return lax.ppermute(a, 'model', across)

    def spread(a):
        return [a, lax.ppermute(a, 'resp', core), lax.ppermute(a, 'resp', chip), lax.ppermute(a, 'resp', both)]

    def device_body(x_prompt, x_resp, targets, resp_lens, attn_gain, w_query, w_key, w_value, w_out, mlp_gain, w_gate, w_up, w_down, final_gain, w_vocab):
        me = lax.axis_index('resp')
        side = lax.axis_index('model')
        resp_len = x_resp.shape[1]
        dim = x_resp.shape[2]
        prompt_len = x_prompt.shape[0] * groups
        tokens = prompt_len + resp_len
        blocks = tokens // BLOCK
        key_rows = -(-tokens // 128) * 128
        q_width = w_query.shape[2] * HEAD
        ffn = w_gate.shape[2]
        vocab = w_vocab.shape[1]
        w_out = w_out.reshape(w_out.shape[0], q_width, dim)
        w_query = jnp.transpose(w_query, (0, 2, 1, 3))
        w_key = jnp.transpose(w_key, (0, 2, 1, 3))
        w_value = jnp.transpose(w_value, (0, 2, 1, 3))
        q_heads = q_width // HEAD
        own_qkv = (w_query, w_key, w_value)

        def in_order(pieces):
            stack = jnp.stack(pieces)
            return jnp.concatenate([lax.dynamic_index_in_dim(stack, me ^ j, 0, keepdims=False) for j in range(groups)], axis=0)

        every_row = slice(None)
        r_in, r_out, piece = dim // groups, q_width // groups, vocab // groups

        def attention_jobs(l, first):
            rows_in = lambda me: pl.ds(me * r_in, r_in)
            return [
                (0, lambda me: (l, every_row, rows_in(me), every_row), first, (slice(0, q_heads),)),
                (1, lambda me: (l, every_row, rows_in(me), every_row), first, (slice(q_heads, q_heads + 1),)),
                (2, lambda me: (l, every_row, rows_in(me), every_row), first, (slice(q_heads + 1, q_heads + 2),)),
                (3, lambda me: (l, pl.ds(me * r_out, r_out), every_row), first + 1, (slice(None),)),
            ]

        attention_shapes = [(q_heads + 2, r_in, HEAD), (r_out, dim)]
        qkv0, out0 = pack(attention_jobs(0, 0), attention_shapes, *own_qkv, w_out)
        jobs = attention_jobs(1, 0) + [(7, lambda me: (every_row, pl.ds(me * piece, piece)), 2, (slice(None),))]
        shapes = attention_shapes + [(dim, piece)]
        main = sum(CHUNKS)
        tail_blocks = (ffn - groups * main) // TAIL
        done = 0
        for c, size in enumerate(CHUNKS + (TAIL,)):
            if c < len(CHUNKS):
                at = lambda me, done=done: pl.multiple_of(me * main + done, 128)
            else:
                at = lambda me: pl.multiple_of(groups * main + jnp.minimum(me, tail_blocks - 1) * TAIL, 128)
            n = len(shapes)
            jobs += [
                (4, lambda me, at=at, size=size: (1, every_row, pl.ds(at(me), size)), n, (every_row, slice(0, size))),
                (5, lambda me, at=at, size=size: (1, every_row, pl.ds(at(me), size)), n, (every_row, slice(size, 2 * size))),
                (6, lambda me, at=at, size=size: (1, pl.ds(at(me), size), every_row), n + 1, (every_row,)),
            ]
            shapes += [(dim, 2 * size), (size, dim)]
            done += size
        qkv0_y = swap(qkv0)
        qkv1, out1, voc, *chunks = pack(jobs, shapes, *own_qkv, w_out, w_gate, w_up, w_down, w_vocab)

        qkv_far0 = spread(qkv0_y)
        out_far0 = spread(swap(out0))
        qkv_far1 = spread(swap(qkv1))
        out_far1 = spread(swap(out1))
        vocab_far = spread(swap(voc))
        wide, tall = [], []
        for c in range(len(chunks) // 2):
            w, t = swap(chunks[2 * c]), swap(chunks[2 * c + 1])
            wf, tf = lax.ppermute(w, 'resp', chip), lax.ppermute(t, 'resp', chip)
            wide.append([w, lax.ppermute(w, 'resp', core), wf, lax.ppermute(wf, 'resp', core)])
            tall.append([t, lax.ppermute(t, 'resp', core), tf, lax.ppermute(tf, 'resp', core)])

        prompt = in_order(spread(x_prompt))
        x = jnp.concatenate([prompt, x_resp[0]], axis=0)

        half = HEAD // 2
        frequency = (ROPE_BASE ** (-(np.arange(HEAD) % half) / half)).astype(np.float32)

        def turn(positions, axis):
            angles = positions.astype(np.float32)[:, None] * frequency
            return jnp.asarray(np.stack([np.cos(angles), np.sin(angles)], axis=axis))

        turns = (turn(np.arange(blocks) * BLOCK, 1), turn(np.arange(BLOCK), 0))

        every = jnp.arange(blocks, dtype=jnp.int32)
        owned = jnp.array(OWNED, jnp.int32)
        mine = owned[side]
        theirs = owned[1 - side]
        per_side = len(OWNED[0])
        q_own, kv_own = project(0, every, x, attn_gain, own_qkv, False, turns, key_rows)
        a = attention(theirs, q_own, [kv_own], blocks, per_side, True)
        q_far, kv_far = project(0, every, x, attn_gain, qkv_far0, True, turns, key_rows)
        b = attention(theirs, q_far, [kv_far], blocks, per_side, True)
        _, u = project_out(0, theirs, x, a, b, w_out, out_far0, mlp_gain, True)
        got = []
        for i in range(per_side):
            part = mlp_own(0, jnp.full((1,), i, jnp.int32), u, BLOCK, 512, w_gate, w_up, w_down)
            got.append(swap(part))
        a = attention(mine, q_own, [kv_own], blocks, per_side, True)
        b = attention(mine, q_far, [kv_far], blocks, per_side, True)
        x, u = project_out(0, mine, x, a, b, w_out, out_far0, mlp_gain, True)
        zero = jnp.zeros((1,), jnp.int32)
        part_mine = mlp_own(0, zero, u, per_side * BLOCK, TILE, w_gate, w_up, w_down)
        x = (x.astype(jnp.float32) + (part_mine + jnp.concatenate(got, axis=0))).astype(jnp.bfloat16)

        q_far, kv_far = project(1, mine, x, attn_gain, qkv_far1, True, turns, per_side * BLOCK)
        got_own = swap(kv_far)
        q_own, kv_own = project(1, mine, x, attn_gain, own_qkv, False, turns, per_side * BLOCK)
        got_far = swap(kv_own)

        def merge(own_part, far_part):
            def split(a):
                return [a[i * BLOCK:(i + 1) * BLOCK] for i in range(a.shape[0] // BLOCK)]

            a, b = split(own_part), split(far_part)
            order = [[None] * blocks, [None] * blocks]
            for s in range(2):
                for i, blk in enumerate(OWNED[s]):
                    order[s][blk] = a[i]
                for i, blk in enumerate(OWNED[1 - s]):
                    order[s][blk] = b[i]
            return jnp.concatenate([jnp.where(side == 0, p0, p1) for p0, p1 in zip(*order)], axis=0)

        mine_first = jnp.concatenate([mine, theirs])
        mixed_own = attention(mine_first, q_own, [kv_own, got_own], blocks, per_side, False)
        mixed_far = attention(mine_first, q_far, [kv_far, got_far], blocks, per_side, False)
        x, u = project_out(1, mine, x, mixed_own, mixed_far, w_out, out_far1, mlp_gain, False)
        padded_targets = jnp.concatenate([jnp.zeros((prompt_len,), targets.dtype), targets[0]]).reshape(blocks, BLOCK)
        target_own = jnp.concatenate([lax.dynamic_index_in_dim(padded_targets, mine[i], 0, keepdims=False) for i in range(per_side)])[:, None]
        total = None
        for n, call in enumerate(CALLS):
            if n == 1:
                total = mlp_own(1, zero, u, per_side * BLOCK, TILE, w_gate, w_up, w_down, total, 0, SPLIT)
            if n == 2:
                total = mlp_own(1, zero, u, per_side * BLOCK, TILE, w_gate, w_up, w_down, total, SPLIT, ffn - SPLIT)
            head = (x, final_gain[None, :], target_own, w_vocab, *vocab_far) if n == len(CALLS) - 1 else ()
            total = mlp_pieces(u, total, [wide[c] for c in call], [tall[c] for c in call], tail_blocks if len(CHUNKS) in call else 0, head)
        log_probs = total[:, 0]
        log_probs = merge(log_probs, swap(log_probs))[prompt_len:]
        log_probs = jnp.where(jnp.arange(resp_len) < resp_lens[0], log_probs, 0.0)
        return log_probs[None, :]

    return jax.shard_map(device_body, mesh=mesh, in_specs=in_specs, out_specs=P(row_axes, None), check_vma=False)
```

time: 1810 us -> 882 us (0.49)
  waiting for transfers between devices: 1120 us -> 259 us
  Pallas kernels: 0 us -> 484 us
  matrix products: 456 us -> 0 us
  other arithmetic: 145 us -> 7.46 us
  starting transfers between devices: 0.13 us -> 66.6 us
  blocking collectives: 44.4 us -> 0 us
  local copies, waits for them, and re-layouts: 19 us -> 53.1 us
    psum x4 -> x0, waiting for transfers between devices: 1120 us -> none  [the longest x2 568 us: device_step(): lax.psum(attn_part, 'model')]
    pallas_call x0 -> x26, Pallas kernels: none -> 484 us  [the longest x6 194 us: mlp_own(): pl.pallas_call(functools.partial(mlp_kernel, columns, tile), grid_spec=pl...]
    dot_general x18 -> x0, matrix products: 451 us -> none  [the longest x2 87.5 us: device_step(): jnp.dot(hidden, w_up[layer_idx], preferred_element_type=jnp.float32)]
    ppermute x0 -> x93, waiting for transfers between devices: none -> 259 us  [the longest x27 175 us: swap(): return lax.ppermute(a, 'model', across)]
    reduce_sum x8 -> x0, other arithmetic: 109 us -> none  [the longest x2 69.8 us: attend(): row_sum = jnp.moveaxis(jnp.sum(exp_scores, axis=-1), -1, -3)]
    ppermute x0 -> x93, starting transfers between devices: none -> 66.6 us  [the longest x27 30.1 us: swap(): return lax.ppermute(a, 'model', across)]
    unnamed x65 -> x242, local copies, waits for them, and re-layouts: 12.7 us -> 47.8 us
    all_gather x4 -> x0, blocking collectives: 32.5 us -> none  [the longest x2 18.1 us: device_step(): prompt_keys = lax.all_gather(keys[:prompt_rows], 'resp', axis=0, tiled=True)]
  transfers between devices with their start and end apart: 4 -> 93, of which waited for: 4 -> 17; matrix products, arithmetic and copies ran while one was open for 1% -> 1% of each run, Pallas kernels for 0% -> 53%
where the time goes in v3:
time: 882 us; the launch traced here: 878 us
  Pallas kernels  484 us (55%)
  waiting for transfers between devices  259 us (29%)
  starting transfers between devices  66.6 us (8%)
  local copies, waits for them, and re-layouts  53.1 us (6%)
    pallas_call x6, Pallas kernels, mlp_own(): pl.pallas_call(functools.partial(mlp_kernel, columns, tile), grid_spec=pl...  194 us
    ppermute x27, waiting for transfers between devices, swap(): return lax.ppermute(a, 'model', across)  175 us
    pallas_call x6, Pallas kernels, attention(): pl.pallas_call(functools.partial(attention_kernel, num_blocks, width // H...  121 us
    pallas_call x5, Pallas kernels, mlp_pieces(): pl.pallas_call(functools.partial(mlp_pieces_kernel, counts, sizes, tail_b...  88.9 us
    unnamed x242, local copies, waits for them, and re-layouts  47.8 us
    ppermute x16, waiting for transfers between devices, device_body(): wf, tf = (lax.ppermute(w, 'resp', chip), lax.ppermute(t, 'resp', chip))  43.2 us
    pallas_call x4, Pallas kernels, project(): pl.pallas_call(functools.partial(project_kernel, layer, far, q_heads), gr...  39.4 us
    ppermute x27, starting transfers between devices, swap(): return lax.ppermute(a, 'model', across)  30.1 us
  transfers between devices with their start and end apart: 93, of which 17 were waited for; matrix products, arithmetic and copies ran while one was open for 1% of the time, Pallas kernels for 53%

profile of v3, /device:TPU:0, one launch (start us, length us, event | category | flops | bytes accessed | tf_op | source)
XLA Modules:
  0.0 878.0 jit_solution(10547860108525567731)
XLA Ops:
  8.2 10.0 %shard_map.186 = (bf16[8,384,128]{2,1,0:T(8,128)(2,1)}, bf16[192,1536]{1,0:T(8,128)(2,1)}, bf16[1536,256]{1,0:T(8,128)(2,1)}, bf16[1536,512]{1,0:T(8,128)(2,1)},...) custom-call(bf16[2,6,1536,128]{3,2,1,0:T(8,128)(2,1)} %bitcast.30, ...), custom_call_target="tpu_custom_call" | custom-call | flops 1000000000 | bytes 25559040 | tf_op jit(solution)/shard_map/pallas_call | solution.py:69
  26.4 12.8 %shard_map.172 = (bf16[2112,768]{1,0:T(8,128)(2,1)S(1)}, bf16[2176,256]{1,0:T(8,128)(2,1)S(1)}) custom-call(s32[6]{0:T(128)S(1)} %iota.9.ids_ref, bf16[2112,1536]{1,0:T(8,128)(2,1)} %copy-done.17, f32[2,1536]{1,0:T(2,128)S(1)} %copy-done.77, f32[6,2,128]{2,1,0:T(2,128)S(1)} %copy-done.83, f32[2,352,128]{2,1,0:T(8,128)S(1)} %copy-done.80, ...), custom_call_target="tpu_custom_call" | custom-call | flops 6643777536 | bytes 13959168 | tf_op jit(solution)/shard_map/pallas_call | solution.py:126
  39.2 15.1 %shard_map.179.a_ref = bf16[1056,768]{1,0:T(8,128)(2,1)S(1)} custom-call(s32[3]{0:T(128)S(1)} %get-tuple-element.91.ids_ref, bf16[2112,768]{1,0:T(8,128)(2,1)S(1)} %get-tuple-element.39.q_ref, bf16[2176,256]{1,0:T(8,128)(2,1)S(1)} %get-tuple-element.40.refs_0_), custom_call_target="tpu_custom_call" | custom-call | flops 14118027264 | bytes 4358144 | tf_op jit(solution)/shard_map/pallas_call | solution.py:235
  57.3 29.3 %shard_map.173.a_ref = bf16[1056,768]{1,0:T(8,128)(2,1)S(1)} custom-call(s32[3]{0:T(128)S(1)} %get-tuple-element.90.ids_ref, bf16[2112,768]{1,0:T(8,128)(2,1)S(1)} %get-tuple-element.39.q_ref, bf16[2176,256]{1,0:T(8,128)(2,1)S(1)} %get-tuple-element.40.refs_0_), custom_call_target="tpu_custom_call" | custom-call | flops 14118027264 | bytes 4358144 | tf_op jit(solution)/shard_map/pallas_call | solution.py:235
  93.3 11.6 %shard_map.175 = (bf16[2112,768]{1,0:T(8,128)(2,1)S(1)}, bf16[2176,256]{1,0:T(8,128)(2,1)S(1)}) custom-call(s32[6]{0:T(128)S(1)} %iota.10.ids_ref, bf16[2112,1536]{1,0:T(8,128)(2,1)S(1)} %bitcast.42, f32[2,1536]{1,0:T(2,128)S(1)} %copy-done.77, f32[6,2,128]{2,1,0:T(2,128)S(1)} %copy-done.83, f32[2,352,128]{2,1,0:T(8,128)S(1)} %copy-done.80, ...), custom_call_target="tpu_custom_call" | custom-call | flops 6643777536 | bytes 13959168 | tf_op jit(solution)/shard_map/pallas_call | solution.py:126
  104.9 27.0 %shard_map.180.b_ref = bf16[1056,768]{1,0:T(8,128)(2,1)S(1)} custom-call(s32[3]{0:T(128)S(1)} %get-tuple-element.91.ids_ref, bf16[2112,768]{1,0:T(8,128)(2,1)S(1)} %get-tuple-element.42.q_ref, bf16[2176,256]{1,0:T(8,128)(2,1)S(1)} %get-tuple-element.43.refs_0_), custom_call_target="tpu_custom_call" | custom-call | flops 14118027264 | bytes 4358144 | tf_op jit(solution)/shard_map/pallas_call | solution.py:235
  136.3 10.1 %shard_map.181 = (bf16[1056,1536]{1,0:T(8,128)(2,1)}, bf16[1056,1536]{1,0:T(8,128)(2,1)S(1)}) custom-call(s32[3]{0:T(128)S(1)} %get-tuple-element.91.ids_ref, bf16[2112,1536]{1,0:T(8,128)(2,1)} %copy-done.17, bf16[1056,768]{1,0:T(8,128)(2,1)S(1)} %copy-done.89, bf16[1056,768]{1,0:T(8,128)(2,1)S(1)} %shard_map.180.b_ref, bf16[2,768,1536]{2,1,0:T(8,128)(2,1)} %bitcast.45, ...), custom_call_target="tpu_custom_call" | custom-call | flops 4982833152 | bytes 19169280 | tf_op jit(solution)/shard_map/pallas_call | solution.py:271
  155.4 23.2 %shard_map.182 = f32[352,1536]{1,0:T(8,128)} custom-call(s32[1]{0:T(128)} %constant.48.clone.1.ids_ref, bf16[1056,1536]{1,0:T(8,128)(2,1)} %copy-done, bf16[2,1536,4480]{2,1,0:T(8,128)(2,1)} %gate_ref.11, bf16[2,1536,4480]{2,1,0:T(8,128)(2,1)} %up_ref.11, bf16[2,4480,1536]{2,1,0:T(8,128)(2,1)} %down_ref.11), custom_call_target="tpu_custom_call" | custom-call | flops 14533263360 | bytes 44531712 | tf_op jit(solution)/shard_map/pallas_call | solution.py:339
  188.8 23.2 %shard_map.183 = f32[352,1536]{1,0:T(8,128)} custom-call(s32[1]{0:T(128)} %constant.49.clone.1.ids_ref, bf16[1056,1536]{1,0:T(8,128)(2,1)} %copy-done, bf16[2,1536,4480]{2,1,0:T(8,128)(2,1)} %gate_ref.11, bf16[2,1536,4480]{2,1,0:T(8,128)(2,1)} %up_ref.11, bf16[2,4480,1536]{2,1,0:T(8,128)(2,1)} %down_ref.11), custom_call_target="tpu_custom_call" | custom-call | flops 14533263360 | bytes 44531712 | tf_op jit(solution)/shard_map/pallas_call | solution.py:339
  222.1 14.7 %collective-permute-done.32.refs_1_ = bf16[1536,256]{1,0:T(8,128)(2,1)S(1)} collective-permute-done((bf16[1536,256]{1,0:T(8,128)(2,1)}, bf16[1536,256]{1,0:T(8,128)(2,1)S(1)}, u32[]{:S(2)}, u32[]{:S(2)}) %collective-permute-start.32) | collective-permute-done | bytes 786464 | tf_op jit(solution)/shard_map/ppermute | solution.py:450
  237.3 16.4 %collective-permute-done.36.refs_5_ = bf16[1536,256]{1,0:T(8,128)(2,1)} collective-permute-done((bf16[1536,256]{1,0:T(8,128)(2,1)}, bf16[1536,256]{1,0:T(8,128)(2,1)}, u32[]{:S(2)}, u32[]{:S(2)}) %collective-permute-start.36) | collective-permute-done | bytes 786464 | tf_op jit(solution)/shard_map/ppermute | solution.py:450
  254.3 23.3 %shard_map.184 = f32[352,1536]{1,0:T(8,128)} custom-call(s32[1]{0:T(128)} %constant.50.clone.1.ids_ref, bf16[1056,1536]{1,0:T(8,128)(2,1)} %copy-done, bf16[2,1536,4480]{2,1,0:T(8,128)(2,1)} %gate_ref.11, bf16[2,1536,4480]{2,1,0:T(8,128)(2,1)} %up_ref.11, bf16[2,4480,1536]{2,1,0:T(8,128)(2,1)} %down_ref.11), custom_call_target="tpu_custom_call" | custom-call | flops 14533263360 | bytes 44531712 | tf_op jit(solution)/shard_map/pallas_call | solution.py:339
  291.2 15.8 %shard_map.176.b_ref = bf16[1056,768]{1,0:T(8,128)(2,1)S(1)} custom-call(s32[3]{0:T(128)S(1)} %get-tuple-element.90.ids_ref, bf16[2112,768]{1,0:T(8,128)(2,1)S(1)} %copy-done.93, bf16[2176,256]{1,0:T(8,128)(2,1)S(1)} %copy-done.95), custom_call_target="tpu_custom_call" | custom-call | flops 14118027264 | bytes 4358144 | tf_op jit(solution)/shard_map/pallas_call | solution.py:235
  309.2 9.5 %shard_map.177 = (bf16[1056,1536]{1,0:T(8,128)(2,1)S(1)}, bf16[1056,1536]{1,0:T(8,128)(2,1)S(1)}) custom-call(s32[3]{0:T(128)S(1)} %get-tuple-element.90.ids_ref, bf16[2112,1536]{1,0:T(8,128)(2,1)} %copy-done.17, bf16[1056,768]{1,0:T(8,128)(2,1)S(1)} %copy-done.87, bf16[1056,768]{1,0:T(8,128)(2,1)S(1)} %shard_map.176.b_ref, bf16[2,768,1536]{2,1,0:T(8,128)(2,1)} %bitcast.46, ...), custom_call_target="tpu_custom_call" | custom-call | flops 4982833152 | bytes 19169280 | tf_op jit(solution)/shard_map/pallas_call | solution.py:271
  328.3 56.4 %shard_map.178 = f32[1056,1536]{1,0:T(8,128)} custom-call(s32[1]{0:T(128)} %constant.48.clone.1.ids_ref, bf16[1056,1536]{1,0:T(8,128)(2,1)} %copy-done.85, bf16[2,1536,4480]{2,1,0:T(8,128)(2,1)} %gate_ref.11, bf16[2,1536,4480]{2,1,0:T(8,128)(2,1)} %up_ref.11, bf16[2,4480,1536]{2,1,0:T(8,128)(2,1)} %down_ref.11), custom_call_target="tpu_custom_call" | custom-call | flops 43599790080 | bytes 51019776 | tf_op jit(solution)/shard_map/pallas_call | solution.py:339
  387.6 32.4 %collective-permute-done.12 = f32[352,1536]{1,0:T(8,128)} collective-permute-done((f32[352,1536]{1,0:T(8,128)}, f32[352,1536]{1,0:T(8,128)}, u32[]{:S(2)}, u32[]{:S(2)}) %collective-permute-start.12) | collective-permute-done | bytes 2162720 | tf_op jit(solution)/shard_map/ppermute | solution.py:450
  421.5 44.8 %collective-permute-done.13 = f32[352,1536]{1,0:T(8,128)} collective-permute-done((f32[352,1536]{1,0:T(8,128)}, f32[352,1536]{1,0:T(8,128)}, u32[]{:S(2)}, u32[]{:S(2)}) %collective-permute-start.13) | collective-permute-done | bytes 2162720 | tf_op jit(solution)/shard_map/ppermute | solution.py:450
  472.7 43.1 %collective-permute-done.84.refs_9_ = bf16[1536,256]{1,0:T(8,128)(2,1)S(1)} collective-permute-done((bf16[1536,256]{1,0:T(8,128)(2,1)}, bf16[1536,256]{1,0:T(8,128)(2,1)S(1)}, u32[]{:S(2)}, u32[]{:S(2)}) %collective-permute-start.84) | collective-permute-done | bytes 786464 | tf_op jit(solution)/shard_map/ppermute | solution.py:450
  553.5 16.6 %shard_map.189.b_ref = bf16[1056,768]{1,0:T(8,128)(2,1)S(1)} custom-call(s32[6]{0:T(128)S(1)} %pad_add_fusion.ids_ref, bf16[1056,768]{1,0:T(8,128)(2,1)S(1)} %get-tuple-element.52.q_ref, bf16[1056,256]{1,0:T(8,128)(2,1)S(1)} %get-tuple-element.51.refs_0_, bf16[1056,256]{1,0:T(8,128)(2,1)} %collective-permute-done.19.refs_1_), custom_call_target="tpu_custom_call" | custom-call | flops 14118027264 | bytes 4358144 | tf_op jit(solution)/shard_map/pallas_call | solution.py:235
  570.7 25.6 %collective-permute-done.22.refs_2_ = bf16[192,1536]{1,0:T(8,128)(2,1)S(1)} collective-permute-done((bf16[192,1536]{1,0:T(8,128)(2,1)S(1)}, bf16[192,1536]{1,0:T(8,128)(2,1)S(1)}, u32[]{:S(2)}, u32[]{:S(2)}) %collective-permute-start.22) | collective-permute-done | bytes 589856 | tf_op jit(solution)/shard_map/ppermute | solution.py:453
  596.2 16.8 %collective-permute-done.30.refs_6_ = bf16[256,1536]{1,0:T(8,128)(2,1)S(1)} collective-permute-done((bf16[256,1536]{1,0:T(8,128)(2,1)S(1)}, bf16[256,1536]{1,0:T(8,128)(2,1)S(1)}, u32[]{:S(2)}, u32[]{:S(2)}) %collective-permute-start.30) | collective-permute-done | bytes 786464 | tf_op jit(solution)/shard_map/ppermute | solution.py:521
  613.6 17.0 %shard_map.188.a_ref = bf16[1056,768]{1,0:T(8,128)(2,1)S(1)} custom-call(s32[6]{0:T(128)S(1)} %pad_add_fusion.ids_ref, bf16[1056,768]{1,0:T(8,128)(2,1)S(1)} %copy-done.91, bf16[1056,256]{1,0:T(8,128)(2,1)} %get-tuple-element.49.refs_0_, bf16[1056,256]{1,0:T(8,128)(2,1)S(1)} %collective-permute-done.18.refs_1_), custom_call_target="tpu_custom_call" | custom-call | flops 14118027264 | bytes 4358144 | tf_op jit(solution)/shard_map/pallas_call | solution.py:235
  648.4 16.1 %shard_map.191.refs_0_ = f32[1056,1536]{1,0:T(8,128)} custom-call(bf16[1056,1536]{1,0:T(8,128)(2,1)} %copy-done.1, bf16[1536,512]{1,0:T(8,128)(2,1)} %collective-permute-done.24.refs_0_, bf16[1536,512]{1,0:T(8,128)(2,1)} %copy-done.106, bf16[1536,512]{1,0:T(8,128)(2,1)} %copy-done.105, bf16[1536,512]{1,0:T(8,128)(2,1)} %copy-done.107, ...), custom_call_target="tpu_custom_call" | custom-call | flops 9965666304 | bytes 25657344 | tf_op jit(solution)/shard_map/pallas_call | solution.py:424
  667.9 13.2 %collective-permute-done.38.refs_7_ = bf16[1536,256]{1,0:T(8,128)(2,1)} collective-permute-done((bf16[1536,256]{1,0:T(8,128)(2,1)}, bf16[1536,256]{1,0:T(8,128)(2,1)}, u32[]{:S(2)}, u32[]{:S(2)}) %collective-permute-start.38) | collective-permute-done | bytes 786464 | tf_op jit(solution)/shard_map/ppermute | solution.py:521
  681.1 31.1 %shard_map.192.refs_0_ = f32[1056,1536]{1,0:T(8,128)} custom-call(s32[1]{0:T(128)} %constant.48.clone.1.ids_ref, bf16[1056,1536]{1,0:T(8,128)(2,1)} %copy-done.1, bf16[2,1536,4480]{2,1,0:T(8,128)(2,1)} %gate_ref.11, bf16[2,1536,4480]{2,1,0:T(8,128)(2,1)} %up_ref.11, bf16[2,4480,1536]{2,1,0:T(8,128)(2,1)} %down_ref.11, f32[1056,1536]{1,0:T(8,128)} %shard_map.191.refs_0_), custom_call_target="tpu_custom_call" | custom-call | flops 19931332608 | bytes 28606464 | tf_op jit(solution)/shard_map/pallas_call | solution.py:339
  718.7 17.4 %shard_map.193.refs_0_ = f32[1056,1536]{1,0:T(8,128)} custom-call(bf16[1056,1536]{1,0:T(8,128)(2,1)} %copy-done.1, f32[1056,1536]{1,0:T(8,128)} %shard_map.192.refs_0_, bf16[1536,256]{1,0:T(8,128)(2,1)S(1)} %copy-done.21, bf16[1536,256]{1,0:T(8,128)(2,1)} %collective-permute-done.33.refs_2_, bf16[1536,256]{1,0:T(8,128)(2,1)} %collective-permute-done.34.refs_3_, ...), custom_call_target="tpu_custom_call" | custom-call | flops 9965666304 | bytes 25657344 | tf_op jit(solution)/shard_map/pallas_call | solution.py:424
  739.0 11.3 %collective-permute-done.54.refs_7_ = bf16[1536,256]{1,0:T(8,128)(2,1)} collective-permute-done((bf16[1536,256]{1,0:T(8,128)(2,1)}, bf16[1536,256]{1,0:T(8,128)(2,1)}, u32[]{:S(2)}, u32[]{:S(2)}) %collective-permute-start.54) | collective-permute-done | bytes 786464 | tf_op jit(solution)/shard_map/ppermute | solution.py:521
  751.7 36.9 %shard_map.194.refs_0_ = f32[1056,1536]{1,0:T(8,128)} custom-call(s32[1]{0:T(128)} %constant.48.clone.1.ids_ref, bf16[1056,1536]{1,0:T(8,128)(2,1)} %copy-done.1, bf16[2,1536,4480]{2,1,0:T(8,128)(2,1)} %gate_ref.11, bf16[2,1536,4480]{2,1,0:T(8,128)(2,1)} %up_ref.11, bf16[2,4480,1536]{2,1,0:T(8,128)(2,1)} %down_ref.11, f32[1056,1536]{1,0:T(8,128)} %shard_map.193.refs_0_), custom_call_target="tpu_custom_call" | custom-call | flops 23668457472 | bytes 32145408 | tf_op jit(solution)/shard_map/pallas_call | solution.py:339
  797.2 17.2 %shard_map.195.refs_0_ = f32[1056,1536]{1,0:T(8,128)} custom-call(bf16[1056,1536]{1,0:T(8,128)(2,1)} %copy-done.1, f32[1056,1536]{1,0:T(8,128)} %shard_map.194.refs_0_, bf16[1536,256]{1,0:T(8,128)(2,1)S(1)} %copy-done.19, bf16[1536,256]{1,0:T(8,128)(2,1)S(1)} %copy-done.25, bf16[1536,256]{1,0:T(8,128)(2,1)} %collective-permute-done.50.refs_3_, ...), custom_call_target="tpu_custom_call" | custom-call | flops 9965666304 | bytes 25657344 | tf_op jit(solution)/shard_map/pallas_call | solution.py:424
  821.8 17.3 %shard_map.196.refs_0_ = f32[1056,1536]{1,0:T(8,128)} custom-call(bf16[1056,1536]{1,0:T(8,128)(2,1)} %copy-done.1, f32[1056,1536]{1,0:T(8,128)} %shard_map.195.refs_0_, bf16[1536,256]{1,0:T(8,128)(2,1)} %collective-permute-done.64.refs_1_, bf16[1536,256]{1,0:T(8,128)(2,1)S(1)} %collective-permute-done.65.refs_2_, ...), custom_call_target="tpu_custom_call" | custom-call | flops 9965666304 | bytes 25657344 | tf_op jit(solution)/shard_map/pallas_call | solution.py:424
  839.2 11.8 %collective-permute-done.83.refs_8_ = bf16[1536,256]{1,0:T(8,128)(2,1)S(1)} collective-permute-done((bf16[1536,256]{1,0:T(8,128)(2,1)}, bf16[1536,256]{1,0:T(8,128)(2,1)S(1)}, u32[]{:S(2)}, u32[]{:S(2)}) %collective-permute-start.83) | collective-permute-done | bytes 786464 | tf_op jit(solution)/shard_map/ppermute | solution.py:453
  852.2 20.8 %shard_map.197 = f32[1056,1]{1,0:T(8,128)S(1)} custom-call(bf16[1056,1536]{1,0:T(8,128)(2,1)} %copy-done.1, f32[1056,1536]{1,0:T(8,128)} %shard_map.196.refs_0_, bf16[1056,1536]{1,0:T(8,128)(2,1)} %copy-done.6, f32[1,1536]{1,0:T(1,128)S(1)} %broadcast_in_dim.14.refs_2_, s32[1056,1]{1,0:T(8,128)S(1)} %broadcast_in_dim.18.refs_3_, bf16[1536,1024]{1,0:T(8,128)(2,1)} %refs_4_.3, ...), custom_call_target="tpu_custom_call" | custom-call | flops 4982833152 | bytes 20938752 | tf_op jit(solution)/shard_map/pallas_call | solution.py:424
  (442 shorter events, 182.5 us)
Async XLA Ops:
  5.7 49.8 %collective-permute-start.3 = (bf16[8,384,128]{2,1,0:T(8,128)(2,1)}, bf16[8,384,128]{2,1,0:T(8,128)(2,1)S(1)}, u32[]{:S(2)}, u32[]{:S(2)}) collective-permute-start(bf16[8,384,128]{2,1,0:T(8,128)(2,1)} %get-tuple-element.41), channel_id=1, source_target_pairs={{0,4},{4,0},{1,5},{5,1},{2,6},{6,2},{3,7},{7,3}} | collective-permute-start | bytes 2359304 | tf_op jit(solution)/shard_map/ppermute | solution.py:450
  7.5 79.2 %collective-permute-start.7 = (bf16[192,1536]{1,0:T(8,128)(2,1)}, bf16[192,1536]{1,0:T(8,128)(2,1)}, u32[]{:S(2)}, u32[]{:S(2)}) collective-permute-start(bf16[192,1536]{1,0:T(8,128)(2,1)} %get-tuple-element.44), channel_id=1, source_target_pairs={{0,4},{4,0},{1,5},{5,1},{2,6},{6,2},{3,7},{7,3}} | collective-permute-start | bytes 1769480 | tf_op jit(solution)/shard_map/ppermute | solution.py:450
  18.2 170.1 %collective-permute-start.20 = (bf16[192,1536]{1,0:T(8,128)(2,1)}, bf16[192,1536]{1,0:T(8,128)(2,1)S(1)}, u32[]{:S(2)}, u32[]{:S(2)}) collective-permute-start(bf16[192,1536]{1,0:T(8,128)(2,1)} %get-tuple-element.53), channel_id=1, source_target_pairs={{0,4},{4,0},{1,5},{5,1},{2,6},{6,2},{3,7},{7,3}} | collective-permute-start | bytes 1769480 | tf_op jit(solution)/shard_map/ppermute | solution.py:450
  86.7 61.5 %collective-permute-start.40 = (bf16[128,1536]{1,0:T(8,128)(2,1)S(1)}, bf16[128,1536]{1,0:T(8,128)(2,1)}, u32[]{:S(2)}, u32[]{:S(2)}) collective-permute-start(bf16[128,1536]{1,0:T(8,128)(2,1)S(1)} %copy-done.116), channel_id=1, source_target_pairs={{0,4},{4,0},{1,5},{5,1},{2,6},{6,2},{3,7},{7,3}} | collective-permute-start | bytes 1179656 | tf_op jit(solution)/shard_map/ppermute | solution.py:450
  88.3 46.0 %collective-permute-start.8 = (bf16[192,1536]{1,0:T(8,128)(2,1)}, bf16[192,1536]{1,0:T(8,128)(2,1)S(1)}, u32[]{:S(2)}, u32[]{:S(2)}) collective-permute-start(bf16[192,1536]{1,0:T(8,128)(2,1)} %collective-permute-done.7.refs_0_), channel_id=1, source_target_pairs={{0,1},{1,0},{2,3},{3,2},{4,5},{5,4},{6,7},{7,6}} | collective-permute-start | bytes 1769480 | tf_op jit(solution)/shard_map/ppermute | solution.py:453
  180.7 56.0 %collective-permute-start.32 = (bf16[1536,256]{1,0:T(8,128)(2,1)}, bf16[1536,256]{1,0:T(8,128)(2,1)S(1)}, u32[]{:S(2)}, u32[]{:S(2)}) collective-permute-start(bf16[1536,256]{1,0:T(8,128)(2,1)} %get-tuple-element.57), channel_id=1, source_target_pairs={{0,4},{4,0},{1,5},{5,1},{2,6},{6,2},{3,7},{7,3}} | collective-permute-start | bytes 2359304 | tf_op jit(solution)/shard_map/ppermute | solution.py:450
  186.2 67.5 %collective-permute-start.36 = (bf16[1536,256]{1,0:T(8,128)(2,1)}, bf16[1536,256]{1,0:T(8,128)(2,1)}, u32[]{:S(2)}, u32[]{:S(2)}) collective-permute-start(bf16[1536,256]{1,0:T(8,128)(2,1)} %get-tuple-element.58), channel_id=1, source_target_pairs={{0,4},{4,0},{1,5},{5,1},{2,6},{6,2},{3,7},{7,3}} | collective-permute-start | bytes 2359304 | tf_op jit(solution)/shard_map/ppermute | solution.py:450
  188.4 66.0 %collective-permute-start.42 = (bf16[128,1536]{1,0:T(8,128)(2,1)}, bf16[128,1536]{1,0:T(8,128)(2,1)}, u32[]{:S(2)}, u32[]{:S(2)}) collective-permute-start(bf16[128,1536]{1,0:T(8,128)(2,1)} %collective-permute-done.40.refs_9_), channel_id=1, source_target_pairs={{0,2},{1,3},{2,0},{3,1},{4,6},{5,7},{6,4},{7,5}} | collective-permute-start | bytes 1179656 | tf_op jit(solution)/shard_map/ppermute | solution.py:521
  212.1 70.0 %collective-permute-start.48 = (bf16[1536,256]{1,0:T(8,128)(2,1)}, bf16[1536,256]{1,0:T(8,128)(2,1)S(1)}, u32[]{:S(2)}, u32[]{:S(2)}) collective-permute-start(bf16[1536,256]{1,0:T(8,128)(2,1)} %get-tuple-element.61), channel_id=1, source_target_pairs={{0,4},{4,0},{1,5},{5,1},{2,6},{6,2},{3,7},{7,3}} | collective-permute-start | bytes 2359304 | tf_op jit(solution)/shard_map/ppermute | solution.py:450
  219.9 67.5 %collective-permute-start.52 = (bf16[1536,256]{1,0:T(8,128)(2,1)}, bf16[1536,256]{1,0:T(8,128)(2,1)}, u32[]{:S(2)}, u32[]{:S(2)}) collective-permute-start(bf16[1536,256]{1,0:T(8,128)(2,1)} %get-tuple-element.62), channel_id=1, source_target_pairs={{0,4},{4,0},{1,5},{5,1},{2,6},{6,2},{3,7},{7,3}} | collective-permute-start | bytes 2359304 | tf_op jit(solution)/shard_map/ppermute | solution.py:450
  322.9 61.9 %collective-permute-start.73 = (bf16[128,1536]{1,0:T(8,128)(2,1)S(1)}, bf16[128,1536]{1,0:T(8,128)(2,1)S(1)}, u32[]{:S(2)}, u32[]{:S(2)}) collective-permute-start(bf16[128,1536]{1,0:T(8,128)(2,1)S(1)} %collective-permute-done.72.refs_9_), channel_id=1, source_target_pairs={{0,1},{1,0},{2,3},{3,2},{4,5},{5,4},{6,7},{7,6}} | collective-permute-start | bytes 1179656 | tf_op jit(solution)/shard_map/ppermute | solution.py:523
  322.9 63.5 %collective-permute-start.77 = (bf16[128,1536]{1,0:T(8,128)(2,1)S(1)}, bf16[128,1536]{1,0:T(8,128)(2,1)S(1)}, u32[]{:S(2)}, u32[]{:S(2)}) collective-permute-start(bf16[128,1536]{1,0:T(8,128)(2,1)S(1)} %copy-done.39), channel_id=1, source_target_pairs={{0,1},{1,0},{2,3},{3,2},{4,5},{5,4},{6,7},{7,6}} | collective-permute-start | bytes 1179656 | tf_op jit(solution)/shard_map/ppermute | solution.py:523
  323.4 64.2 %collective-permute-start.11 = (f32[352,1536]{1,0:T(8,128)}, f32[352,1536]{1,0:T(8,128)}, u32[]{:S(2)}, u32[]{:S(2)}) collective-permute-start(f32[352,1536]{1,0:T(8,128)} %shard_map.182), channel_id=1, source_target_pairs={{0,4},{4,0},{1,5},{5,1},{2,6},{6,2},{3,7},{7,3}} | collective-permute-start | bytes 6488072 | tf_op jit(solution)/shard_map/ppermute | solution.py:450
  324.6 95.4 %collective-permute-start.12 = (f32[352,1536]{1,0:T(8,128)}, f32[352,1536]{1,0:T(8,128)}, u32[]{:S(2)}, u32[]{:S(2)}) collective-permute-start(f32[352,1536]{1,0:T(8,128)} %shard_map.183), channel_id=1, source_target_pairs={{0,4},{4,0},{1,5},{5,1},{2,6},{6,2},{3,7},{7,3}} | collective-permute-start | bytes 6488072 | tf_op jit(solution)/shard_map/ppermute | solution.py:450
  327.2 139.1 %collective-permute-start.13 = (f32[352,1536]{1,0:T(8,128)}, f32[352,1536]{1,0:T(8,128)}, u32[]{:S(2)}, u32[]{:S(2)}) collective-permute-start(f32[352,1536]{1,0:T(8,128)} %shard_map.184), channel_id=1, source_target_pairs={{0,4},{4,0},{1,5},{5,1},{2,6},{6,2},{3,7},{7,3}} | collective-permute-start | bytes 6488072 | tf_op jit(solution)/shard_map/ppermute | solution.py:450
  385.5 153.8 %collective-permute-start.24 = (bf16[1536,512]{1,0:T(8,128)(2,1)}, bf16[1536,512]{1,0:T(8,128)(2,1)}, u32[]{:S(2)}, u32[]{:S(2)}) collective-permute-start(bf16[1536,512]{1,0:T(8,128)(2,1)} %get-tuple-element.55), channel_id=1, source_target_pairs={{0,4},{4,0},{1,5},{5,1},{2,6},{6,2},{3,7},{7,3}} | collective-permute-start | bytes 4718600 | tf_op jit(solution)/shard_map/ppermute | solution.py:450
  386.4 129.4 %collective-permute-start.84 = (bf16[1536,256]{1,0:T(8,128)(2,1)}, bf16[1536,256]{1,0:T(8,128)(2,1)S(1)}, u32[]{:S(2)}, u32[]{:S(2)}) collective-permute-start(bf16[1536,256]{1,0:T(8,128)(2,1)} %get-tuple-element.71), channel_id=1, source_target_pairs={{0,4},{4,0},{1,5},{5,1},{2,6},{6,2},{3,7},{7,3}} | collective-permute-start | bytes 2359304 | tf_op jit(solution)/shard_map/ppermute | solution.py:450
  387.5 140.9 %collective-permute-start.15 = (bf16[8,384,128]{2,1,0:T(8,128)(2,1)}, bf16[8,384,128]{2,1,0:T(8,128)(2,1)S(1)}, u32[]{:S(2)}, u32[]{:S(2)}) collective-permute-start(bf16[8,384,128]{2,1,0:T(8,128)(2,1)} %collective-permute-done.14.refs_0_), channel_id=1, source_target_pairs={{0,1},{1,0},{2,3},{3,2},{4,5},{5,4},{6,7},{7,6}} | collective-permute-start | bytes 2359304 | tf_op jit(solution)/shard_map/ppermute | solution.py:453
  419.9 117.7 %collective-permute-start.16 = (bf16[8,384,128]{2,1,0:T(8,128)(2,1)}, bf16[8,384,128]{2,1,0:T(8,128)(2,1)}, u32[]{:S(2)}, u32[]{:S(2)}) collective-permute-start(bf16[8,384,128]{2,1,0:T(8,128)(2,1)} %collective-permute-done.14.refs_0_), channel_id=1, source_target_pairs={{0,2},{1,3},{2,0},{3,1},{4,6},{5,7},{6,4},{7,5}} | collective-permute-start | bytes 2359304 | tf_op jit(solution)/shard_map/ppermute | solution.py:453
  466.3 72.9 %collective-permute-start.17 = (bf16[8,384,128]{2,1,0:T(8,128)(2,1)}, bf16[8,384,128]{2,1,0:T(8,128)(2,1)}, u32[]{:S(2)}, u32[]{:S(2)}) collective-permute-start(bf16[8,384,128]{2,1,0:T(8,128)(2,1)} %collective-permute-done.14.refs_0_), channel_id=1, source_target_pairs={{0,3},{1,2},{2,1},{3,0},{4,7},{5,6},{6,5},{7,4}} | collective-permute-start | bytes 2359304 | tf_op jit(solution)/shard_map/ppermute | solution.py:453
  539.3 73.8 %collective-permute-start.26 = (bf16[1536,512]{1,0:T(8,128)(2,1)}, bf16[1536,512]{1,0:T(8,128)(2,1)S(1)}, u32[]{:S(2)}, u32[]{:S(2)}) collective-permute-start(bf16[1536,512]{1,0:T(8,128)(2,1)} %collective-permute-done.24.refs_0_), channel_id=1, source_target_pairs={{0,2},{1,3},{2,0},{3,1},{4,6},{5,7},{6,4},{7,5}} | collective-permute-start | bytes 4718600 | tf_op jit(solution)/shard_map/ppermute | solution.py:521
  550.2 46.0 %collective-permute-start.22 = (bf16[192,1536]{1,0:T(8,128)(2,1)S(1)}, bf16[192,1536]{1,0:T(8,128)(2,1)S(1)}, u32[]{:S(2)}, u32[]{:S(2)}) collective-permute-start(bf16[192,1536]{1,0:T(8,128)(2,1)S(1)} %copy-done.29), channel_id=1, source_target_pairs={{0,2},{1,3},{2,0},{3,1},{4,6},{5,7},{6,4},{7,5}} | collective-permute-start | bytes 1769480 | tf_op jit(solution)/shard_map/ppermute | solution.py:453
  551.7 61.4 %collective-permute-start.30 = (bf16[256,1536]{1,0:T(8,128)(2,1)S(1)}, bf16[256,1536]{1,0:T(8,128)(2,1)S(1)}, u32[]{:S(2)}, u32[]{:S(2)}) collective-permute-start(bf16[256,1536]{1,0:T(8,128)(2,1)S(1)} %copy-done.23), channel_id=1, source_target_pairs={{0,2},{1,3},{2,0},{3,1},{4,6},{5,7},{6,4},{7,5}} | collective-permute-start | bytes 2359304 | tf_op jit(solution)/shard_map/ppermute | solution.py:521
  552.2 61.4 %collective-permute-start.18 = (bf16[1056,256]{1,0:T(8,128)(2,1)S(1)}, bf16[1056,256]{1,0:T(8,128)(2,1)S(1)}, u32[]{:S(2)}, u32[]{:S(2)}) collective-permute-start(bf16[1056,256]{1,0:T(8,128)(2,1)S(1)} %get-tuple-element.51.refs_0_), channel_id=1, source_target_pairs={{0,4},{4,0},{1,5},{5,1},{2,6},{6,2},{3,7},{7,3}} | collective-permute-start | bytes 1622024 | tf_op jit(solution)/shard_map/ppermute | solution.py:450
  570.1 60.6 %collective-permute-start.23 = (bf16[192,1536]{1,0:T(8,128)(2,1)S(1)}, bf16[192,1536]{1,0:T(8,128)(2,1)S(1)}, u32[]{:S(2)}, u32[]{:S(2)}) collective-permute-start(bf16[192,1536]{1,0:T(8,128)(2,1)S(1)} %copy-done.29), channel_id=1, source_target_pairs={{0,3},{1,2},{2,1},{3,0},{4,7},{5,6},{6,5},{7,4}} | collective-permute-start | bytes 1769480 | tf_op jit(solution)/shard_map/ppermute | solution.py:453
  596.2 49.9 %collective-permute-start.29 = (bf16[256,1536]{1,0:T(8,128)(2,1)S(1)}, bf16[256,1536]{1,0:T(8,128)(2,1)S(1)}, u32[]{:S(2)}, u32[]{:S(2)}) collective-permute-start(bf16[256,1536]{1,0:T(8,128)(2,1)S(1)} %copy-done.23), channel_id=1, source_target_pairs={{0,1},{1,0},{2,3},{3,2},{4,5},{5,4},{6,7},{7,6}} | collective-permute-start | bytes 2359304 | tf_op jit(solution)/shard_map/ppermute | solution.py:523
  665.3 49.1 %collective-permute-start.33 = (bf16[1536,256]{1,0:T(8,128)(2,1)S(1)}, bf16[1536,256]{1,0:T(8,128)(2,1)}, u32[]{:S(2)}, u32[]{:S(2)}) collective-permute-start(bf16[1536,256]{1,0:T(8,128)(2,1)S(1)} %copy-done.21), channel_id=1, source_target_pairs={{0,1},{1,0},{2,3},{3,2},{4,5},{5,4},{6,7},{7,6}} | collective-permute-start | bytes 2359304 | tf_op jit(solution)/shard_map/ppermute | solution.py:522
  666.6 48.1 %collective-permute-start.37 = (bf16[1536,256]{1,0:T(8,128)(2,1)}, bf16[1536,256]{1,0:T(8,128)(2,1)}, u32[]{:S(2)}, u32[]{:S(2)}) collective-permute-start(bf16[1536,256]{1,0:T(8,128)(2,1)} %collective-permute-done.36.refs_5_), channel_id=1, source_target_pairs={{0,1},{1,0},{2,3},{3,2},{4,5},{5,4},{6,7},{7,6}} | collective-permute-start | bytes 2359304 | tf_op jit(solution)/shard_map/ppermute | solution.py:522
  667.9 47.3 %collective-permute-start.35 = (bf16[1536,256]{1,0:T(8,128)(2,1)}, bf16[1536,256]{1,0:T(8,128)(2,1)}, u32[]{:S(2)}, u32[]{:S(2)}) collective-permute-start(bf16[1536,256]{1,0:T(8,128)(2,1)} %collective-permute-done.34.refs_3_), channel_id=1, source_target_pairs={{0,1},{1,0},{2,3},{3,2},{4,5},{5,4},{6,7},{7,6}} | collective-permute-start | bytes 2359304 | tf_op jit(solution)/shard_map/ppermute | solution.py:522
  736.9 51.7 %collective-permute-start.53 = (bf16[1536,256]{1,0:T(8,128)(2,1)}, bf16[1536,256]{1,0:T(8,128)(2,1)}, u32[]{:S(2)}, u32[]{:S(2)}) collective-permute-start(bf16[1536,256]{1,0:T(8,128)(2,1)} %collective-permute-done.52.refs_5_), channel_id=1, source_target_pairs={{0,1},{1,0},{2,3},{3,2},{4,5},{5,4},{6,7},{7,6}} | collective-permute-start | bytes 2359304 | tf_op jit(solution)/shard_map/ppermute | solution.py:522
  736.9 51.8 %collective-permute-start.66 = (bf16[1536,256]{1,0:T(8,128)(2,1)}, bf16[1536,256]{1,0:T(8,128)(2,1)}, u32[]{:S(2)}, u32[]{:S(2)}) collective-permute-start(bf16[1536,256]{1,0:T(8,128)(2,1)} %collective-permute-done.64.refs_1_), channel_id=1, source_target_pairs={{0,2},{1,3},{2,0},{3,1},{4,6},{5,7},{6,4},{7,5}} | collective-permute-start | bytes 2359304 | tf_op jit(solution)/shard_map/ppermute | solution.py:521
  738.4 50.7 %collective-permute-start.70 = (bf16[1536,256]{1,0:T(8,128)(2,1)}, bf16[1536,256]{1,0:T(8,128)(2,1)}, u32[]{:S(2)}, u32[]{:S(2)}) collective-permute-start(bf16[1536,256]{1,0:T(8,128)(2,1)} %collective-permute-done.68.refs_5_), channel_id=1, source_target_pairs={{0,2},{1,3},{2,0},{3,1},{4,6},{5,7},{6,4},{7,5}} | collective-permute-start | bytes 2359304 | tf_op jit(solution)/shard_map/ppermute | solution.py:521
  (180 other events, 3903.4 us)
